TPU v7x, 32 devices: a whole 2x2x4 slice. The times are simulated.
32 devices in a mesh: rows: 32 (over z, y, x, core).
Axes of the slice: x: 2, y: 2, z: 4, core: 2. Of those that a mesh axis runs over, the one named last changes fastest.
Arguments:
- right_sides: float32 [32, 32768], P(None, 'rows'), may hold values from -48 to 48
- initial: float32 [32, 32768], P(None, 'rows'), may hold values from -1.2 to 1.2
- diag_blocks: float32 [32768, 256], P('rows'), may hold values from -2 to 9
- sub_blocks: float32 [32768, 256], P('rows'), may hold values from -0.21875 to 0.21875
- super_blocks: float32 [32768, 256], P('rows'), may hold values from -0.21875 to 0.21875
- local_inverse: bfloat16 [32768, 1024], P('rows'), may hold values from -1 to 1
- upper_spikes: bfloat16 [256, 32768], P(None, 'rows'), may hold values from -0.21875 to 0.21875
- lower_spikes: bfloat16 [256, 32768], P(None, 'rows'), may hold values from -2 to 2
Outputs:
- solution: float32 [32, 32768], P(None, 'rows')
- residual_norms: float32 [3, 32], replicated
All inputs are finite; a program needn't handle non-finite values.
Results may differ from a plain program's by a relative error of at most 0.002.
The roundings to bfloat16 on the way count: a program that leaves them out, or rounds other values in their place, can miss the bound.
Values may be sent and summed in bfloat16 or wider, within the bound.
No kernel may reach another device: no remote copies, remote signals or barrier semaphores. Data moves between devices by JAX's collectives and lax.ppermute only.
A program may use at most 64 MiB of HBM per device.

v0:
```python
import functools
import math

import jax
import jax.numpy as jnp
from jax import lax
from jax.experimental import pallas as pl
from jax.experimental.pallas import tpu as pltpu
from jax.sharding import PartitionSpec as P


ITERS = 2
AXIS = "rows"
F32 = jnp.float32
BF16 = jnp.bfloat16


def exchange(values, distance):
    count = lax.axis_size(AXIS)
    return lax.ppermute(values, AXIS, [(i, i ^ distance) for i in range(count)])


def across(values):
    count = lax.axis_size(AXIS)
    pairs = [(i, i + 1) for i in range(1, count - 1, 2)]
    return lax.ppermute(values, AXIS, pairs + [(b, a) for a, b in pairs])


def kernel_call(kernel, outs, *args, micros=0.3):
    specs = [
        pl.BlockSpec(memory_space=pltpu.HBM if isinstance(a, tuple) else pltpu.VMEM) for a in args
    ]
    held = sum(math.prod(shape) * jnp.dtype(dtype).itemsize for shape, dtype in outs)
    return pl.pallas_call(
        kernel,
        in_specs=specs,
        out_specs=[pl.BlockSpec(memory_space=pltpu.VMEM)] * len(outs),
        out_shape=[pltpu.VMEM(shape, dtype) for shape, dtype in outs],
        scratch_shapes=[],
        cost_estimate=pl.CostEstimate(flops=int(micros * 1e8), transcendentals=0, bytes_accessed=held),
        compiler_params=pltpu.CompilerParams(vmem_limit_bytes=16 * 2**20),
    )(*(pltpu.with_memory_space_constraint(a[0], pltpu.HBM) if isinstance(a, tuple) else a for a in args))


def is_even():
    return lax.axis_index(AXIS) % 2 == 0


def on_right(level):
    return (lax.axis_index(AXIS) >> level) % 2 == 1


def split3(values):
    high = values.astype(BF16)
    rest = values - high.astype(F32)
    mid = rest.astype(BF16)
    low = (rest - mid.astype(F32)).astype(BF16)
    return high, mid, low


def dot(left, right):
    return jnp.dot(left, right, preferred_element_type=F32)


def fold(product, count):
    rows = product.shape[0] // count
    total = product[(count - 1) * rows :]
    for i in range(count - 2, -1, -1):
        total = total + product[i * rows : (i + 1) * rows]
    return total


def times_exact(parts, right):
    return fold(dot(jnp.concatenate(parts, 0), right), 3)


def times_split(parts, high, mid, low):
    small = dot(parts[0], low) + fold(dot(jnp.concatenate(parts[:2], 0), mid), 2)
    return fold(dot(jnp.concatenate(parts, 0), high), 3) + small


def gather_copies(pairs, sems):
    copies = [pltpu.make_async_copy(a, b, sems.at[i]) for i, (a, b) in enumerate(pairs)]
    for copy in copies:
        copy.start()
    return copies


def payload_kernel(x_hbm, u_hbm, l_hbm, xn_ref, xf_ref, sn_ref, sf_ref, chain_ref):
    even = is_even()
    width = xn_ref.shape[1]
    last = x_hbm.shape[1] - width

    def work(first, final, up, low, bottom, sems):
        head, tail = pl.ds(0, width), pl.ds(last, width)
        copies = gather_copies(
            [
                (x_hbm.at[:, head], first),
                (x_hbm.at[:, tail], final),
                (l_hbm.at[:, tail], bottom),
                (u_hbm.at[:, tail], up),
                (l_hbm.at[:, head], low),
            ],
            sems,
        )
        for copy in copies:
            copy.wait()
        xn_ref[...] = jnp.where(even, final[...], first[...])
        xf_ref[...] = jnp.where(even, first[...], final[...])
        chain_ref[...] = -bottom[...]
        low_tip, up_tip = low[...].astype(F32), up[...].astype(F32)
        sn_ref[...] = jnp.where(even, up_tip, low_tip).astype(BF16)
        sf_ref[...] = jnp.where(even, low_tip, up_tip).astype(BF16)

    vec = pltpu.VMEM(xn_ref.shape, F32)
    mat = pltpu.VMEM(sn_ref.shape, BF16)
    pl.run_scoped(work, vec, vec, mat, mat, mat, pltpu.SemaphoreType.DMA((5,)))


def split_store(ref, rows, values):
    for j, part in enumerate(split3(values)):
        ref[j, rows, :] = part


def first_local_kernel(b_hbm, x_hbm, d_hbm, s_hbm, p_hbm, z_hbm, u_hbm, l_hbm, acc_ref, b_ref, x_ref, d3_ref, s3_ref, p3_ref, z_ref, u_ref, l_ref):
    width = d_hbm.shape[1]

    def work(d_ref, s_ref, p_ref, sems):
        copies = gather_copies(
            [(x_hbm, x_ref), (d_hbm, d_ref), (s_hbm, s_ref), (p_hbm, p_ref), (b_hbm, b_ref), (z_hbm, z_ref), (u_hbm, u_ref), (l_hbm, l_ref)],
            sems,
        )
        for copy in copies[:2]:
            copy.wait()
        for source, target, copy in ((d_ref, d3_ref, 2), (s_ref, s3_ref, 3), (p_ref, p3_ref, 4)):
            for k in range(d_ref.shape[0] // width):
                split_store(target, pl.ds(k * width, width), source[k * width : (k + 1) * width, :])
            copies[copy].wait()
        local_part(b_ref, x_ref, d3_ref, s3_ref, p3_ref, acc_ref)
        for copy in copies[5:]:
            copy.wait()

    mat = pltpu.VMEM(d_hbm.shape, F32)
    pl.run_scoped(work, mat, mat, mat, pltpu.SemaphoreType.DMA((8,)))


def local_part(b_ref, x_ref, d3_ref, s3_ref, p3_ref, acc_ref):
    width = d3_ref.shape[2]
    last = d3_ref.shape[1] // width - 1
    x = [split3(x_ref[:, k * width : (k + 1) * width]) for k in range(last + 1)]
    for k in range(last + 1):
        rows = pl.ds(k * width, width)
        part = times_split(x[k], *(d3_ref[j, rows, :] for j in range(3)))
        if k > 0:
            part = part + times_split(x[k - 1], *(s3_ref[j, rows, :] for j in range(3)))
        if k < last:
            part = part + times_split(x[k + 1], *(p3_ref[j, rows, :] for j in range(3)))
        acc_ref[:, k * width : (k + 1) * width] = b_ref[:, k * width : (k + 1) * width] - part


def close_residual(acc_ref, near_ref, far_ref, s3_ref, p3_ref):
    even = is_even()
    width = s3_ref.shape[2]
    last = s3_ref.shape[1] - width
    near, far = near_ref[...], far_ref[...]
    before = split3(jnp.where(even, far, near))
    after = split3(jnp.where(even, near, far))
    first = acc_ref[:, :width] - times_split(before, *(s3_ref[j, :width, :] for j in range(3)))
    final = acc_ref[:, last:] - times_split(after, *(p3_ref[j, last:, :] for j in range(3)))
    return first, acc_ref[:, width:last], final


def squares(parts, turn, lanes):
    total = sum(jnp.sum(p * p, axis=1, keepdims=True) for p in parts)
    rows = total.shape[0]
    row = lax.broadcasted_iota(jnp.int32, (rows, lanes), 0)
    lane = lax.broadcasted_iota(jnp.int32, (rows, lanes), 1)
    return jnp.sum(jnp.where(lane == row + turn * rows, total, 0.0), axis=0, keepdims=True)


def solve_kernel(acc_ref, near_ref, far_ref, s3_ref, p3_ref, z_ref, mix_ref, norm_in, both_ref, top_ref, local_ref, norm_ref, *, turn):
    parts = close_residual(acc_ref, near_ref, far_ref, s3_ref, p3_ref)
    width = s3_ref.shape[2]
    rows = acc_ref.shape[0]
    rounded = jnp.concatenate([p.astype(BF16) for p in parts], 1)
    local = dot(rounded, z_ref[...])
    local_ref[...] = local
    own_top = local[:, :width]
    mixed = times_split(split3(own_top), *(mix_ref[j] for j in range(3)))
    both_ref[:rows, :] = local[:, -width:] - mixed
    both_ref[rows:, :] = own_top
    top_ref[...] = own_top
    norm = squares(parts, turn, norm_ref.shape[1])
    norm_ref[...] = norm if norm_in is None else norm_in[...] + norm


def norm_kernel(acc_ref, near_ref, far_ref, s3_ref, p3_ref, norm_in, norm_ref, *, turn):
    norm = squares(close_residual(acc_ref, near_ref, far_ref, s3_ref, p3_ref), turn, norm_ref.shape[1])
    norm_ref[...] = jnp.broadcast_to(norm_in[...] + norm, norm_ref.shape)


def mix_kernel(near_ref, far_ref, chain_ref, before_ref, after_ref, mix_ref):
    even = is_even()
    near, far = near_ref[...].astype(F32), far_ref[...].astype(F32)
    before = jnp.where(even, far, near).astype(BF16)
    before_ref[...] = before
    after_ref[...] = jnp.where(even, near, far).astype(BF16)
    for j, part in enumerate(split3(dot(before, chain_ref[...]))):
        mix_ref[j] = part


def start_static_kernel(own_ref, other_ref, second_ref, prefix_ref, whole_ref=None, half_ref=None):
    right = on_right(0)
    own, other = own_ref[...].astype(F32), other_ref[...].astype(F32)
    second = jnp.where(right, own, other).astype(BF16)
    first = jnp.where(right, other, own).astype(BF16)
    second_ref[...] = second
    width = own.shape[0]
    row = lax.broadcasted_iota(jnp.int32, (width, width), 0)
    col = lax.broadcasted_iota(jnp.int32, (width, width), 1)
    prefix = jnp.where(right, other, jnp.where(row == col, 1.0, 0.0))
    for j, part in enumerate(split3(prefix)):
        prefix_ref[j] = part
    if whole_ref is not None:
        whole = dot(first, second)
        half = half_ref.shape[0]
        half_ref[...] = jnp.where(right, whole[half:], whole[:half])
        whole_ref[...] = whole


def static_kernel(whole_ref, got_ref, twin_ref, prefix_ref, second_ref, prefix_out, whole_out=None, half_out=None, *, level):
    even, right = is_even(), on_right(level)
    half = got_ref.shape[0]
    got, twin = got_ref[...], twin_ref[...]
    other = jnp.concatenate([jnp.where(even, got, twin), jnp.where(even, twin, got)], 0)
    whole = whole_ref[...]
    second3 = split3(jnp.where(right, whole, other))
    first3 = split3(jnp.where(right, other, whole))
    for j, part in enumerate(second3):
        second_ref[j] = part
    if whole_out is not None:
        both = times_split(first3, *second3)
        whole_out[...] = both
        half_out[...] = jnp.where(even, both[:half], both[half:])
    prefix = [prefix_ref[j] for j in range(3)]
    for j, part in enumerate(split3(times_split(first3, *prefix))):
        prefix_out[j] = jnp.where(right, part.astype(F32), prefix[j].astype(F32)).astype(BF16)


def level0_kernel(both_ref, got_ref, second_ref, total_ref, carry_ref):
    right = on_right(0)
    rows = total_ref.shape[0]
    total, got = both_ref[:rows, :], got_ref[:rows, :]
    carry_ref[...] = jnp.where(right, got, 0.0)
    first = split3(jnp.where(right, got, total))
    total_ref[...] = times_exact(first, second_ref[...]) + jnp.where(right, total, got)


def level_kernel(total_ref, got_ref, carry_ref, reach_ref, second_ref, total_out, carry_out, *, level):
    right = on_right(level)
    total, got = total_ref[...], got_ref[...]
    first = split3(jnp.where(right, got, total))
    total_out[...] = times_split(first, *(second_ref[j] for j in range(3))) + jnp.where(right, total, got)
    step = times_split(first, *(reach_ref[j] for j in range(3)))
    carry_out[...] = carry_ref[...] + jnp.where(right, step, 0.0)


def tips_kernel(
    got_ref, carry_ref, reach_ref, near_ref, far_ref, local_ref, x_ref, u_ref, l_ref,
    before_ref, after_ref, chain_ref, top_out, previous_out, near_out, far_out, *, level
):
    even, right = is_even(), on_right(level)
    rows, width = got_ref.shape
    step = times_split(split3(got_ref[...]), *(reach_ref[j] for j in range(3)))
    carry = carry_ref[...] + jnp.where(right, step, 0.0)
    own_top = local_ref[:, :width]
    own_bottom = local_ref[:, -width:]
    next_top = jnp.where(even, near_ref[rows:, :], far_ref[...])
    offset = own_bottom - times_exact(split3(next_top), u_ref[:, -width:])
    previous = carry - times_exact(split3(own_top), before_ref[...])
    bottom = offset + times_exact(split3(previous), chain_ref[...])
    top = (next_top - times_exact(split3(bottom), after_ref[...])).astype(BF16)
    previous = previous.astype(BF16)
    top_out[...] = top
    previous_out[...] = previous

    def updated(columns):
        change = local_ref[:, columns] - dot(top, u_ref[:, columns]) - dot(previous, l_ref[:, columns])
        return x_ref[:, columns] + change

    size = x_ref.shape[1]
    first = updated(slice(0, width))
    final = updated(slice(size - width, size))
    near_out[...] = jnp.where(even, final, first)
    far_out[...] = jnp.where(even, first, final)


def update_kernel(top_ref, previous_ref, local_ref, x_ref, u_ref, l_ref, b_ref, d3_ref, s3_ref, p3_ref, x_out, acc_ref):
    change = local_ref[...] - dot(top_ref[...], u_ref[...]) - dot(previous_ref[...], l_ref[...])
    x_out[...] = x_ref[...] + change
    local_part(b_ref, x_out, d3_ref, s3_ref, p3_ref, acc_ref)


def finish_kernel(gathered_ref, out_ref, *, total):
    sums = jnp.sqrt(jnp.sum(gathered_ref[...], axis=0, keepdims=True) / total)
    rows = out_ref.shape[1]
    for turn in range(out_ref.shape[0]):
        out_ref[pl.ds(turn, 1), :] = sums[:, turn * rows : (turn + 1) * rows]


def body(
    right_sides,
    initial,
    diag_blocks,
    sub_blocks,
    super_blocks,
    local_inverse,
    upper_spikes,
    lower_spikes,
):
    width = diag_blocks.shape[1]
    rows, size = right_sides.shape
    count = lax.axis_size(AXIS)
    levels = (count - 1).bit_length()
    tip = ((rows, width), F32)
    low_tip = ((rows, width), BF16)
    square = ((width, width), F32)
    low_square = ((width, width), BF16)
    triple = ((3, width, width), BF16)
    half = ((width // 2, width), F32)
    wide = ((rows, size), F32)
    big = ((3, size, width), BF16)
    lanes = -(-rows * (ITERS + 1) // 128) * 128
    norm_row = ((1, lanes), F32)

    x_near, x_far, s_near, s_far, chain = kernel_call(
        payload_kernel, [tip, tip, low_square, low_square, low_square], (initial,), (upper_spikes,), (lower_spikes,)
    )
    near = exchange(x_near, 1)
    far = across(x_far)
    other = exchange(chain, 1)
    s_near = exchange(s_near, 1)
    s_far = across(s_far)
    acc, right_sides, solution, d3, s3, p3, local_inverse, upper_spikes, lower_spikes = kernel_call(
        first_local_kernel,
        [wide, wide, wide, big, big, big, (local_inverse.shape, BF16), (upper_spikes.shape, BF16), (lower_spikes.shape, BF16)],
        *((a,) for a in (right_sides, initial, diag_blocks, sub_blocks, super_blocks, local_inverse, upper_spikes, lower_spikes)),
        micros=3,
    )
    before, after, mix = kernel_call(mix_kernel, [low_square, low_square, triple], s_near, s_far, chain)

    outs = [square, half]
    second, prefix, *rest = kernel_call(start_static_kernel, [low_square, triple] + outs * (levels > 2), chain, other)
    mats = [(None, second)]
    for level in range(1, levels - 1):
        whole, piece = rest
        got = exchange(piece, 1 << level)
        twin = exchange(got, 1)
        reach = prefix
        second, prefix, *rest = kernel_call(
            functools.partial(static_kernel, level=level),
            [triple, triple] + outs * (level < levels - 2), whole, got, twin, prefix, micros=1,
        )
        mats.append((reach, second))

    norm = None
    for turn in range(ITERS):
        args = [acc, near, far, s3, p3, local_inverse, mix]
        solve = functools.partial(solve_kernel, turn=turn)
        if norm is None:
            solve = functools.partial(lambda *refs, turn: solve_kernel(*refs[:7], None, *refs[7:], turn=turn), turn=turn)
        else:
            args.append(norm)
        both, own_top, local, norm = kernel_call(
            solve, [((2 * rows, width), F32), tip, wide, norm_row], *args, micros=0.8
        )
        swapped = exchange(both, 1)
        far_top = across(own_top)
        total, carry = kernel_call(level0_kernel, [tip, tip], both, swapped, mats[0][1])
        for level in range(1, levels - 1):
            got = exchange(total, 1 << level)
            reach, second = mats[level]
            total, carry = kernel_call(
                functools.partial(level_kernel, level=level), [tip, tip], total, got, carry, reach, second
            )
        got = exchange(total, 1 << (levels - 1))
        top, previous, near, far = kernel_call(
            functools.partial(tips_kernel, level=levels - 1), [low_tip, low_tip, tip, tip],
            got, carry, prefix, swapped, far_top, local, solution, upper_spikes, lower_spikes, before, after, chain, micros=1,
        )
        near = exchange(near, 1)
        far = across(far)
        solution, acc = kernel_call(
            update_kernel, [wide, wide],
            top, previous, local, solution, upper_spikes, lower_spikes, right_sides, d3, s3, p3, micros=1,
        )
    mine = kernel_call(
        functools.partial(norm_kernel, turn=ITERS), [((count, lanes), F32)], acc, near, far, s3, p3, norm
    )[0]
    gathered = lax.all_to_all(mine, AXIS, 0, 0, tiled=True)
    norms = pl.pallas_call(
        functools.partial(finish_kernel, total=size * count), out_shape=jax.ShapeDtypeStruct((ITERS + 1, rows), F32),
        compiler_params=pltpu.CompilerParams(vmem_limit_bytes=16 * 2**20),
    )(gathered)
    return solution, norms


def solution(mesh):
    return jax.shard_map(
        body,
        mesh=mesh,
        in_specs=(
            P(None, AXIS),
            P(None, AXIS),
            P(AXIS, None),
            P(AXIS, None),
            P(AXIS, None),
            P(AXIS, None),
            P(None, AXIS),
            P(None, AXIS),
        ),
        out_specs=(P(None, AXIS), P()),
        check_vma=False,
    )
```

profile of v0, /device:TPU:0, one launch (start us, length us, event | category | flops | bytes accessed | tf_op | source)
XLA Modules:
  0.0 100.0 jit_solution(9726923699167968477)
XLA Ops:
  0.6 1.2 %shard_map.96 = (f32[32,256]{1,0:T(8,128)S(1)}, f32[32,256]{1,0:T(8,128)S(1)}, bf16[256,256]{1,0:T(8,128)(2,1)S(1)}, bf16[256,256]{1,0:T(8,128)(2,1)S(1)}, bf16[256,256]{1,0:T(8,128)(2,1)S(1)}) custom-call(f32[32,1024]{1,0:T(8,128)} %x_hbm.3, bf16[256,1024]{1,0:T(8,128)(2,1)} %u_hbm.3, bf16[256,1024]{1,0:T(8,128)(2,1)} %l_hbm.3), custom_call_target="tpu_custom_call" | custom-call | flops 30000000 | bytes 458752 | tf_op jit(solution)/shard_map/pallas_call | solution.py:34
  1.8 0.6 collective-permute-start.5
  2.4 1.0 collective-permute-done.5.other_ref
  3.4 0.3 shard_map.99
  3.6 2.9 %collective-permute-start.7 = (f32[128,256]{1,0:T(8,128)S(1)}, f32[128,256]{1,0:T(8,128)S(1)}, u32[]{:S(2)}, u32[]{:S(2)}) collective-permute-start(f32[128,256]{1,0:T(8,128)S(1)} %get-tuple-element.85), channel_id=1, source_target_pairs={{0,2},{1,3},{2,0},{3,1},{4,6},{5,7},{6,4},{7,5},{8,10},{9,11},{10,... | collective-permute-start | bytes 393224 | tf_op jit(solution)/shard_map/ppermute | solution.py:20
  6.5 3.8 %collective-permute-done.7.got_ref = f32[128,256]{1,0:T(8,128)S(1)} collective-permute-done((f32[128,256]{1,0:T(8,128)S(1)}, f32[128,256]{1,0:T(8,128)S(1)}, u32[]{:S(2)}, u32[]{:S(2)}) %collective-permute-start.7) | collective-permute-done | bytes 131104 | tf_op jit(solution)/shard_map/ppermute | solution.py:20
  10.3 1.3 %collective-permute-done.8.twin_ref = f32[128,256]{1,0:T(8,128)S(1)} collective-permute-done((f32[128,256]{1,0:T(8,128)S(1)}, f32[128,256]{1,0:T(8,128)S(1)}, u32[]{:S(2)}, u32[]{:S(2)}) %collective-permute-start.8) | collective-permute-done | bytes 131104 | tf_op jit(solution)/shard_map/ppermute | solution.py:20
  11.7 0.6 shard_map.101
  12.3 1.8 %collective-permute-start.10 = (f32[128,256]{1,0:T(8,128)S(1)}, f32[128,256]{1,0:T(8,128)S(1)}, u32[]{:S(2)}, u32[]{:S(2)}) collective-permute-start(f32[128,256]{1,0:T(8,128)S(1)} %get-tuple-element.91), channel_id=1, source_target_pairs={{0,4},{1,5},{2,6},{3,7},{4,0},{5,1},{6,2},{7,3},{8,12},{9,13},{10,... | collective-permute-start | bytes 393224 | tf_op jit(solution)/shard_map/ppermute | solution.py:20
  14.2 3.8 %collective-permute-done.10.got_ref = f32[128,256]{1,0:T(8,128)S(1)} collective-permute-done((f32[128,256]{1,0:T(8,128)S(1)}, f32[128,256]{1,0:T(8,128)S(1)}, u32[]{:S(2)}, u32[]{:S(2)}) %collective-permute-start.10) | collective-permute-done | bytes 131104 | tf_op jit(solution)/shard_map/ppermute | solution.py:20
  18.0 0.5 collective-permute-start.2
  18.5 0.7 collective-permute-start.3
  19.1 0.2 collective-permute-done.11.twin_ref
  19.3 0.6 shard_map.103
  20.0 4.9 %collective-permute-start.13 = (f32[128,256]{1,0:T(8,128)S(1)}, f32[128,256]{1,0:T(8,128)S(1)}, u32[]{:S(2)}, u32[]{:S(2)}) collective-permute-start(f32[128,256]{1,0:T(8,128)S(1)} %get-tuple-element.97), channel_id=1, source_target_pairs={{0,8},{1,9},{2,10},{3,11},{4,12},{5,13},{6,14},{7,15},{8,0},{9,1},... | collective-permute-start | bytes 393224 | tf_op jit(solution)/shard_map/ppermute | solution.py:20
  24.8 0.7 collective-permute-start.1
  25.5 3.0 %shard_map.95 = (f32[32,1024]{1,0:T(8,128)S(1)}, f32[32,1024]{1,0:T(8,128)S(1)}, f32[32,1024]{1,0:T(8,128)S(1)}, bf16[3,1024,256]{2,1,0:T(8,128)(2,1)S(1)}, bf16...) custom-call(f32[32,1024]{1,0:T(8,128)} %b_hbm.1, ...), custom_call_target="tpu_custom_call" | custom-call | flops 300000000 | bytes 8257536 | tf_op jit(solution)/shard_map/pallas_call | solution.py:34
  28.5 0.2 shard_map.97
  28.8 0.8 shard_map.98
  29.6 2.3 %collective-permute-start.4 = (f32[64,256]{1,0:T(8,128)S(1)}, f32[64,256]{1,0:T(8,128)S(1)}, u32[]{:S(2)}, u32[]{:S(2)}) collective-permute-start(f32[64,256]{1,0:T(8,128)S(1)} %get-tuple-element.79.both_ref), channel_id=1, source_target_pairs={{0,1},{1,0},{2,3},{3,2},{4,5},{5,4},{6,7},{7,6},{8,9},{9,8},{10,11... | collective-permute-start | bytes 196616 | tf_op jit(solution)/shard_map/ppermute | solution.py:20
  31.9 0.1 collective-permute-start.14
  31.9 0.8 collective-permute-done.4.got_ref.near_ref
  32.8 0.1 shard_map.100
  32.9 1.5 %collective-permute-start.6 = (f32[32,256]{1,0:T(8,128)S(1)}, f32[32,256]{1,0:T(8,128)S(1)}, u32[]{:S(2)}, u32[]{:S(2)}) collective-permute-start(f32[32,256]{1,0:T(8,128)S(1)} %get-tuple-element.81.total_ref), channel_id=1, source_target_pairs={{0,2},{1,3},{2,0},{3,1},{4,6},{5,7},{6,4},{7,5},{8,10},{9,11},{10,... | collective-permute-start | bytes 98312 | tf_op jit(solution)/shard_map/ppermute | solution.py:20
  34.4 2.4 %collective-permute-done.6.got_ref = f32[32,256]{1,0:T(8,128)S(1)} collective-permute-done((f32[32,256]{1,0:T(8,128)S(1)}, f32[32,256]{1,0:T(8,128)S(1)}, u32[]{:S(2)}, u32[]{:S(2)}) %collective-permute-start.6) | collective-permute-done | bytes 32800 | tf_op jit(solution)/shard_map/ppermute | solution.py:20
  36.8 0.2 shard_map.102
  37.1 1.6 %collective-permute-start.9 = (f32[32,256]{1,0:T(8,128)S(1)}, f32[32,256]{1,0:T(8,128)S(1)}, u32[]{:S(2)}, u32[]{:S(2)}) collective-permute-start(f32[32,256]{1,0:T(8,128)S(1)} %get-tuple-element.87.total_ref), channel_id=1, source_target_pairs={{0,4},{1,5},{2,6},{3,7},{4,0},{5,1},{6,2},{7,3},{8,12},{9,13},{10,... | collective-permute-start | bytes 98312 | tf_op jit(solution)/shard_map/ppermute | solution.py:20
  38.7 2.4 %collective-permute-done.9.got_ref = f32[32,256]{1,0:T(8,128)S(1)} collective-permute-done((f32[32,256]{1,0:T(8,128)S(1)}, f32[32,256]{1,0:T(8,128)S(1)}, u32[]{:S(2)}, u32[]{:S(2)}) %collective-permute-start.9) | collective-permute-done | bytes 32800 | tf_op jit(solution)/shard_map/ppermute | solution.py:20
  41.1 0.2 shard_map.104
  41.3 2.3 %collective-permute-start.12 = (f32[32,256]{1,0:T(8,128)S(1)}, f32[32,256]{1,0:T(8,128)S(1)}, u32[]{:S(2)}, u32[]{:S(2)}) collective-permute-start(f32[32,256]{1,0:T(8,128)S(1)} %get-tuple-element.93.total_ref), channel_id=1, source_target_pairs={{0,8},{1,9},{2,10},{3,11},{4,12},{5,13},{6,14},{7,15},{8,0},{9,1},... | collective-permute-start | bytes 98312 | tf_op jit(solution)/shard_map/ppermute | solution.py:20
  43.6 0.7 collective-permute-start.16
  44.3 0.4 shard_map.105
  44.7 0.8 collective-permute-done.12.got_ref
  45.5 0.2 shard_map.106
  45.8 3.6 %collective-permute-start.15 = (f32[32,256]{1,0:T(8,128)S(1)}, f32[32,256]{1,0:T(8,128)S(1)}, u32[]{:S(2)}, u32[]{:S(2)}) collective-permute-start(f32[32,256]{1,0:T(8,128)S(1)} %get-tuple-element.99), channel_id=1, source_target_pairs={{0,16},{1,17},{2,18},{3,19},{4,20},{5,21},{6,22},{7,23},{8,24},{9,... | collective-permute-start | bytes 98312 | tf_op jit(solution)/shard_map/ppermute | solution.py:20
  49.4 2.3 %collective-permute-done.15.got_ref = f32[32,256]{1,0:T(8,128)S(1)} collective-permute-done((f32[32,256]{1,0:T(8,128)S(1)}, f32[32,256]{1,0:T(8,128)S(1)}, u32[]{:S(2)}, u32[]{:S(2)}) %collective-permute-start.15) | collective-permute-done | bytes 32800 | tf_op jit(solution)/shard_map/ppermute | solution.py:20
  51.7 0.7 shard_map.107
  52.4 0.2 collective-permute-start.17
  52.5 0.7 collective-permute-start.18
  53.2 1.0 shard_map.108
  54.2 0.8 shard_map.109
  55.0 4.0 %collective-permute-start.19 = (f32[64,256]{1,0:T(8,128)S(1)}, f32[64,256]{1,0:T(8,128)S(1)}, u32[]{:S(2)}, u32[]{:S(2)}) collective-permute-start(f32[64,256]{1,0:T(8,128)S(1)} %get-tuple-element.117.both_ref), channel_id=1, source_target_pairs={{0,1},{1,0},{2,3},{3,2},{4,5},{5,4},{6,7},{7,6},{8,9},{9,8},{10,11... | collective-permute-start | bytes 196616 | tf_op jit(solution)/shard_map/ppermute | solution.py:20
  59.0 0.9 collective-permute-done.19.got_ref.near_ref
  59.9 0.1 shard_map.110
  60.1 1.9 %collective-permute-start.20 = (f32[32,256]{1,0:T(8,128)S(1)}, f32[32,256]{1,0:T(8,128)S(1)}, u32[]{:S(2)}, u32[]{:S(2)}) collective-permute-start(f32[32,256]{1,0:T(8,128)S(1)} %get-tuple-element.118.total_ref), channel_id=1, source_target_pairs={{0,2},{1,3},{2,0},{3,1},{4,6},{5,7},{6,4},{7,5},{8,10},{9,11},{10,... | collective-permute-start | bytes 98312 | tf_op jit(solution)/shard_map/ppermute | solution.py:20
  62.0 2.0 %collective-permute-done.20.got_ref = f32[32,256]{1,0:T(8,128)S(1)} collective-permute-done((f32[32,256]{1,0:T(8,128)S(1)}, f32[32,256]{1,0:T(8,128)S(1)}, u32[]{:S(2)}, u32[]{:S(2)}) %collective-permute-start.20) | collective-permute-done | bytes 32800 | tf_op jit(solution)/shard_map/ppermute | solution.py:20
  64.0 0.2 shard_map.111
  64.3 2.5 %collective-permute-start.21 = (f32[32,256]{1,0:T(8,128)S(1)}, f32[32,256]{1,0:T(8,128)S(1)}, u32[]{:S(2)}, u32[]{:S(2)}) collective-permute-start(f32[32,256]{1,0:T(8,128)S(1)} %get-tuple-element.120.total_ref), channel_id=1, source_target_pairs={{0,4},{1,5},{2,6},{3,7},{4,0},{5,1},{6,2},{7,3},{8,12},{9,13},{10,... | collective-permute-start | bytes 98312 | tf_op jit(solution)/shard_map/ppermute | solution.py:20
  66.8 1.9 %collective-permute-done.21.got_ref = f32[32,256]{1,0:T(8,128)S(1)} collective-permute-done((f32[32,256]{1,0:T(8,128)S(1)}, f32[32,256]{1,0:T(8,128)S(1)}, u32[]{:S(2)}, u32[]{:S(2)}) %collective-permute-start.21) | collective-permute-done | bytes 32800 | tf_op jit(solution)/shard_map/ppermute | solution.py:20
  68.7 0.2 shard_map.112
  68.9 2.2 %collective-permute-start.22 = (f32[32,256]{1,0:T(8,128)S(1)}, f32[32,256]{1,0:T(8,128)S(1)}, u32[]{:S(2)}, u32[]{:S(2)}) collective-permute-start(f32[32,256]{1,0:T(8,128)S(1)} %get-tuple-element.122.total_ref), channel_id=1, source_target_pairs={{0,8},{1,9},{2,10},{3,11},{4,12},{5,13},{6,14},{7,15},{8,0},{9,1},... | collective-permute-start | bytes 98312 | tf_op jit(solution)/shard_map/ppermute | solution.py:20
  71.2 0.7 collective-permute-start.24
  71.8 1.2 %collective-permute-done.22.got_ref = f32[32,256]{1,0:T(8,128)S(1)} collective-permute-done((f32[32,256]{1,0:T(8,128)S(1)}, f32[32,256]{1,0:T(8,128)S(1)}, u32[]{:S(2)}, u32[]{:S(2)}) %collective-permute-start.22) | collective-permute-done | bytes 32800 | tf_op jit(solution)/shard_map/ppermute | solution.py:20
  73.1 0.2 shard_map.113
  73.3 3.6 %collective-permute-start.23 = (f32[32,256]{1,0:T(8,128)S(1)}, f32[32,256]{1,0:T(8,128)S(1)}, u32[]{:S(2)}, u32[]{:S(2)}) collective-permute-start(f32[32,256]{1,0:T(8,128)S(1)} %get-tuple-element.124), channel_id=1, source_target_pairs={{0,16},{1,17},{2,18},{3,19},{4,20},{5,21},{6,22},{7,23},{8,24},{9,... | collective-permute-start | bytes 98312 | tf_op jit(solution)/shard_map/ppermute | solution.py:20
  76.9 2.4 %collective-permute-done.23.got_ref = f32[32,256]{1,0:T(8,128)S(1)} collective-permute-done((f32[32,256]{1,0:T(8,128)S(1)}, f32[32,256]{1,0:T(8,128)S(1)}, u32[]{:S(2)}, u32[]{:S(2)}) %collective-permute-start.23) | collective-permute-done | bytes 32800 | tf_op jit(solution)/shard_map/ppermute | solution.py:20
  79.3 0.7 shard_map.114
  80.1 0.7 collective-permute-start.26
  80.7 1.0 shard_map.115
  81.8 1.0 shard_map.116
  82.7 9.4 %all-to-all-start = ((f32[32,1,128]{2,1,0:T(1,128)}), f32[32,1,128]{2,1,0:T(1,128)S(1)}, u32[]{:S(2)}, u32[]{:S(2)}) async-start(f32[32,1,128]{2,1,0:T(1,128)} %bitcast.1), calls=%async_computation | async-start | bytes 32768 | tf_op jit(solution)/shard_map/all_to_all | solution.py:400
  92.1 0.7 copy.11
  92.8 6.5 %all-to-all-done = f32[32,1,128]{2,1,0:T(1,128)S(1)} async-done(((f32[32,1,128]{2,1,0:T(1,128)}), f32[32,1,128]{2,1,0:T(1,128)S(1)}, u32[]{:S(2)}, u32[]{:S(2)}) %all-to-all-start) | async-done | bytes 16416 | tf_op jit(solution)/shard_map/all_to_all | solution.py:400
  99.3 0.7 shard_map.117
  (16 shorter events, 0.2 us)
Async XLA Ops:
  1.8 1.5 %collective-permute-start.5 = (bf16[256,256]{1,0:T(8,128)(2,1)S(1)}, bf16[256,256]{1,0:T(8,128)(2,1)S(1)}, u32[]{:S(2)}, u32[]{:S(2)}) collective-permute-start(bf16[256,256]{1,0:T(8,128)(2,1)S(1)} %get-tuple-element.77.chain_ref.own_ref), channel_id=1, source_target_pairs={{0,1},{1,0},{2,3},{3,2},{4,5},{5,4},{6,7},{7,6},{8,9},{9,8},{10,11... | collective-permute-start | bytes 393224 | tf_op jit(solution)/shard_map/ppermute | solution.py:20
  3.6 6.7 %collective-permute-start.7 = (f32[128,256]{1,0:T(8,128)S(1)}, f32[128,256]{1,0:T(8,128)S(1)}, u32[]{:S(2)}, u32[]{:S(2)}) collective-permute-start(f32[128,256]{1,0:T(8,128)S(1)} %get-tuple-element.85), channel_id=1, source_target_pairs={{0,2},{1,3},{2,0},{3,1},{4,6},{5,7},{6,4},{7,5},{8,10},{9,11},{10,... | collective-permute-start | bytes 393224 | tf_op jit(solution)/shard_map/ppermute | solution.py:20
  10.3 1.3 %collective-permute-start.8 = (f32[128,256]{1,0:T(8,128)S(1)}, f32[128,256]{1,0:T(8,128)S(1)}, u32[]{:S(2)}, u32[]{:S(2)}) collective-permute-start(f32[128,256]{1,0:T(8,128)S(1)} %collective-permute-done.7.got_ref), channel_id=1, source_target_pairs={{0,1},{1,0},{2,3},{3,2},{4,5},{5,4},{6,7},{7,6},{8,9},{9,8},{10,11... | collective-permute-start | bytes 393224 | tf_op jit(solution)/shard_map/ppermute | solution.py:20
  12.3 5.6 %collective-permute-start.10 = (f32[128,256]{1,0:T(8,128)S(1)}, f32[128,256]{1,0:T(8,128)S(1)}, u32[]{:S(2)}, u32[]{:S(2)}) collective-permute-start(f32[128,256]{1,0:T(8,128)S(1)} %get-tuple-element.91), channel_id=1, source_target_pairs={{0,4},{1,5},{2,6},{3,7},{4,0},{5,1},{6,2},{7,3},{8,12},{9,13},{10,... | collective-permute-start | bytes 393224 | tf_op jit(solution)/shard_map/ppermute | solution.py:20
  18.0 1.3 %collective-permute-start.11 = (f32[128,256]{1,0:T(8,128)S(1)}, f32[128,256]{1,0:T(8,128)S(1)}, u32[]{:S(2)}, u32[]{:S(2)}) collective-permute-start(f32[128,256]{1,0:T(8,128)S(1)} %collective-permute-done.10.got_ref), channel_id=1, source_target_pairs={{0,1},{1,0},{2,3},{3,2},{4,5},{5,4},{6,7},{7,6},{8,9},{9,8},{10,11... | collective-permute-start | bytes 393224 | tf_op jit(solution)/shard_map/ppermute | solution.py:20
  18.0 10.5 %collective-permute-start.2 = (bf16[256,256]{1,0:T(8,128)(2,1)S(1)}, bf16[256,256]{1,0:T(8,128)(2,1)S(1)}, u32[]{:S(2)}, u32[]{:S(2)}) collective-permute-start(bf16[256,256]{1,0:T(8,128)(2,1)S(1)} %get-tuple-element.75), channel_id=1, source_target_pairs={{0,1},{1,0},{2,3},{3,2},{4,5},{5,4},{6,7},{7,6},{8,9},{9,8},{10,11... | collective-permute-start | bytes 393224 | tf_op jit(solution)/shard_map/ppermute | solution.py:20
  18.5 10.0 %collective-permute-start.3 = (bf16[256,256]{1,0:T(8,128)(2,1)S(1)}, bf16[256,256]{1,0:T(8,128)(2,1)S(1)}, u32[]{:S(2)}, u32[]{:S(2)}) collective-permute-start(bf16[256,256]{1,0:T(8,128)(2,1)S(1)} %get-tuple-element.76), channel_id=1, source_target_pairs={{1,2},{3,4},{5,6},{7,8},{9,10},{11,12},{13,14},{15,16},{17,18},{19... | collective-permute-start | bytes 393224 | tf_op jit(solution)/shard_map/ppermute | solution.py:26
  20.0 11.9 %collective-permute-start.13 = (f32[128,256]{1,0:T(8,128)S(1)}, f32[128,256]{1,0:T(8,128)S(1)}, u32[]{:S(2)}, u32[]{:S(2)}) collective-permute-start(f32[128,256]{1,0:T(8,128)S(1)} %get-tuple-element.97), channel_id=1, source_target_pairs={{0,8},{1,9},{2,10},{3,11},{4,12},{5,13},{6,14},{7,15},{8,0},{9,1},... | collective-permute-start | bytes 393224 | tf_op jit(solution)/shard_map/ppermute | solution.py:20
  24.8 3.9 %collective-permute-start = (f32[32,256]{1,0:T(8,128)S(1)}, f32[32,256]{1,0:T(8,128)S(1)}, u32[]{:S(2)}, u32[]{:S(2)}) collective-permute-start(f32[32,256]{1,0:T(8,128)S(1)} %get-tuple-element.70), channel_id=1, source_target_pairs={{0,1},{1,0},{2,3},{3,2},{4,5},{5,4},{6,7},{7,6},{8,9},{9,8},{10,11... | collective-permute-start | bytes 98312 | tf_op jit(solution)/shard_map/ppermute | solution.py:20
  24.8 3.9 %collective-permute-start.1 = (f32[32,256]{1,0:T(8,128)S(1)}, f32[32,256]{1,0:T(8,128)S(1)}, u32[]{:S(2)}, u32[]{:S(2)}) collective-permute-start(f32[32,256]{1,0:T(8,128)S(1)} %get-tuple-element.71), channel_id=1, source_target_pairs={{1,2},{3,4},{5,6},{7,8},{9,10},{11,12},{13,14},{15,16},{17,18},{19... | collective-permute-start | bytes 98312 | tf_op jit(solution)/shard_map/ppermute | solution.py:26
  29.6 3.2 %collective-permute-start.4 = (f32[64,256]{1,0:T(8,128)S(1)}, f32[64,256]{1,0:T(8,128)S(1)}, u32[]{:S(2)}, u32[]{:S(2)}) collective-permute-start(f32[64,256]{1,0:T(8,128)S(1)} %get-tuple-element.79.both_ref), channel_id=1, source_target_pairs={{0,1},{1,0},{2,3},{3,2},{4,5},{5,4},{6,7},{7,6},{8,9},{9,8},{10,11... | collective-permute-start | bytes 196616 | tf_op jit(solution)/shard_map/ppermute | solution.py:20
  31.9 12.4 %collective-permute-start.14 = (f32[128,256]{1,0:T(8,128)S(1)}, f32[128,256]{1,0:T(8,128)S(1)}, u32[]{:S(2)}, u32[]{:S(2)}) collective-permute-start(f32[128,256]{1,0:T(8,128)S(1)} %collective-permute-done.13.got_ref), channel_id=1, source_target_pairs={{0,1},{1,0},{2,3},{3,2},{4,5},{5,4},{6,7},{7,6},{8,9},{9,8},{10,11... | collective-permute-start | bytes 393224 | tf_op jit(solution)/shard_map/ppermute | solution.py:20
  32.9 3.9 %collective-permute-start.6 = (f32[32,256]{1,0:T(8,128)S(1)}, f32[32,256]{1,0:T(8,128)S(1)}, u32[]{:S(2)}, u32[]{:S(2)}) collective-permute-start(f32[32,256]{1,0:T(8,128)S(1)} %get-tuple-element.81.total_ref), channel_id=1, source_target_pairs={{0,2},{1,3},{2,0},{3,1},{4,6},{5,7},{6,4},{7,5},{8,10},{9,11},{10,... | collective-permute-start | bytes 98312 | tf_op jit(solution)/shard_map/ppermute | solution.py:20
  37.1 4.0 %collective-permute-start.9 = (f32[32,256]{1,0:T(8,128)S(1)}, f32[32,256]{1,0:T(8,128)S(1)}, u32[]{:S(2)}, u32[]{:S(2)}) collective-permute-start(f32[32,256]{1,0:T(8,128)S(1)} %get-tuple-element.87.total_ref), channel_id=1, source_target_pairs={{0,4},{1,5},{2,6},{3,7},{4,0},{5,1},{6,2},{7,3},{8,12},{9,13},{10,... | collective-permute-start | bytes 98312 | tf_op jit(solution)/shard_map/ppermute | solution.py:20
  41.3 4.2 %collective-permute-start.12 = (f32[32,256]{1,0:T(8,128)S(1)}, f32[32,256]{1,0:T(8,128)S(1)}, u32[]{:S(2)}, u32[]{:S(2)}) collective-permute-start(f32[32,256]{1,0:T(8,128)S(1)} %get-tuple-element.93.total_ref), channel_id=1, source_target_pairs={{0,8},{1,9},{2,10},{3,11},{4,12},{5,13},{6,14},{7,15},{8,0},{9,1},... | collective-permute-start | bytes 98312 | tf_op jit(solution)/shard_map/ppermute | solution.py:20
  43.6 5.8 %collective-permute-start.16 = (f32[32,256]{1,0:T(8,128)S(1)}, f32[32,256]{1,0:T(8,128)S(1)}, u32[]{:S(2)}, u32[]{:S(2)}) collective-permute-start(f32[32,256]{1,0:T(8,128)S(1)} %get-tuple-element.102), channel_id=1, source_target_pairs={{1,2},{3,4},{5,6},{7,8},{9,10},{11,12},{13,14},{15,16},{17,18},{19... | collective-permute-start | bytes 98312 | tf_op jit(solution)/shard_map/ppermute | solution.py:26
  45.8 5.9 %collective-permute-start.15 = (f32[32,256]{1,0:T(8,128)S(1)}, f32[32,256]{1,0:T(8,128)S(1)}, u32[]{:S(2)}, u32[]{:S(2)}) collective-permute-start(f32[32,256]{1,0:T(8,128)S(1)} %get-tuple-element.99), channel_id=1, source_target_pairs={{0,16},{1,17},{2,18},{3,19},{4,20},{5,21},{6,22},{7,23},{8,24},{9,... | collective-permute-start | bytes 98312 | tf_op jit(solution)/shard_map/ppermute | solution.py:20
  52.4 1.8 %collective-permute-start.17 = (f32[32,256]{1,0:T(8,128)S(1)}, f32[32,256]{1,0:T(8,128)S(1)}, u32[]{:S(2)}, u32[]{:S(2)}) collective-permute-start(f32[32,256]{1,0:T(8,128)S(1)} %get-tuple-element.114), channel_id=1, source_target_pairs={{0,1},{1,0},{2,3},{3,2},{4,5},{5,4},{6,7},{7,6},{8,9},{9,8},{10,11... | collective-permute-start | bytes 98312 | tf_op jit(solution)/shard_map/ppermute | solution.py:20
  52.5 1.7 %collective-permute-start.18 = (f32[32,256]{1,0:T(8,128)S(1)}, f32[32,256]{1,0:T(8,128)S(1)}, u32[]{:S(2)}, u32[]{:S(2)}) collective-permute-start(f32[32,256]{1,0:T(8,128)S(1)} %get-tuple-element.115), channel_id=1, source_target_pairs={{1,2},{3,4},{5,6},{7,8},{9,10},{11,12},{13,14},{15,16},{17,18},{19... | collective-permute-start | bytes 98312 | tf_op jit(solution)/shard_map/ppermute | solution.py:26
  55.0 4.9 %collective-permute-start.19 = (f32[64,256]{1,0:T(8,128)S(1)}, f32[64,256]{1,0:T(8,128)S(1)}, u32[]{:S(2)}, u32[]{:S(2)}) collective-permute-start(f32[64,256]{1,0:T(8,128)S(1)} %get-tuple-element.117.both_ref), channel_id=1, source_target_pairs={{0,1},{1,0},{2,3},{3,2},{4,5},{5,4},{6,7},{7,6},{8,9},{9,8},{10,11... | collective-permute-start | bytes 196616 | tf_op jit(solution)/shard_map/ppermute | solution.py:20
  60.1 3.9 %collective-permute-start.20 = (f32[32,256]{1,0:T(8,128)S(1)}, f32[32,256]{1,0:T(8,128)S(1)}, u32[]{:S(2)}, u32[]{:S(2)}) collective-permute-start(f32[32,256]{1,0:T(8,128)S(1)} %get-tuple-element.118.total_ref), channel_id=1, source_target_pairs={{0,2},{1,3},{2,0},{3,1},{4,6},{5,7},{6,4},{7,5},{8,10},{9,11},{10,... | collective-permute-start | bytes 98312 | tf_op jit(solution)/shard_map/ppermute | solution.py:20
  64.3 4.4 %collective-permute-start.21 = (f32[32,256]{1,0:T(8,128)S(1)}, f32[32,256]{1,0:T(8,128)S(1)}, u32[]{:S(2)}, u32[]{:S(2)}) collective-permute-start(f32[32,256]{1,0:T(8,128)S(1)} %get-tuple-element.120.total_ref), channel_id=1, source_target_pairs={{0,4},{1,5},{2,6},{3,7},{4,0},{5,1},{6,2},{7,3},{8,12},{9,13},{10,... | collective-permute-start | bytes 98312 | tf_op jit(solution)/shard_map/ppermute | solution.py:20
  68.9 4.1 %collective-permute-start.22 = (f32[32,256]{1,0:T(8,128)S(1)}, f32[32,256]{1,0:T(8,128)S(1)}, u32[]{:S(2)}, u32[]{:S(2)}) collective-permute-start(f32[32,256]{1,0:T(8,128)S(1)} %get-tuple-element.122.total_ref), channel_id=1, source_target_pairs={{0,8},{1,9},{2,10},{3,11},{4,12},{5,13},{6,14},{7,15},{8,0},{9,1},... | collective-permute-start | bytes 98312 | tf_op jit(solution)/shard_map/ppermute | solution.py:20
  71.2 5.8 %collective-permute-start.24 = (f32[32,256]{1,0:T(8,128)S(1)}, f32[32,256]{1,0:T(8,128)S(1)}, u32[]{:S(2)}, u32[]{:S(2)}) collective-permute-start(f32[32,256]{1,0:T(8,128)S(1)} %get-tuple-element.126), channel_id=1, source_target_pairs={{1,2},{3,4},{5,6},{7,8},{9,10},{11,12},{13,14},{15,16},{17,18},{19... | collective-permute-start | bytes 98312 | tf_op jit(solution)/shard_map/ppermute | solution.py:26
  73.3 6.0 %collective-permute-start.23 = (f32[32,256]{1,0:T(8,128)S(1)}, f32[32,256]{1,0:T(8,128)S(1)}, u32[]{:S(2)}, u32[]{:S(2)}) collective-permute-start(f32[32,256]{1,0:T(8,128)S(1)} %get-tuple-element.124), channel_id=1, source_target_pairs={{0,16},{1,17},{2,18},{3,19},{4,20},{5,21},{6,22},{7,23},{8,24},{9,... | collective-permute-start | bytes 98312 | tf_op jit(solution)/shard_map/ppermute | solution.py:20
  80.0 1.8 %collective-permute-start.25 = (f32[32,256]{1,0:T(8,128)S(1)}, f32[32,256]{1,0:T(8,128)S(1)}, u32[]{:S(2)}, u32[]{:S(2)}) collective-permute-start(f32[32,256]{1,0:T(8,128)S(1)} %get-tuple-element.133), channel_id=1, source_target_pairs={{0,1},{1,0},{2,3},{3,2},{4,5},{5,4},{6,7},{7,6},{8,9},{9,8},{10,11... | collective-permute-start | bytes 98312 | tf_op jit(solution)/shard_map/ppermute | solution.py:20
  80.1 1.7 %collective-permute-start.26 = (f32[32,256]{1,0:T(8,128)S(1)}, f32[32,256]{1,0:T(8,128)S(1)}, u32[]{:S(2)}, u32[]{:S(2)}) collective-permute-start(f32[32,256]{1,0:T(8,128)S(1)} %get-tuple-element.134), channel_id=1, source_target_pairs={{1,2},{3,4},{5,6},{7,8},{9,10},{11,12},{13,14},{15,16},{17,18},{19... | collective-permute-start | bytes 98312 | tf_op jit(solution)/shard_map/ppermute | solution.py:26
  82.7 16.6 %all-to-all-start = ((f32[32,1,128]{2,1,0:T(1,128)}), f32[32,1,128]{2,1,0:T(1,128)S(1)}, u32[]{:S(2)}, u32[]{:S(2)}) async-start(f32[32,1,128]{2,1,0:T(1,128)} %bitcast.1), calls=%async_computation | async-start | bytes 32768 | tf_op jit(solution)/shard_map/all_to_all | solution.py:400
where the time goes:
time: 100 us
  starting transfers between devices  50 us (50%)
  waiting for transfers between devices  33.8 us (34%)
  Pallas kernels  14.6 us (15%)
    ppermute x21, starting transfers between devices, exchange(): return lax.ppermute(values, AXIS, [(i, i ^ distance) for i in range(count)])  36.7 us
    ppermute x21, waiting for transfers between devices, exchange(): return lax.ppermute(values, AXIS, [(i, i ^ distance) for i in range(count)])  27.3 us
    pallas_call x22, Pallas kernels, kernel_call(): pl.pallas_call(kernel, in_specs=specs, out_specs=[pl.BlockSpec(memory_spa...  13.9 us
    all_to_all x1, starting transfers between devices, body(): gathered = lax.all_to_all(mine, AXIS, 0, 0, tiled=True)  9.4 us
    all_to_all x1, waiting for transfers between devices, body(): gathered = lax.all_to_all(mine, AXIS, 0, 0, tiled=True)  6.52 us
    ppermute x6, starting transfers between devices, across(): return lax.ppermute(values, AXIS, pairs + [(b, a) for a, b in pairs])  3.92 us
  transfers between devices with their start and end apart: 28, of which 16 were waited for; matrix products, arithmetic and copies ran while one was open for 1% of the time, Pallas kernels for 8%

commit v1 on v0

--- a/solution.py
+++ b/solution.py
@@ -86,9 +86,10 @@
     return copies
 
 
-def payload_kernel(x_hbm, u_hbm, l_hbm, xn_ref, xf_ref, sn_ref, sf_ref, chain_ref):
+def payload_kernel(x_hbm, u_hbm, l_hbm, near_ref, far_ref, chain_ref):
     even = is_even()
-    width = xn_ref.shape[1]
+    width = chain_ref.shape[0]
+    rows = x_hbm.shape[0]
     last = x_hbm.shape[1] - width
 
     def work(first, final, up, low, bottom, sems):
@@ -105,15 +106,18 @@
         )
         for copy in copies:
             copy.wait()
-        xn_ref[...] = jnp.where(even, final[...], first[...])
-        xf_ref[...] = jnp.where(even, first[...], final[...])
-        chain_ref[...] = -bottom[...]
+        for ref, here, there in ((near_ref, final, first), (far_ref, first, final)):
+            for j, part in enumerate(split3(jnp.where(even, here[...], there[...]))):
+                ref[pl.ds(j * rows, rows), :] = part
+        chain = -bottom[...]
+        chain_ref[...] = chain
         low_tip, up_tip = low[...].astype(F32), up[...].astype(F32)
-        sn_ref[...] = jnp.where(even, up_tip, low_tip).astype(BF16)
-        sf_ref[...] = jnp.where(even, low_tip, up_tip).astype(BF16)
-
-    vec = pltpu.VMEM(xn_ref.shape, F32)
-    mat = pltpu.VMEM(sn_ref.shape, BF16)
+        near_ref[pl.ds(3 * rows, width), :] = jnp.where(even, up_tip, low_tip).astype(BF16)
+        far_ref[pl.ds(3 * rows, width), :] = jnp.where(even, low_tip, up_tip).astype(BF16)
+        near_ref[pl.ds(3 * rows + width, width), :] = chain
+
+    vec = pltpu.VMEM((rows, width), F32)
+    mat = pltpu.VMEM(chain_ref.shape, BF16)
     pl.run_scoped(work, vec, vec, mat, mat, mat, pltpu.SemaphoreType.DMA((5,)))
 
 
@@ -158,27 +162,49 @@
         acc_ref[:, k * width : (k + 1) * width] = b_ref[:, k * width : (k + 1) * width] - part
 
 
+def choose(condition, left, right):
+    return jnp.where(condition, left.astype(F32), right.astype(F32)).astype(left.dtype)
+
+
+def sides_of(near_ref, far_ref, rows):
+    even = is_even()
+    if near_ref.dtype == F32:
+        near, far = near_ref[...], far_ref[...]
+        return split3(jnp.where(even, far, near)), split3(jnp.where(even, near, far))
+    near = [near_ref[pl.ds(j * rows, rows), :] for j in range(3)]
+    far = [far_ref[pl.ds(j * rows, rows), :] for j in range(3)]
+    before = [choose(even, f, n) for n, f in zip(near, far)]
+    after = [choose(even, n, f) for n, f in zip(near, far)]
+    return before, after
+
+
 def close_residual(acc_ref, near_ref, far_ref, s3_ref, p3_ref):
-    even = is_even()
     width = s3_ref.shape[2]
     last = s3_ref.shape[1] - width
-    near, far = near_ref[...], far_ref[...]
-    before = split3(jnp.where(even, far, near))
-    after = split3(jnp.where(even, near, far))
+    before, after = sides_of(near_ref, far_ref, acc_ref.shape[0])
     first = acc_ref[:, :width] - times_split(before, *(s3_ref[j, :width, :] for j in range(3)))
     final = acc_ref[:, last:] - times_split(after, *(p3_ref[j, last:, :] for j in range(3)))
     return first, acc_ref[:, width:last], final
 
 
-def squares(parts, turn, lanes):
-    total = sum(jnp.sum(p * p, axis=1, keepdims=True) for p in parts)
+def squares(parts):
+    total = None
+    for part in parts:
+        for i in range(0, part.shape[1], 128):
+            piece = part[:, i : i + 128]
+            total = piece * piece if total is None else total + piece * piece
+    return total
+
+
+def lane_row(total, turn, lanes):
+    total = jnp.sum(total, axis=1, keepdims=True)
     rows = total.shape[0]
     row = lax.broadcasted_iota(jnp.int32, (rows, lanes), 0)
     lane = lax.broadcasted_iota(jnp.int32, (rows, lanes), 1)
     return jnp.sum(jnp.where(lane == row + turn * rows, total, 0.0), axis=0, keepdims=True)
 
 
-def solve_kernel(acc_ref, near_ref, far_ref, s3_ref, p3_ref, z_ref, mix_ref, norm_in, both_ref, top_ref, local_ref, norm_ref, *, turn):
+def solve_kernel(acc_ref, near_ref, far_ref, s3_ref, p3_ref, z_ref, mix_ref, both_ref, top_ref, local_ref, norm_ref):
     parts = close_residual(acc_ref, near_ref, far_ref, s3_ref, p3_ref)
     width = s3_ref.shape[2]
     rows = acc_ref.shape[0]
@@ -190,32 +216,35 @@
     both_ref[:rows, :] = local[:, -width:] - mixed
     both_ref[rows:, :] = own_top
     top_ref[...] = own_top
-    norm = squares(parts, turn, norm_ref.shape[1])
-    norm_ref[...] = norm if norm_in is None else norm_in[...] + norm
-
-
-def norm_kernel(acc_ref, near_ref, far_ref, s3_ref, p3_ref, norm_in, norm_ref, *, turn):
-    norm = squares(close_residual(acc_ref, near_ref, far_ref, s3_ref, p3_ref), turn, norm_ref.shape[1])
-    norm_ref[...] = jnp.broadcast_to(norm_in[...] + norm, norm_ref.shape)
+    norm_ref[...] = squares(parts)
+
+
+def norm_kernel(acc_ref, near_ref, far_ref, s3_ref, p3_ref, middle_ref, rest_ref, norm_ref, *, turn):
+    first, _, final = close_residual(acc_ref, near_ref, far_ref, s3_ref, p3_ref)
+    row = rest_ref[...] + lane_row(middle_ref[...] + squares((first, final)), turn, norm_ref.shape[1])
+    norm_ref[...] = jnp.broadcast_to(row, norm_ref.shape)
 
 
 def mix_kernel(near_ref, far_ref, chain_ref, before_ref, after_ref, mix_ref):
     even = is_even()
-    near, far = near_ref[...].astype(F32), far_ref[...].astype(F32)
-    before = jnp.where(even, far, near).astype(BF16)
+    width = chain_ref.shape[0]
+    spikes = pl.ds(far_ref.shape[0] - width, width)
+    near, far = near_ref[spikes, :], far_ref[spikes, :]
+    before = choose(even, far, near)
     before_ref[...] = before
-    after_ref[...] = jnp.where(even, near, far).astype(BF16)
+    after_ref[...] = choose(even, near, far)
     for j, part in enumerate(split3(dot(before, chain_ref[...]))):
         mix_ref[j] = part
 
 
-def start_static_kernel(own_ref, other_ref, second_ref, prefix_ref, whole_ref=None, half_ref=None):
+def start_static_kernel(own_ref, near_ref, second_ref, prefix_ref, whole_ref=None, half_ref=None):
     right = on_right(0)
-    own, other = own_ref[...].astype(F32), other_ref[...].astype(F32)
+    width = own_ref.shape[0]
+    own = own_ref[...].astype(F32)
+    other = near_ref[pl.ds(near_ref.shape[0] - width, width), :].astype(F32)
     second = jnp.where(right, own, other).astype(BF16)
     first = jnp.where(right, other, own).astype(BF16)
     second_ref[...] = second
-    width = own.shape[0]
     row = lax.broadcasted_iota(jnp.int32, (width, width), 0)
     col = lax.broadcasted_iota(jnp.int32, (width, width), 1)
     prefix = jnp.where(right, other, jnp.where(row == col, 1.0, 0.0))
@@ -247,32 +276,71 @@
         prefix_out[j] = jnp.where(right, part.astype(F32), prefix[j].astype(F32)).astype(BF16)
 
 
+def merged(right, total, got, matrix):
+    first = split3(jnp.where(right, got, total))
+    product = times_split(first, *matrix) if isinstance(matrix, list) else times_exact(first, matrix)
+    return product + jnp.where(right, total, got)
+
+
+def parts_of(ref):
+    return [ref[j] for j in range(3)]
+
+
+def carry_step(level, values, reach_ref):
+    return jnp.where(on_right(level), times_split(split3(values), *parts_of(reach_ref)), 0.0)
+
+
+def sent_on(level, total, second_ref, carried_ref):
+    product = times_split(split3(total), *parts_of(second_ref))
+    carried_ref[...] = jnp.where(on_right(level), total, product)
+
+
 def level0_kernel(both_ref, got_ref, second_ref, total_ref, carry_ref):
     right = on_right(0)
     rows = total_ref.shape[0]
     total, got = both_ref[:rows, :], got_ref[:rows, :]
     carry_ref[...] = jnp.where(right, got, 0.0)
-    first = split3(jnp.where(right, got, total))
-    total_ref[...] = times_exact(first, second_ref[...]) + jnp.where(right, total, got)
+    total_ref[...] = merged(right, total, got, second_ref[...])
+
+
+def level0_wide_kernel(both_ref, got_ref, second_ref, next_ref, total_ref, carry_ref, carried_ref):
+    level0_kernel(both_ref, got_ref, second_ref, total_ref, carry_ref)
+    sent_on(1, total_ref[...], next_ref, carried_ref)
 
 
 def level_kernel(total_ref, got_ref, carry_ref, reach_ref, second_ref, total_out, carry_out, *, level):
-    right = on_right(level)
-    total, got = total_ref[...], got_ref[...]
-    first = split3(jnp.where(right, got, total))
-    total_out[...] = times_split(first, *(second_ref[j] for j in range(3))) + jnp.where(right, total, got)
-    step = times_split(first, *(reach_ref[j] for j in range(3)))
-    carry_out[...] = carry_ref[...] + jnp.where(right, step, 0.0)
-
-
-def tips_kernel(
-    got_ref, carry_ref, reach_ref, near_ref, far_ref, local_ref, x_ref, u_ref, l_ref,
-    before_ref, after_ref, chain_ref, top_out, previous_out, near_out, far_out, *, level
+    got = got_ref[...]
+    total_out[...] = merged(on_right(level), total_ref[...], got, parts_of(second_ref))
+    carry_out[...] = carry_ref[...] + carry_step(level, got, reach_ref)
+
+
+def wide_kernel(
+    total_ref, carried_ref, got_ref, low_ref, cross_ref, carry_ref, reach_ref, reach2_ref, second_ref, second2_ref,
+    *rest, level
 ):
-    even, right = is_even(), on_right(level)
-    rows, width = got_ref.shape
-    step = times_split(split3(got_ref[...]), *(reach_ref[j] for j in range(3)))
-    carry = carry_ref[...] + jnp.where(right, step, 0.0)
+    next_ref = rest[0] if len(rest) == 4 else None
+    total_out, carry_out = rest[-3:-1] if next_ref is not None else rest
+    right, right2 = on_right(level), on_right(level + 1)
+    got, low = got_ref[...], low_ref[...] + cross_ref[...]
+    carry_out[...] = carry_ref[...] + carry_step(level, got, reach_ref) + carry_step(level + 1, low, reach2_ref)
+    passed = times_split(split3(got), *parts_of(second_ref))
+    pair = jnp.where(right, passed + total_ref[...], carried_ref[...] + got)
+    total = merged(right2, pair, low, parts_of(second2_ref))
+    total_out[...] = total
+    if next_ref is not None:
+        sent_on(level + 2, total, next_ref, rest[-1])
+
+
+def tips_kernel(*refs, level, wide):
+    gots, refs = refs[: 3 if wide else 1], refs[3 if wide else 1 :]
+    reaches, refs = refs[: 2 if wide else 1], refs[2 if wide else 1 :]
+    carry_ref, near_ref, far_ref, local_ref, x_ref, u_ref, l_ref, before_ref, after_ref, chain_ref = refs[:10]
+    top_out, previous_out, near_out, far_out = refs[10:]
+    even = is_even()
+    rows, width = carry_ref.shape
+    carry = carry_ref[...] + carry_step(level, gots[0][...], reaches[0])
+    if wide:
+        carry = carry + carry_step(level + 1, gots[1][...] + gots[2][...], reaches[1])
     own_top = local_ref[:, :width]
     own_bottom = local_ref[:, -width:]
     next_top = jnp.where(even, near_ref[rows:, :], far_ref[...])
@@ -295,10 +363,16 @@
     far_out[...] = jnp.where(even, first, final)
 
 
-def update_kernel(top_ref, previous_ref, local_ref, x_ref, u_ref, l_ref, b_ref, d3_ref, s3_ref, p3_ref, x_out, acc_ref):
+def update_kernel(top_ref, previous_ref, local_ref, x_ref, u_ref, l_ref, b_ref, d3_ref, s3_ref, p3_ref, *refs):
+    x_out, acc_ref = refs[-2:] if len(refs) == 2 else refs[-4:-2]
     change = local_ref[...] - dot(top_ref[...], u_ref[...]) - dot(previous_ref[...], l_ref[...])
     x_out[...] = x_ref[...] + change
     local_part(b_ref, x_out, d3_ref, s3_ref, p3_ref, acc_ref)
+    if len(refs) > 2:
+        norms, middle_ref, row_ref = refs[:-4], refs[-2], refs[-1]
+        width = d3_ref.shape[2]
+        middle_ref[...] = squares((acc_ref[:, width : acc_ref.shape[1] - width],))
+        row_ref[...] = sum(lane_row(ref[...], turn, row_ref.shape[1]) for turn, ref in enumerate(norms))
 
 
 def finish_kernel(gathered_ref, out_ref, *, total):
@@ -331,78 +405,99 @@
     wide = ((rows, size), F32)
     big = ((3, size, width), BF16)
     lanes = -(-rows * (ITERS + 1) // 128) * 128
-    norm_row = ((1, lanes), F32)
-
-    x_near, x_far, s_near, s_far, chain = kernel_call(
-        payload_kernel, [tip, tip, low_square, low_square, low_square], (initial,), (upper_spikes,), (lower_spikes,)
+
+    near_pack, far_pack, chain = kernel_call(
+        payload_kernel,
+        [((3 * rows + 2 * width, width), BF16), ((3 * rows + width, width), BF16), low_square],
+        (initial,), (upper_spikes,), (lower_spikes,),
     )
-    near = exchange(x_near, 1)
-    far = across(x_far)
-    other = exchange(chain, 1)
-    s_near = exchange(s_near, 1)
-    s_far = across(s_far)
+    near = exchange(near_pack, 1)
+    far = across(far_pack)
     acc, right_sides, solution, d3, s3, p3, local_inverse, upper_spikes, lower_spikes = kernel_call(
         first_local_kernel,
         [wide, wide, wide, big, big, big, (local_inverse.shape, BF16), (upper_spikes.shape, BF16), (lower_spikes.shape, BF16)],
         *((a,) for a in (right_sides, initial, diag_blocks, sub_blocks, super_blocks, local_inverse, upper_spikes, lower_spikes)),
         micros=3,
     )
-    before, after, mix = kernel_call(mix_kernel, [low_square, low_square, triple], s_near, s_far, chain)
+    before, after, mix = kernel_call(mix_kernel, [low_square, low_square, triple], near, far, chain)
 
     outs = [square, half]
-    second, prefix, *rest = kernel_call(start_static_kernel, [low_square, triple] + outs * (levels > 2), chain, other)
-    mats = [(None, second)]
+    second, prefix, *rest = kernel_call(start_static_kernel, [low_square, triple] + outs * (levels > 2), chain, near)
+    seconds, reaches = [second], [None, prefix]
     for level in range(1, levels - 1):
         whole, piece = rest
         got = exchange(piece, 1 << level)
         twin = exchange(got, 1)
-        reach = prefix
         second, prefix, *rest = kernel_call(
             functools.partial(static_kernel, level=level),
             [triple, triple] + outs * (level < levels - 2), whole, got, twin, prefix, micros=1,
         )
-        mats.append((reach, second))
-
-    norm = None
+        seconds.append(second)
+        reaches.append(prefix)
+
+    norms = []
     for turn in range(ITERS):
-        args = [acc, near, far, s3, p3, local_inverse, mix]
-        solve = functools.partial(solve_kernel, turn=turn)
-        if norm is None:
-            solve = functools.partial(lambda *refs, turn: solve_kernel(*refs[:7], None, *refs[7:], turn=turn), turn=turn)
-        else:
-            args.append(norm)
         both, own_top, local, norm = kernel_call(
-            solve, [((2 * rows, width), F32), tip, wide, norm_row], *args, micros=0.8
+            solve_kernel, [((2 * rows, width), F32), tip, wide, ((rows, 128), F32)],
+            acc, near, far, s3, p3, local_inverse, mix, micros=0.8,
         )
+        norms.append(norm)
         swapped = exchange(both, 1)
         far_top = across(own_top)
-        total, carry = kernel_call(level0_kernel, [tip, tip], both, swapped, mats[0][1])
-        for level in range(1, levels - 1):
-            got = exchange(total, 1 << level)
-            reach, second = mats[level]
-            total, carry = kernel_call(
-                functools.partial(level_kernel, level=level), [tip, tip], total, got, carry, reach, second
-            )
-        got = exchange(total, 1 << (levels - 1))
+        groups = [(0, 1)]
+        while sum(groups[-1]) < levels:
+            level = sum(groups[-1])
+            groups.append((level, 2 if turn > 0 and level + 2 <= levels else 1))
+        carried = None
+        for i, (level, size_of) in enumerate(groups[:-1]):
+            after_size = groups[i + 1][1]
+            outs = [tip, tip] + [tip] * (after_size == 2)
+            following = [seconds[level + size_of]] if after_size == 2 else []
+            if level == 0:
+                kernel = level0_wide_kernel if after_size == 2 else level0_kernel
+                total, carry, *more = kernel_call(kernel, outs, both, swapped, seconds[0], *following)
+            elif size_of == 1:
+                got = exchange(total, 1 << level)
+                total, carry, *more = kernel_call(
+                    functools.partial(level_kernel, level=level), outs, total, got, carry, reaches[level], seconds[level]
+                )
+            else:
+                step = 1 << level
+                got = exchange(total, step)
+                low = exchange(carried, 2 * step)
+                cross = exchange(carried, 3 * step)
+                total, carry, *more = kernel_call(
+                    functools.partial(wide_kernel, level=level), outs, total, carried, got, low, cross, carry,
+                    reaches[level], reaches[level + 1], seconds[level], seconds[level + 1], *following,
+                )
+            carried = more[0] if more else None
+        level, size_of = groups[-1]
+        gots = [exchange(total, 1 << level)]
+        if size_of == 2:
+            gots.append(exchange(carried, 2 << level))
+            gots.append(exchange(carried, 3 << level))
         top, previous, near, far = kernel_call(
-            functools.partial(tips_kernel, level=levels - 1), [low_tip, low_tip, tip, tip],
-            got, carry, prefix, swapped, far_top, local, solution, upper_spikes, lower_spikes, before, after, chain, micros=1,
+            functools.partial(tips_kernel, level=level, wide=size_of == 2), [low_tip, low_tip, tip, tip],
+            *gots, *reaches[level : level + size_of], carry, swapped, far_top, local, solution, upper_spikes, lower_spikes,
+            before, after, chain, micros=1,
         )
         near = exchange(near, 1)
         far = across(far)
-        solution, acc = kernel_call(
-            update_kernel, [wide, wide],
-            top, previous, local, solution, upper_spikes, lower_spikes, right_sides, d3, s3, p3, micros=1,
+        final = turn == ITERS - 1
+        solution, acc, *sums = kernel_call(
+            update_kernel, [wide, wide] + [((rows, 128), F32), ((1, lanes), F32)] * final,
+            top, previous, local, solution, upper_spikes, lower_spikes, right_sides, d3, s3, p3, *(norms if final else ()),
+            micros=1,
         )
     mine = kernel_call(
-        functools.partial(norm_kernel, turn=ITERS), [((count, lanes), F32)], acc, near, far, s3, p3, norm
+        functools.partial(norm_kernel, turn=ITERS), [((count, lanes), F32)], acc, near, far, s3, p3, *sums
     )[0]
     gathered = lax.all_to_all(mine, AXIS, 0, 0, tiled=True)
-    norms = pl.pallas_call(
+    result = pl.pallas_call(
         functools.partial(finish_kernel, total=size * count), out_shape=jax.ShapeDtypeStruct((ITERS + 1, rows), F32),
         compiler_params=pltpu.CompilerParams(vmem_limit_bytes=16 * 2**20),
     )(gathered)
-    return solution, norms
+    return solution, result
 
 
 def solution(mesh):

time: 100 us -> 93.9 us (0.939)
  starting transfers between devices: 50 us -> 39.8 us
  waiting for transfers between devices: 33.8 us -> 37.5 us
    ppermute x21, starting transfers between devices: 36.7 us -> 28.8 us  [exchange(): return lax.ppermute(values, AXIS, [(i, i ^ distance) for i in range(count)])]
    ppermute x21, waiting for transfers between devices: 27.3 us -> 30.9 us  [exchange(): return lax.ppermute(values, AXIS, [(i, i ^ distance) for i in range(count)])]
    all_to_all x1, starting transfers between devices: 9.4 us -> 7.76 us  [body(): gathered = lax.all_to_all(mine, AXIS, 0, 0, tiled=True)]
    ppermute x6 -> x5, starting transfers between devices: 3.92 us -> 3.28 us  [across(): return lax.ppermute(values, AXIS, pairs + [(b, a) for a, b in pairs])]
    pallas_call x22 -> x20, Pallas kernels: 13.9 us -> 14.2 us  [kernel_call(): pl.pallas_call(kernel, in_specs=specs, out_specs=[pl.BlockSpec(memory_spa...]
  transfers between devices with their start and end apart: 28 -> 27, of which waited for: 16 -> 17; matrix products, arithmetic and copies ran while one was open for 1% -> 1% of each run, Pallas kernels for 8% -> 9%
where the time goes in v1:
time: 93.9 us; the launch traced here: 93.7 us
  starting transfers between devices  39.8 us (42%)
  waiting for transfers between devices  37.5 us (40%)
  Pallas kernels  14.9 us (16%)
    ppermute x21, waiting for transfers between devices, exchange(): return lax.ppermute(values, AXIS, [(i, i ^ distance) for i in range(count)])  30.9 us
    ppermute x21, starting transfers between devices, exchange(): return lax.ppermute(values, AXIS, [(i, i ^ distance) for i in range(count)])  28.8 us
    pallas_call x20, Pallas kernels, kernel_call(): pl.pallas_call(kernel, in_specs=specs, out_specs=[pl.BlockSpec(memory_spa...  14.2 us
    all_to_all x1, starting transfers between devices, body(): gathered = lax.all_to_all(mine, AXIS, 0, 0, tiled=True)  7.76 us
    all_to_all x1, waiting for transfers between devices, body(): gathered = lax.all_to_all(mine, AXIS, 0, 0, tiled=True)  6.51 us
    ppermute x5, starting transfers between devices, across(): return lax.ppermute(values, AXIS, pairs + [(b, a) for a, b in pairs])  3.28 us
  transfers between devices with their start and end apart: 27, of which 17 were waited for; matrix products, arithmetic and copies ran while one was open for 1% of the time, Pallas kernels for 9%

profile of v1, /device:TPU:0, one launch (start us, length us, event | category | flops | bytes accessed | tf_op | source)
XLA Modules:
  0.0 93.7 jit_solution(2624137610924942038)
XLA Ops:
  0.6 1.2 %shard_map.96 = (bf16[608,256]{1,0:T(8,128)(2,1)S(1)}, bf16[352,256]{1,0:T(8,128)(2,1)S(1)}, bf16[256,256]{1,0:T(8,128)(2,1)S(1)}) custom-call(f32[32,1024]{1,0:T(8,128)} %x_hbm.3, bf16[256,1024]{1,0:T(8,128)(2,1)} %u_hbm.3, bf16[256,1024]{1,0:T(8,128)(2,1)} %l_hbm.3), custom_call_target="tpu_custom_call" | custom-call | flops 30000000 | bytes 622592 | tf_op jit(solution)/shard_map/pallas_call | solution.py:34
  1.8 0.6 collective-permute-start
  2.4 1.2 %collective-permute-done.near_ref = bf16[608,256]{1,0:T(8,128)(2,1)S(1)} collective-permute-done((bf16[608,256]{1,0:T(8,128)(2,1)S(1)}, bf16[608,256]{1,0:T(8,128)(2,1)S(1)}, u32[]{:S(2)}, u32[]{:S(2)}) %collective-permute-start) | collective-permute-done | bytes 311328 | tf_op jit(solution)/shard_map/ppermute | solution.py:20
  3.6 0.3 shard_map.99
  3.9 2.9 %collective-permute-start.4 = (f32[128,256]{1,0:T(8,128)S(1)}, f32[128,256]{1,0:T(8,128)S(1)}, u32[]{:S(2)}, u32[]{:S(2)}) collective-permute-start(f32[128,256]{1,0:T(8,128)S(1)} %get-tuple-element.81), channel_id=1, source_target_pairs={{0,2},{1,3},{2,0},{3,1},{4,6},{5,7},{6,4},{7,5},{8,10},{9,11},{10,... | collective-permute-start | bytes 393224 | tf_op jit(solution)/shard_map/ppermute | solution.py:20
  6.8 3.8 %collective-permute-done.4.got_ref = f32[128,256]{1,0:T(8,128)S(1)} collective-permute-done((f32[128,256]{1,0:T(8,128)S(1)}, f32[128,256]{1,0:T(8,128)S(1)}, u32[]{:S(2)}, u32[]{:S(2)}) %collective-permute-start.4) | collective-permute-done | bytes 131104 | tf_op jit(solution)/shard_map/ppermute | solution.py:20
  10.6 1.3 %collective-permute-done.5.twin_ref = f32[128,256]{1,0:T(8,128)S(1)} collective-permute-done((f32[128,256]{1,0:T(8,128)S(1)}, f32[128,256]{1,0:T(8,128)S(1)}, u32[]{:S(2)}, u32[]{:S(2)}) %collective-permute-start.5) | collective-permute-done | bytes 131104 | tf_op jit(solution)/shard_map/ppermute | solution.py:20
  11.9 0.6 shard_map.101
  12.6 1.8 %collective-permute-start.7 = (f32[128,256]{1,0:T(8,128)S(1)}, f32[128,256]{1,0:T(8,128)S(1)}, u32[]{:S(2)}, u32[]{:S(2)}) collective-permute-start(f32[128,256]{1,0:T(8,128)S(1)} %get-tuple-element.87), channel_id=1, source_target_pairs={{0,4},{1,5},{2,6},{3,7},{4,0},{5,1},{6,2},{7,3},{8,12},{9,13},{10,... | collective-permute-start | bytes 393224 | tf_op jit(solution)/shard_map/ppermute | solution.py:20
  14.4 3.8 %collective-permute-done.7.got_ref = f32[128,256]{1,0:T(8,128)S(1)} collective-permute-done((f32[128,256]{1,0:T(8,128)S(1)}, f32[128,256]{1,0:T(8,128)S(1)}, u32[]{:S(2)}, u32[]{:S(2)}) %collective-permute-start.7) | collective-permute-done | bytes 131104 | tf_op jit(solution)/shard_map/ppermute | solution.py:20
  18.2 0.7 collective-permute-start.1
  18.9 0.7 collective-permute-done.8.twin_ref
  19.6 0.6 shard_map.103
  20.2 4.9 %collective-permute-start.10 = (f32[128,256]{1,0:T(8,128)S(1)}, f32[128,256]{1,0:T(8,128)S(1)}, u32[]{:S(2)}, u32[]{:S(2)}) collective-permute-start(f32[128,256]{1,0:T(8,128)S(1)} %get-tuple-element.93), channel_id=1, source_target_pairs={{0,8},{1,9},{2,10},{3,11},{4,12},{5,13},{6,14},{7,15},{8,0},{9,1},... | collective-permute-start | bytes 393224 | tf_op jit(solution)/shard_map/ppermute | solution.py:20
  25.1 3.0 %shard_map.95 = (f32[32,1024]{1,0:T(8,128)S(1)}, f32[32,1024]{1,0:T(8,128)S(1)}, f32[32,1024]{1,0:T(8,128)S(1)}, bf16[3,1024,256]{2,1,0:T(8,128)(2,1)S(1)}, bf16...) custom-call(f32[32,1024]{1,0:T(8,128)} %b_hbm.1, ...), custom_call_target="tpu_custom_call" | custom-call | flops 300000000 | bytes 8257536 | tf_op jit(solution)/shard_map/pallas_call | solution.py:34
  28.1 0.2 shard_map.97
  28.3 0.8 shard_map.98
  29.1 0.1 collective-permute-start.2
  29.2 0.8 collective-permute-done.10.got_ref
  30.0 0.4 collective-permute-done.2.got_ref.refs_3_
  30.4 0.1 shard_map.100
  30.6 1.0 %collective-permute-start.3 = (f32[32,256]{1,0:T(8,128)S(1)}, f32[32,256]{1,0:T(8,128)S(1)}, u32[]{:S(2)}, u32[]{:S(2)}) collective-permute-start(f32[32,256]{1,0:T(8,128)S(1)} %get-tuple-element.77.total_ref), channel_id=1, source_target_pairs={{0,2},{1,3},{2,0},{3,1},{4,6},{5,7},{6,4},{7,5},{8,10},{9,11},{10,... | collective-permute-start | bytes 98312 | tf_op jit(solution)/shard_map/ppermute | solution.py:20
  31.6 2.9 %collective-permute-done.3.got_ref = f32[32,256]{1,0:T(8,128)S(1)} collective-permute-done((f32[32,256]{1,0:T(8,128)S(1)}, f32[32,256]{1,0:T(8,128)S(1)}, u32[]{:S(2)}, u32[]{:S(2)}) %collective-permute-start.3) | collective-permute-done | bytes 32800 | tf_op jit(solution)/shard_map/ppermute | solution.py:20
  34.5 0.2 shard_map.102
  34.7 1.1 %collective-permute-start.6 = (f32[32,256]{1,0:T(8,128)S(1)}, f32[32,256]{1,0:T(8,128)S(1)}, u32[]{:S(2)}, u32[]{:S(2)}) collective-permute-start(f32[32,256]{1,0:T(8,128)S(1)} %get-tuple-element.83.total_ref), channel_id=1, source_target_pairs={{0,4},{1,5},{2,6},{3,7},{4,0},{5,1},{6,2},{7,3},{8,12},{9,13},{10,... | collective-permute-start | bytes 98312 | tf_op jit(solution)/shard_map/ppermute | solution.py:20
  35.8 2.9 %collective-permute-done.6.got_ref = f32[32,256]{1,0:T(8,128)S(1)} collective-permute-done((f32[32,256]{1,0:T(8,128)S(1)}, f32[32,256]{1,0:T(8,128)S(1)}, u32[]{:S(2)}, u32[]{:S(2)}) %collective-permute-start.6) | collective-permute-done | bytes 32800 | tf_op jit(solution)/shard_map/ppermute | solution.py:20
  38.7 0.2 shard_map.104
  39.0 0.9 collective-permute-start.9
  39.9 0.7 collective-permute-start.13
  40.5 0.4 shard_map.105
  41.0 1.9 %collective-permute-done.9.got_ref = f32[32,256]{1,0:T(8,128)S(1)} collective-permute-done((f32[32,256]{1,0:T(8,128)S(1)}, f32[32,256]{1,0:T(8,128)S(1)}, u32[]{:S(2)}, u32[]{:S(2)}) %collective-permute-start.9) | collective-permute-done | bytes 32800 | tf_op jit(solution)/shard_map/ppermute | solution.py:20
  42.9 0.2 shard_map.106
  43.2 2.7 %collective-permute-start.12 = (f32[32,256]{1,0:T(8,128)S(1)}, f32[32,256]{1,0:T(8,128)S(1)}, u32[]{:S(2)}, u32[]{:S(2)}) collective-permute-start(f32[32,256]{1,0:T(8,128)S(1)} %get-tuple-element.95), channel_id=1, source_target_pairs={{0,16},{1,17},{2,18},{3,19},{4,20},{5,21},{6,22},{7,23},{8,24},{9,... | collective-permute-start | bytes 98312 | tf_op jit(solution)/shard_map/ppermute | solution.py:20
  45.8 3.1 %collective-permute-done.12.refs_0_ = f32[32,256]{1,0:T(8,128)S(1)} collective-permute-done((f32[32,256]{1,0:T(8,128)S(1)}, f32[32,256]{1,0:T(8,128)S(1)}, u32[]{:S(2)}, u32[]{:S(2)}) %collective-permute-start.12) | collective-permute-done | bytes 32800 | tf_op jit(solution)/shard_map/ppermute | solution.py:20
  48.9 0.7 shard_map.107
  49.6 0.2 collective-permute-start.14
  49.8 0.7 collective-permute-start.15
  50.4 1.0 %shard_map.108 = (f32[32,1024]{1,0:T(8,128)S(1)}, f32[32,1024]{1,0:T(8,128)S(1)}) custom-call(bf16[32,256]{1,0:T(8,128)(2,1)S(1)} %get-tuple-element.105.top_ref, bf16[32,256]{1,0:T(8,128)(2,1)S(1)} %get-tuple-element.106.previous_ref, f32[32,1024]{1,0:T(8,128)S(1)} %get-tuple-element.99.refs_5_.local_ref, f32[32,1024]{1,0:T(8,128)S(1)} %get-tuple-element.100.refs_6_.x_ref, ...), custom_call_target="tpu_custom_call" | custom-call | flops 100000000 | bytes 262144 | tf_op jit(solution)/shard_map/pallas_call | solution.py:34
  51.4 0.0 collective-permute-done.14.near_ref
  51.5 0.8 shard_map.109
  52.3 4.0 %collective-permute-start.16 = (f32[64,256]{1,0:T(8,128)S(1)}, f32[64,256]{1,0:T(8,128)S(1)}, u32[]{:S(2)}, u32[]{:S(2)}) collective-permute-start(f32[64,256]{1,0:T(8,128)S(1)} %get-tuple-element.112.both_ref), channel_id=1, source_target_pairs={{0,1},{1,0},{2,3},{3,2},{4,5},{5,4},{6,7},{7,6},{8,9},{9,8},{10,11... | collective-permute-start | bytes 196616 | tf_op jit(solution)/shard_map/ppermute | solution.py:20
  56.3 0.9 collective-permute-done.16.got_ref.refs_6_
  57.2 0.3 shard_map.110
  57.5 1.9 %collective-permute-start.17 = (f32[32,256]{1,0:T(8,128)S(1)}, f32[32,256]{1,0:T(8,128)S(1)}, u32[]{:S(2)}, u32[]{:S(2)}) collective-permute-start(f32[32,256]{1,0:T(8,128)S(1)} %get-tuple-element.113.total_ref), channel_id=1, source_target_pairs={{0,2},{1,3},{2,0},{3,1},{4,6},{5,7},{6,4},{7,5},{8,10},{9,11},{10,... | collective-permute-start | bytes 98312 | tf_op jit(solution)/shard_map/ppermute | solution.py:20
  59.4 1.9 %collective-permute-start.19 = (f32[32,256]{1,0:T(8,128)S(1)}, f32[32,256]{1,0:T(8,128)S(1)}, u32[]{:S(2)}, u32[]{:S(2)}) collective-permute-start(f32[32,256]{1,0:T(8,128)S(1)} %get-tuple-element.114.carried_ref), channel_id=1, source_target_pairs={{0,6},{1,7},{2,4},{3,5},{4,2},{5,3},{6,0},{7,1},{8,14},{9,15},{10,... | collective-permute-start | bytes 98312 | tf_op jit(solution)/shard_map/ppermute | solution.py:20
  61.3 0.5 collective-permute-start.18
  61.8 0.7 collective-permute-start.23
  62.4 1.8 %collective-permute-done.19.cross_ref = f32[32,256]{1,0:T(8,128)S(1)} collective-permute-done((f32[32,256]{1,0:T(8,128)S(1)}, f32[32,256]{1,0:T(8,128)S(1)}, u32[]{:S(2)}, u32[]{:S(2)}) %collective-permute-start.19) | collective-permute-done | bytes 32800 | tf_op jit(solution)/shard_map/ppermute | solution.py:20
  64.2 1.0 %collective-permute-done.18.low_ref = f32[32,256]{1,0:T(8,128)S(1)} collective-permute-done((f32[32,256]{1,0:T(8,128)S(1)}, f32[32,256]{1,0:T(8,128)S(1)}, u32[]{:S(2)}, u32[]{:S(2)}) %collective-permute-start.18) | collective-permute-done | bytes 32800 | tf_op jit(solution)/shard_map/ppermute | solution.py:20
  65.2 0.7 shard_map.111
  65.9 2.1 %collective-permute-start.20 = (f32[32,256]{1,0:T(8,128)S(1)}, f32[32,256]{1,0:T(8,128)S(1)}, u32[]{:S(2)}, u32[]{:S(2)}) collective-permute-start(f32[32,256]{1,0:T(8,128)S(1)} %get-tuple-element.116), channel_id=1, source_target_pairs={{0,8},{1,9},{2,10},{3,11},{4,12},{5,13},{6,14},{7,15},{8,0},{9,1},... | collective-permute-start | bytes 98312 | tf_op jit(solution)/shard_map/ppermute | solution.py:20
  68.0 1.8 %collective-permute-start.22 = (f32[32,256]{1,0:T(8,128)S(1)}, f32[32,256]{1,0:T(8,128)S(1)}, u32[]{:S(2)}, u32[]{:S(2)}) collective-permute-start(f32[32,256]{1,0:T(8,128)S(1)} %get-tuple-element.117), channel_id=1, source_target_pairs={{0,24},{1,25},{2,26},{3,27},{4,28},{5,29},{6,30},{7,31},{8,16},{9,... | collective-permute-start | bytes 98312 | tf_op jit(solution)/shard_map/ppermute | solution.py:20
  69.8 0.5 collective-permute-start.21
  70.3 3.5 %collective-permute-done.22.refs_2_ = f32[32,256]{1,0:T(8,128)S(1)} collective-permute-done((f32[32,256]{1,0:T(8,128)S(1)}, f32[32,256]{1,0:T(8,128)S(1)}, u32[]{:S(2)}, u32[]{:S(2)}) %collective-permute-start.22) | collective-permute-done | bytes 32800 | tf_op jit(solution)/shard_map/ppermute | solution.py:20
  73.7 0.9 collective-permute-done.21.refs_1_
  74.6 0.7 shard_map.112
  75.3 0.1 collective-permute-start.24
  75.4 0.7 collective-permute-start.25
  76.1 1.0 %shard_map.113 = (f32[32,1024]{1,0:T(8,128)S(1)}, f32[32,1024]{1,0:T(8,128)S(1)}, f32[32,128]{1,0:T(8,128)S(1)}, f32[1,128]{1,0:T(1,128)S(1)}) custom-call(bf16[32,256]{1,0:T(8,128)(2,1)S(1)} %get-tuple-element.122.top_ref, bf16[32,256]{1,0:T(8,128)(2,1)S(1)} %get-tuple-element.123.previous_ref, f32[32,1024]{1,0:T(8,128)S(1)} %get-tuple-element.120.refs_8_.local_ref, ...), custom_call_target="tpu_custom_call" | custom-call | flops 100000000 | bytes 279040 | tf_op jit(solution)/shard_map/pallas_call | solution.py:34
  77.1 1.0 %shard_map.114 = f32[32,128]{1,0:T(8,128)} custom-call(f32[32,1024]{1,0:T(8,128)S(1)} %get-tuple-element.127.acc_ref, f32[32,256]{1,0:T(8,128)S(1)} %collective-permute-done.24.near_ref, f32[32,256]{1,0:T(8,128)S(1)} %collective-permute-done.25.far_ref, bf16[3,1024,256]{2,1,0:T(8,128)(2,1)S(1)} %get-tuple-element.70.s3_ref, ...), custom_call_target="tpu_custom_call" | custom-call | flops 30000000 | bytes 16384 | tf_op jit(solution)/shard_map/pallas_call | solution.py:34
  78.1 7.8 %all-to-all-start = ((f32[32,1,128]{2,1,0:T(1,128)}), f32[32,1,128]{2,1,0:T(1,128)S(1)}, u32[]{:S(2)}, u32[]{:S(2)}) async-start(f32[32,1,128]{2,1,0:T(1,128)} %bitcast.1), calls=%async_computation | async-start | bytes 32768 | tf_op jit(solution)/shard_map/all_to_all | solution.py:495
  85.8 0.7 copy.11
  86.5 6.5 %all-to-all-done = f32[32,1,128]{2,1,0:T(1,128)S(1)} async-done(((f32[32,1,128]{2,1,0:T(1,128)}), f32[32,1,128]{2,1,0:T(1,128)S(1)}, u32[]{:S(2)}, u32[]{:S(2)}) %all-to-all-start) | async-done | bytes 16416 | tf_op jit(solution)/shard_map/all_to_all | solution.py:495
  93.0 0.7 shard_map.115
  (12 shorter events, 0.0 us)
Async XLA Ops:
  1.8 1.8 %collective-permute-start = (bf16[608,256]{1,0:T(8,128)(2,1)S(1)}, bf16[608,256]{1,0:T(8,128)(2,1)S(1)}, u32[]{:S(2)}, u32[]{:S(2)}) collective-permute-start(bf16[608,256]{1,0:T(8,128)(2,1)S(1)} %get-tuple-element.68), channel_id=1, source_target_pairs={{0,1},{1,0},{2,3},{3,2},{4,5},{5,4},{6,7},{7,6},{8,9},{9,8},{10,11... | collective-permute-start | bytes 933896 | tf_op jit(solution)/shard_map/ppermute | solution.py:20
  3.9 6.7 %collective-permute-start.4 = (f32[128,256]{1,0:T(8,128)S(1)}, f32[128,256]{1,0:T(8,128)S(1)}, u32[]{:S(2)}, u32[]{:S(2)}) collective-permute-start(f32[128,256]{1,0:T(8,128)S(1)} %get-tuple-element.81), channel_id=1, source_target_pairs={{0,2},{1,3},{2,0},{3,1},{4,6},{5,7},{6,4},{7,5},{8,10},{9,11},{10,... | collective-permute-start | bytes 393224 | tf_op jit(solution)/shard_map/ppermute | solution.py:20
  10.6 1.3 %collective-permute-start.5 = (f32[128,256]{1,0:T(8,128)S(1)}, f32[128,256]{1,0:T(8,128)S(1)}, u32[]{:S(2)}, u32[]{:S(2)}) collective-permute-start(f32[128,256]{1,0:T(8,128)S(1)} %collective-permute-done.4.got_ref), channel_id=1, source_target_pairs={{0,1},{1,0},{2,3},{3,2},{4,5},{5,4},{6,7},{7,6},{8,9},{9,8},{10,11... | collective-permute-start | bytes 393224 | tf_op jit(solution)/shard_map/ppermute | solution.py:20
  12.6 5.6 %collective-permute-start.7 = (f32[128,256]{1,0:T(8,128)S(1)}, f32[128,256]{1,0:T(8,128)S(1)}, u32[]{:S(2)}, u32[]{:S(2)}) collective-permute-start(f32[128,256]{1,0:T(8,128)S(1)} %get-tuple-element.87), channel_id=1, source_target_pairs={{0,4},{1,5},{2,6},{3,7},{4,0},{5,1},{6,2},{7,3},{8,12},{9,13},{10,... | collective-permute-start | bytes 393224 | tf_op jit(solution)/shard_map/ppermute | solution.py:20
  18.2 1.3 %collective-permute-start.8 = (f32[128,256]{1,0:T(8,128)S(1)}, f32[128,256]{1,0:T(8,128)S(1)}, u32[]{:S(2)}, u32[]{:S(2)}) collective-permute-start(f32[128,256]{1,0:T(8,128)S(1)} %collective-permute-done.7.got_ref), channel_id=1, source_target_pairs={{0,1},{1,0},{2,3},{3,2},{4,5},{5,4},{6,7},{7,6},{8,9},{9,8},{10,11... | collective-permute-start | bytes 393224 | tf_op jit(solution)/shard_map/ppermute | solution.py:20
  18.2 9.9 %collective-permute-start.1 = (bf16[352,256]{1,0:T(8,128)(2,1)S(1)}, bf16[352,256]{1,0:T(8,128)(2,1)S(1)}, u32[]{:S(2)}, u32[]{:S(2)}) collective-permute-start(bf16[352,256]{1,0:T(8,128)(2,1)S(1)} %get-tuple-element.69), channel_id=1, source_target_pairs={{1,2},{3,4},{5,6},{7,8},{9,10},{11,12},{13,14},{15,16},{17,18},{19... | collective-permute-start | bytes 540680 | tf_op jit(solution)/shard_map/ppermute | solution.py:26
  20.2 9.8 %collective-permute-start.10 = (f32[128,256]{1,0:T(8,128)S(1)}, f32[128,256]{1,0:T(8,128)S(1)}, u32[]{:S(2)}, u32[]{:S(2)}) collective-permute-start(f32[128,256]{1,0:T(8,128)S(1)} %get-tuple-element.93), channel_id=1, source_target_pairs={{0,8},{1,9},{2,10},{3,11},{4,12},{5,13},{6,14},{7,15},{8,0},{9,1},... | collective-permute-start | bytes 393224 | tf_op jit(solution)/shard_map/ppermute | solution.py:20
  29.1 1.3 %collective-permute-start.2 = (f32[64,256]{1,0:T(8,128)S(1)}, f32[64,256]{1,0:T(8,128)S(1)}, u32[]{:S(2)}, u32[]{:S(2)}) collective-permute-start(f32[64,256]{1,0:T(8,128)S(1)} %get-tuple-element.75.both_ref), channel_id=1, source_target_pairs={{0,1},{1,0},{2,3},{3,2},{4,5},{5,4},{6,7},{7,6},{8,9},{9,8},{10,11... | collective-permute-start | bytes 196616 | tf_op jit(solution)/shard_map/ppermute | solution.py:20
  30.0 10.5 %collective-permute-start.11 = (f32[128,256]{1,0:T(8,128)S(1)}, f32[128,256]{1,0:T(8,128)S(1)}, u32[]{:S(2)}, u32[]{:S(2)}) collective-permute-start(f32[128,256]{1,0:T(8,128)S(1)} %collective-permute-done.10.got_ref), channel_id=1, source_target_pairs={{0,1},{1,0},{2,3},{3,2},{4,5},{5,4},{6,7},{7,6},{8,9},{9,8},{10,11... | collective-permute-start | bytes 393224 | tf_op jit(solution)/shard_map/ppermute | solution.py:20
  30.6 3.9 %collective-permute-start.3 = (f32[32,256]{1,0:T(8,128)S(1)}, f32[32,256]{1,0:T(8,128)S(1)}, u32[]{:S(2)}, u32[]{:S(2)}) collective-permute-start(f32[32,256]{1,0:T(8,128)S(1)} %get-tuple-element.77.total_ref), channel_id=1, source_target_pairs={{0,2},{1,3},{2,0},{3,1},{4,6},{5,7},{6,4},{7,5},{8,10},{9,11},{10,... | collective-permute-start | bytes 98312 | tf_op jit(solution)/shard_map/ppermute | solution.py:20
  34.7 4.0 %collective-permute-start.6 = (f32[32,256]{1,0:T(8,128)S(1)}, f32[32,256]{1,0:T(8,128)S(1)}, u32[]{:S(2)}, u32[]{:S(2)}) collective-permute-start(f32[32,256]{1,0:T(8,128)S(1)} %get-tuple-element.83.total_ref), channel_id=1, source_target_pairs={{0,4},{1,5},{2,6},{3,7},{4,0},{5,1},{6,2},{7,3},{8,12},{9,13},{10,... | collective-permute-start | bytes 98312 | tf_op jit(solution)/shard_map/ppermute | solution.py:20
  39.0 4.0 %collective-permute-start.9 = (f32[32,256]{1,0:T(8,128)S(1)}, f32[32,256]{1,0:T(8,128)S(1)}, u32[]{:S(2)}, u32[]{:S(2)}) collective-permute-start(f32[32,256]{1,0:T(8,128)S(1)} %get-tuple-element.89.total_ref), channel_id=1, source_target_pairs={{0,8},{1,9},{2,10},{3,11},{4,12},{5,13},{6,14},{7,15},{8,0},{9,1},... | collective-permute-start | bytes 98312 | tf_op jit(solution)/shard_map/ppermute | solution.py:20
  39.9 6.0 %collective-permute-start.13 = (f32[32,256]{1,0:T(8,128)S(1)}, f32[32,256]{1,0:T(8,128)S(1)}, u32[]{:S(2)}, u32[]{:S(2)}) collective-permute-start(f32[32,256]{1,0:T(8,128)S(1)} %get-tuple-element.98), channel_id=1, source_target_pairs={{1,2},{3,4},{5,6},{7,8},{9,10},{11,12},{13,14},{15,16},{17,18},{19... | collective-permute-start | bytes 98312 | tf_op jit(solution)/shard_map/ppermute | solution.py:26
  43.2 5.7 %collective-permute-start.12 = (f32[32,256]{1,0:T(8,128)S(1)}, f32[32,256]{1,0:T(8,128)S(1)}, u32[]{:S(2)}, u32[]{:S(2)}) collective-permute-start(f32[32,256]{1,0:T(8,128)S(1)} %get-tuple-element.95), channel_id=1, source_target_pairs={{0,16},{1,17},{2,18},{3,19},{4,20},{5,21},{6,22},{7,23},{8,24},{9,... | collective-permute-start | bytes 98312 | tf_op jit(solution)/shard_map/ppermute | solution.py:20
  49.6 1.8 %collective-permute-start.14 = (f32[32,256]{1,0:T(8,128)S(1)}, f32[32,256]{1,0:T(8,128)S(1)}, u32[]{:S(2)}, u32[]{:S(2)}) collective-permute-start(f32[32,256]{1,0:T(8,128)S(1)} %get-tuple-element.110), channel_id=1, source_target_pairs={{0,1},{1,0},{2,3},{3,2},{4,5},{5,4},{6,7},{7,6},{8,9},{9,8},{10,11... | collective-permute-start | bytes 98312 | tf_op jit(solution)/shard_map/ppermute | solution.py:20
  49.8 1.7 %collective-permute-start.15 = (f32[32,256]{1,0:T(8,128)S(1)}, f32[32,256]{1,0:T(8,128)S(1)}, u32[]{:S(2)}, u32[]{:S(2)}) collective-permute-start(f32[32,256]{1,0:T(8,128)S(1)} %get-tuple-element.111), channel_id=1, source_target_pairs={{1,2},{3,4},{5,6},{7,8},{9,10},{11,12},{13,14},{15,16},{17,18},{19... | collective-permute-start | bytes 98312 | tf_op jit(solution)/shard_map/ppermute | solution.py:26
  52.3 4.9 %collective-permute-start.16 = (f32[64,256]{1,0:T(8,128)S(1)}, f32[64,256]{1,0:T(8,128)S(1)}, u32[]{:S(2)}, u32[]{:S(2)}) collective-permute-start(f32[64,256]{1,0:T(8,128)S(1)} %get-tuple-element.112.both_ref), channel_id=1, source_target_pairs={{0,1},{1,0},{2,3},{3,2},{4,5},{5,4},{6,7},{7,6},{8,9},{9,8},{10,11... | collective-permute-start | bytes 196616 | tf_op jit(solution)/shard_map/ppermute | solution.py:20
  57.5 4.9 %collective-permute-start.17 = (f32[32,256]{1,0:T(8,128)S(1)}, f32[32,256]{1,0:T(8,128)S(1)}, u32[]{:S(2)}, u32[]{:S(2)}) collective-permute-start(f32[32,256]{1,0:T(8,128)S(1)} %get-tuple-element.113.total_ref), channel_id=1, source_target_pairs={{0,2},{1,3},{2,0},{3,1},{4,6},{5,7},{6,4},{7,5},{8,10},{9,11},{10,... | collective-permute-start | bytes 98312 | tf_op jit(solution)/shard_map/ppermute | solution.py:20
  59.4 4.8 %collective-permute-start.19 = (f32[32,256]{1,0:T(8,128)S(1)}, f32[32,256]{1,0:T(8,128)S(1)}, u32[]{:S(2)}, u32[]{:S(2)}) collective-permute-start(f32[32,256]{1,0:T(8,128)S(1)} %get-tuple-element.114.carried_ref), channel_id=1, source_target_pairs={{0,6},{1,7},{2,4},{3,5},{4,2},{5,3},{6,0},{7,1},{8,14},{9,15},{10,... | collective-permute-start | bytes 98312 | tf_op jit(solution)/shard_map/ppermute | solution.py:20
  61.3 3.9 %collective-permute-start.18 = (f32[32,256]{1,0:T(8,128)S(1)}, f32[32,256]{1,0:T(8,128)S(1)}, u32[]{:S(2)}, u32[]{:S(2)}) collective-permute-start(f32[32,256]{1,0:T(8,128)S(1)} %get-tuple-element.114.carried_ref), channel_id=1, source_target_pairs={{0,4},{1,5},{2,6},{3,7},{4,0},{5,1},{6,2},{7,3},{8,12},{9,13},{10,... | collective-permute-start | bytes 98312 | tf_op jit(solution)/shard_map/ppermute | solution.py:20
  61.8 8.5 %collective-permute-start.23 = (f32[32,256]{1,0:T(8,128)S(1)}, f32[32,256]{1,0:T(8,128)S(1)}, u32[]{:S(2)}, u32[]{:S(2)}) collective-permute-start(f32[32,256]{1,0:T(8,128)S(1)} %get-tuple-element.119), channel_id=1, source_target_pairs={{1,2},{3,4},{5,6},{7,8},{9,10},{11,12},{13,14},{15,16},{17,18},{19... | collective-permute-start | bytes 98312 | tf_op jit(solution)/shard_map/ppermute | solution.py:26
  65.9 4.3 %collective-permute-start.20 = (f32[32,256]{1,0:T(8,128)S(1)}, f32[32,256]{1,0:T(8,128)S(1)}, u32[]{:S(2)}, u32[]{:S(2)}) collective-permute-start(f32[32,256]{1,0:T(8,128)S(1)} %get-tuple-element.116), channel_id=1, source_target_pairs={{0,8},{1,9},{2,10},{3,11},{4,12},{5,13},{6,14},{7,15},{8,0},{9,1},... | collective-permute-start | bytes 98312 | tf_op jit(solution)/shard_map/ppermute | solution.py:20
  68.0 5.7 %collective-permute-start.22 = (f32[32,256]{1,0:T(8,128)S(1)}, f32[32,256]{1,0:T(8,128)S(1)}, u32[]{:S(2)}, u32[]{:S(2)}) collective-permute-start(f32[32,256]{1,0:T(8,128)S(1)} %get-tuple-element.117), channel_id=1, source_target_pairs={{0,24},{1,25},{2,26},{3,27},{4,28},{5,29},{6,30},{7,31},{8,16},{9,... | collective-permute-start | bytes 98312 | tf_op jit(solution)/shard_map/ppermute | solution.py:20
  69.8 4.8 %collective-permute-start.21 = (f32[32,256]{1,0:T(8,128)S(1)}, f32[32,256]{1,0:T(8,128)S(1)}, u32[]{:S(2)}, u32[]{:S(2)}) collective-permute-start(f32[32,256]{1,0:T(8,128)S(1)} %get-tuple-element.117), channel_id=1, source_target_pairs={{0,16},{1,17},{2,18},{3,19},{4,20},{5,21},{6,22},{7,23},{8,24},{9,... | collective-permute-start | bytes 98312 | tf_op jit(solution)/shard_map/ppermute | solution.py:20
  75.3 1.8 %collective-permute-start.24 = (f32[32,256]{1,0:T(8,128)S(1)}, f32[32,256]{1,0:T(8,128)S(1)}, u32[]{:S(2)}, u32[]{:S(2)}) collective-permute-start(f32[32,256]{1,0:T(8,128)S(1)} %get-tuple-element.128), channel_id=1, source_target_pairs={{0,1},{1,0},{2,3},{3,2},{4,5},{5,4},{6,7},{7,6},{8,9},{9,8},{10,11... | collective-permute-start | bytes 98312 | tf_op jit(solution)/shard_map/ppermute | solution.py:20
  75.4 1.7 %collective-permute-start.25 = (f32[32,256]{1,0:T(8,128)S(1)}, f32[32,256]{1,0:T(8,128)S(1)}, u32[]{:S(2)}, u32[]{:S(2)}) collective-permute-start(f32[32,256]{1,0:T(8,128)S(1)} %get-tuple-element.129), channel_id=1, source_target_pairs={{1,2},{3,4},{5,6},{7,8},{9,10},{11,12},{13,14},{15,16},{17,18},{19... | collective-permute-start | bytes 98312 | tf_op jit(solution)/shard_map/ppermute | solution.py:26
  78.1 14.9 %all-to-all-start = ((f32[32,1,128]{2,1,0:T(1,128)}), f32[32,1,128]{2,1,0:T(1,128)S(1)}, u32[]{:S(2)}, u32[]{:S(2)}) async-start(f32[32,1,128]{2,1,0:T(1,128)} %bitcast.1), calls=%async_computation | async-start | bytes 32768 | tf_op jit(solution)/shard_map/all_to_all | solution.py:495

commit v2 on v1

--- a/solution.py
+++ b/solution.py
@@ -237,7 +237,7 @@
         mix_ref[j] = part
 
 
-def start_static_kernel(own_ref, near_ref, second_ref, prefix_ref, whole_ref=None, half_ref=None):
+def pair_kernel(own_ref, near_ref, second_ref, prefix_ref, whole_ref):
     right = on_right(0)
     width = own_ref.shape[0]
     own = own_ref[...].astype(F32)
@@ -250,30 +250,39 @@
     prefix = jnp.where(right, other, jnp.where(row == col, 1.0, 0.0))
     for j, part in enumerate(split3(prefix)):
         prefix_ref[j] = part
-    if whole_ref is not None:
-        whole = dot(first, second)
-        half = half_ref.shape[0]
-        half_ref[...] = jnp.where(right, whole[half:], whole[:half])
-        whole_ref[...] = whole
-
-
-def static_kernel(whole_ref, got_ref, twin_ref, prefix_ref, second_ref, prefix_out, whole_out=None, half_out=None, *, level):
-    even, right = is_even(), on_right(level)
-    half = got_ref.shape[0]
-    got, twin = got_ref[...], twin_ref[...]
-    other = jnp.concatenate([jnp.where(even, got, twin), jnp.where(even, twin, got)], 0)
-    whole = whole_ref[...]
+    whole_ref[...] = dot(first, second)
+
+
+def next_level(level, whole, other, prefix, second_ref, prefix_out, whole_out=None, half_out=None):
+    right = on_right(level)
     second3 = split3(jnp.where(right, whole, other))
     first3 = split3(jnp.where(right, other, whole))
     for j, part in enumerate(second3):
         second_ref[j] = part
+    product = None
     if whole_out is not None:
-        both = times_split(first3, *second3)
-        whole_out[...] = both
-        half_out[...] = jnp.where(even, both[:half], both[half:])
-    prefix = [prefix_ref[j] for j in range(3)]
+        product = times_split(first3, *second3)
+        whole_out[...] = product
+        if half_out is not None:
+            half = half_out.shape[0]
+            half_out[...] = jnp.where(is_even(), product[:half], product[half:])
     for j, part in enumerate(split3(times_split(first3, *prefix))):
-        prefix_out[j] = jnp.where(right, part.astype(F32), prefix[j].astype(F32)).astype(BF16)
+        prefix_out[j] = choose(right, part, prefix[j])
+    return product
+
+
+def static_kernel(whole_ref, got_ref, twin_ref, prefix_ref, *outs, level):
+    even = is_even()
+    got, twin = got_ref[...], twin_ref[...]
+    other = jnp.concatenate([jnp.where(even, got, twin), jnp.where(even, twin, got)], 0)
+    next_level(level, whole_ref[...], other, parts_of(prefix_ref), *outs)
+
+
+def chip_kernel(whole_ref, got_ref, twin_ref, prefix_ref, *outs):
+    even = is_even()
+    got, twin = got_ref[...], twin_ref[...]
+    other = dot(choose(even, got, twin), choose(even, twin, got))
+    next_level(1, whole_ref[...], other, parts_of(prefix_ref), *outs)
 
 
 def merged(right, total, got, matrix):
@@ -421,17 +430,17 @@
     )
     before, after, mix = kernel_call(mix_kernel, [low_square, low_square, triple], near, far, chain)
 
-    outs = [square, half]
-    second, prefix, *rest = kernel_call(start_static_kernel, [low_square, triple] + outs * (levels > 2), chain, near)
+    second, prefix, whole = kernel_call(pair_kernel, [low_square, triple, square], chain, near)
     seconds, reaches = [second], [None, prefix]
     for level in range(1, levels - 1):
-        whole, piece = rest
-        got = exchange(piece, 1 << level)
+        got = exchange(chain if level == 1 else piece, 1 << level)
         twin = exchange(got, 1)
+        kernel = chip_kernel if level == 1 else functools.partial(static_kernel, level=level)
         second, prefix, *rest = kernel_call(
-            functools.partial(static_kernel, level=level),
-            [triple, triple] + outs * (level < levels - 2), whole, got, twin, prefix, micros=1,
+            kernel, [triple, triple] + [square, half] * (level < levels - 2), whole, got, twin, prefix, micros=1
         )
+        if rest:
+            whole, piece = rest
         seconds.append(second)
         reaches.append(prefix)
 

time: 93.9 us -> 92.5 us (0.985)
  waiting for transfers between devices: 37.5 us -> 36.3 us
    ppermute x21, waiting for transfers between devices: 30.9 us -> 29.8 us  [exchange(): return lax.ppermute(values, AXIS, [(i, i ^ distance) for i in range(count)])]
  transfers between devices with their start and end apart: 27 -> 27, of which waited for: 17 -> 16; matrix products, arithmetic and copies ran while one was open for 1% -> 1% of each run, Pallas kernels for 9% -> 10%
where the time goes in v2:
time: 92.5 us; the launch traced here: 92.3 us
  starting transfers between devices  39.4 us (43%)
  waiting for transfers between devices  36.3 us (39%)
  Pallas kernels  15 us (16%)
    ppermute x21, waiting for transfers between devices, exchange(): return lax.ppermute(values, AXIS, [(i, i ^ distance) for i in range(count)])  29.8 us
    ppermute x21, starting transfers between devices, exchange(): return lax.ppermute(values, AXIS, [(i, i ^ distance) for i in range(count)])  28.4 us
    pallas_call x20, Pallas kernels, kernel_call(): pl.pallas_call(kernel, in_specs=specs, out_specs=[pl.BlockSpec(memory_spa...  14.4 us
    all_to_all x1, starting transfers between devices, body(): gathered = lax.all_to_all(mine, AXIS, 0, 0, tiled=True)  7.75 us
    all_to_all x1, waiting for transfers between devices, body(): gathered = lax.all_to_all(mine, AXIS, 0, 0, tiled=True)  6.51 us
    ppermute x5, starting transfers between devices, across(): return lax.ppermute(values, AXIS, pairs + [(b, a) for a, b in pairs])  3.28 us
  transfers between devices with their start and end apart: 27, of which 16 were waited for; matrix products, arithmetic and copies ran while one was open for 1% of the time, Pallas kernels for 10%

profile of v2, /device:TPU:0, one launch (start us, length us, event | category | flops | bytes accessed | tf_op | source)
XLA Modules:
  0.0 92.3 jit_solution(9879082992124189050)
XLA Ops:
  0.6 1.2 %shard_map.96 = (bf16[608,256]{1,0:T(8,128)(2,1)S(1)}, bf16[352,256]{1,0:T(8,128)(2,1)S(1)}, bf16[256,256]{1,0:T(8,128)(2,1)S(1)}) custom-call(f32[32,1024]{1,0:T(8,128)} %x_hbm.3, bf16[256,1024]{1,0:T(8,128)(2,1)} %u_hbm.3, bf16[256,1024]{1,0:T(8,128)(2,1)} %l_hbm.3), custom_call_target="tpu_custom_call" | custom-call | flops 30000000 | bytes 622592 | tf_op jit(solution)/shard_map/pallas_call | solution.py:34
  1.8 0.6 collective-permute-start
  2.4 2.6 %collective-permute-start.4 = (bf16[256,256]{1,0:T(8,128)(2,1)S(1)}, bf16[256,256]{1,0:T(8,128)(2,1)S(1)}, u32[]{:S(2)}, u32[]{:S(2)}) collective-permute-start(bf16[256,256]{1,0:T(8,128)(2,1)S(1)} %get-tuple-element.72.chain_ref.own_ref.refs_11_.refs_14_), channel_id=1, source_target_pairs={{0,2},{1,3},{2,0},{3,1},{4,6},{5,7},{6,4},{7,5},{8,10},{9,11},{10,... | collective-permute-start | bytes 393224 | tf_op jit(solution)/shard_map/ppermute | solution.py:20
  4.9 4.1 %collective-permute-done.4.got_ref = bf16[256,256]{1,0:T(8,128)(2,1)S(1)} collective-permute-done((bf16[256,256]{1,0:T(8,128)(2,1)S(1)}, bf16[256,256]{1,0:T(8,128)(2,1)S(1)}, u32[]{:S(2)}, u32[]{:S(2)}) %collective-permute-start.4) | collective-permute-done | bytes 131104 | tf_op jit(solution)/shard_map/ppermute | solution.py:20
  9.0 0.3 shard_map.99
  9.3 1.1 %collective-permute-done.5.twin_ref = bf16[256,256]{1,0:T(8,128)(2,1)S(1)} collective-permute-done((bf16[256,256]{1,0:T(8,128)(2,1)S(1)}, bf16[256,256]{1,0:T(8,128)(2,1)S(1)}, u32[]{:S(2)}, u32[]{:S(2)}) %collective-permute-start.5) | collective-permute-done | bytes 131104 | tf_op jit(solution)/shard_map/ppermute | solution.py:20
  10.4 0.8 shard_map.101
  11.2 1.8 %collective-permute-start.7 = (f32[128,256]{1,0:T(8,128)S(1)}, f32[128,256]{1,0:T(8,128)S(1)}, u32[]{:S(2)}, u32[]{:S(2)}) collective-permute-start(f32[128,256]{1,0:T(8,128)S(1)} %get-tuple-element.85), channel_id=1, source_target_pairs={{0,4},{1,5},{2,6},{3,7},{4,0},{5,1},{6,2},{7,3},{8,12},{9,13},{10,... | collective-permute-start | bytes 393224 | tf_op jit(solution)/shard_map/ppermute | solution.py:20
  13.0 3.8 %collective-permute-done.7.got_ref = f32[128,256]{1,0:T(8,128)S(1)} collective-permute-done((f32[128,256]{1,0:T(8,128)S(1)}, f32[128,256]{1,0:T(8,128)S(1)}, u32[]{:S(2)}, u32[]{:S(2)}) %collective-permute-start.7) | collective-permute-done | bytes 131104 | tf_op jit(solution)/shard_map/ppermute | solution.py:20
  16.8 0.7 collective-permute-start.1
  17.5 0.7 collective-permute-done.8.twin_ref
  18.2 0.6 shard_map.103
  18.8 4.9 %collective-permute-start.10 = (f32[128,256]{1,0:T(8,128)S(1)}, f32[128,256]{1,0:T(8,128)S(1)}, u32[]{:S(2)}, u32[]{:S(2)}) collective-permute-start(f32[128,256]{1,0:T(8,128)S(1)} %get-tuple-element.91), channel_id=1, source_target_pairs={{0,8},{1,9},{2,10},{3,11},{4,12},{5,13},{6,14},{7,15},{8,0},{9,1},... | collective-permute-start | bytes 393224 | tf_op jit(solution)/shard_map/ppermute | solution.py:20
  23.7 3.0 %shard_map.95 = (f32[32,1024]{1,0:T(8,128)S(1)}, f32[32,1024]{1,0:T(8,128)S(1)}, f32[32,1024]{1,0:T(8,128)S(1)}, bf16[3,1024,256]{2,1,0:T(8,128)(2,1)S(1)}, bf16...) custom-call(f32[32,1024]{1,0:T(8,128)} %b_hbm.1, ...), custom_call_target="tpu_custom_call" | custom-call | flops 300000000 | bytes 8257536 | tf_op jit(solution)/shard_map/pallas_call | solution.py:34
  26.7 0.2 shard_map.97
  26.9 0.8 shard_map.98
  27.7 0.1 collective-permute-start.2
  27.8 0.8 collective-permute-done.10.got_ref
  28.6 0.0 collective-permute-start.11
  28.6 0.4 collective-permute-done.2.got_ref.refs_3_
  29.0 0.1 shard_map.100
  29.2 1.0 %collective-permute-start.3 = (f32[32,256]{1,0:T(8,128)S(1)}, f32[32,256]{1,0:T(8,128)S(1)}, u32[]{:S(2)}, u32[]{:S(2)}) collective-permute-start(f32[32,256]{1,0:T(8,128)S(1)} %get-tuple-element.76.total_ref), channel_id=1, source_target_pairs={{0,2},{1,3},{2,0},{3,1},{4,6},{5,7},{6,4},{7,5},{8,10},{9,11},{10,... | collective-permute-start | bytes 98312 | tf_op jit(solution)/shard_map/ppermute | solution.py:20
  30.2 2.9 %collective-permute-done.3.got_ref = f32[32,256]{1,0:T(8,128)S(1)} collective-permute-done((f32[32,256]{1,0:T(8,128)S(1)}, f32[32,256]{1,0:T(8,128)S(1)}, u32[]{:S(2)}, u32[]{:S(2)}) %collective-permute-start.3) | collective-permute-done | bytes 32800 | tf_op jit(solution)/shard_map/ppermute | solution.py:20
  33.1 0.2 shard_map.102
  33.3 1.1 %collective-permute-start.6 = (f32[32,256]{1,0:T(8,128)S(1)}, f32[32,256]{1,0:T(8,128)S(1)}, u32[]{:S(2)}, u32[]{:S(2)}) collective-permute-start(f32[32,256]{1,0:T(8,128)S(1)} %get-tuple-element.81.total_ref), channel_id=1, source_target_pairs={{0,4},{1,5},{2,6},{3,7},{4,0},{5,1},{6,2},{7,3},{8,12},{9,13},{10,... | collective-permute-start | bytes 98312 | tf_op jit(solution)/shard_map/ppermute | solution.py:20
  34.4 2.9 %collective-permute-done.6.got_ref = f32[32,256]{1,0:T(8,128)S(1)} collective-permute-done((f32[32,256]{1,0:T(8,128)S(1)}, f32[32,256]{1,0:T(8,128)S(1)}, u32[]{:S(2)}, u32[]{:S(2)}) %collective-permute-start.6) | collective-permute-done | bytes 32800 | tf_op jit(solution)/shard_map/ppermute | solution.py:20
  37.3 0.2 shard_map.104
  37.6 0.9 collective-permute-start.9
  38.5 0.7 collective-permute-start.13
  39.1 0.4 shard_map.105
  39.6 2.0 %collective-permute-done.9.got_ref = f32[32,256]{1,0:T(8,128)S(1)} collective-permute-done((f32[32,256]{1,0:T(8,128)S(1)}, f32[32,256]{1,0:T(8,128)S(1)}, u32[]{:S(2)}, u32[]{:S(2)}) %collective-permute-start.9) | collective-permute-done | bytes 32800 | tf_op jit(solution)/shard_map/ppermute | solution.py:20
  41.5 0.2 shard_map.106
  41.8 2.6 %collective-permute-start.12 = (f32[32,256]{1,0:T(8,128)S(1)}, f32[32,256]{1,0:T(8,128)S(1)}, u32[]{:S(2)}, u32[]{:S(2)}) collective-permute-start(f32[32,256]{1,0:T(8,128)S(1)} %get-tuple-element.93), channel_id=1, source_target_pairs={{0,16},{1,17},{2,18},{3,19},{4,20},{5,21},{6,22},{7,23},{8,24},{9,... | collective-permute-start | bytes 98312 | tf_op jit(solution)/shard_map/ppermute | solution.py:20
  44.4 3.1 %collective-permute-done.12.refs_0_ = f32[32,256]{1,0:T(8,128)S(1)} collective-permute-done((f32[32,256]{1,0:T(8,128)S(1)}, f32[32,256]{1,0:T(8,128)S(1)}, u32[]{:S(2)}, u32[]{:S(2)}) %collective-permute-start.12) | collective-permute-done | bytes 32800 | tf_op jit(solution)/shard_map/ppermute | solution.py:20
  47.5 0.7 shard_map.107
  48.2 0.2 collective-permute-start.14
  48.4 0.7 collective-permute-start.15
  49.0 1.0 %shard_map.108 = (f32[32,1024]{1,0:T(8,128)S(1)}, f32[32,1024]{1,0:T(8,128)S(1)}) custom-call(bf16[32,256]{1,0:T(8,128)(2,1)S(1)} %get-tuple-element.103.top_ref, bf16[32,256]{1,0:T(8,128)(2,1)S(1)} %get-tuple-element.104.previous_ref, f32[32,1024]{1,0:T(8,128)S(1)} %get-tuple-element.97.refs_5_.local_ref, f32[32,1024]{1,0:T(8,128)S(1)} %get-tuple-element.98.refs_6_.x_ref, ...), custom_call_target="tpu_custom_call" | custom-call | flops 100000000 | bytes 262144 | tf_op jit(solution)/shard_map/pallas_call | solution.py:34
  50.0 0.0 collective-permute-done.14.near_ref
  50.1 0.8 shard_map.109
  50.9 4.0 %collective-permute-start.16 = (f32[64,256]{1,0:T(8,128)S(1)}, f32[64,256]{1,0:T(8,128)S(1)}, u32[]{:S(2)}, u32[]{:S(2)}) collective-permute-start(f32[64,256]{1,0:T(8,128)S(1)} %get-tuple-element.110.both_ref), channel_id=1, source_target_pairs={{0,1},{1,0},{2,3},{3,2},{4,5},{5,4},{6,7},{7,6},{8,9},{9,8},{10,11... | collective-permute-start | bytes 196616 | tf_op jit(solution)/shard_map/ppermute | solution.py:20
  54.9 0.9 collective-permute-done.16.got_ref.refs_6_
  55.8 0.3 shard_map.110
  56.1 1.9 %collective-permute-start.17 = (f32[32,256]{1,0:T(8,128)S(1)}, f32[32,256]{1,0:T(8,128)S(1)}, u32[]{:S(2)}, u32[]{:S(2)}) collective-permute-start(f32[32,256]{1,0:T(8,128)S(1)} %get-tuple-element.111.total_ref), channel_id=1, source_target_pairs={{0,2},{1,3},{2,0},{3,1},{4,6},{5,7},{6,4},{7,5},{8,10},{9,11},{10,... | collective-permute-start | bytes 98312 | tf_op jit(solution)/shard_map/ppermute | solution.py:20
  58.0 1.9 %collective-permute-start.19 = (f32[32,256]{1,0:T(8,128)S(1)}, f32[32,256]{1,0:T(8,128)S(1)}, u32[]{:S(2)}, u32[]{:S(2)}) collective-permute-start(f32[32,256]{1,0:T(8,128)S(1)} %get-tuple-element.112.carried_ref), channel_id=1, source_target_pairs={{0,6},{1,7},{2,4},{3,5},{4,2},{5,3},{6,0},{7,1},{8,14},{9,15},{10,... | collective-permute-start | bytes 98312 | tf_op jit(solution)/shard_map/ppermute | solution.py:20
  59.9 0.5 collective-permute-start.18
  60.4 0.7 collective-permute-start.23
  61.0 1.8 %collective-permute-done.19.cross_ref = f32[32,256]{1,0:T(8,128)S(1)} collective-permute-done((f32[32,256]{1,0:T(8,128)S(1)}, f32[32,256]{1,0:T(8,128)S(1)}, u32[]{:S(2)}, u32[]{:S(2)}) %collective-permute-start.19) | collective-permute-done | bytes 32800 | tf_op jit(solution)/shard_map/ppermute | solution.py:20
  62.8 1.0 %collective-permute-done.18.low_ref = f32[32,256]{1,0:T(8,128)S(1)} collective-permute-done((f32[32,256]{1,0:T(8,128)S(1)}, f32[32,256]{1,0:T(8,128)S(1)}, u32[]{:S(2)}, u32[]{:S(2)}) %collective-permute-start.18) | collective-permute-done | bytes 32800 | tf_op jit(solution)/shard_map/ppermute | solution.py:20
  63.8 0.7 shard_map.111
  64.5 2.1 %collective-permute-start.20 = (f32[32,256]{1,0:T(8,128)S(1)}, f32[32,256]{1,0:T(8,128)S(1)}, u32[]{:S(2)}, u32[]{:S(2)}) collective-permute-start(f32[32,256]{1,0:T(8,128)S(1)} %get-tuple-element.114), channel_id=1, source_target_pairs={{0,8},{1,9},{2,10},{3,11},{4,12},{5,13},{6,14},{7,15},{8,0},{9,1},... | collective-permute-start | bytes 98312 | tf_op jit(solution)/shard_map/ppermute | solution.py:20
  66.6 1.8 %collective-permute-start.22 = (f32[32,256]{1,0:T(8,128)S(1)}, f32[32,256]{1,0:T(8,128)S(1)}, u32[]{:S(2)}, u32[]{:S(2)}) collective-permute-start(f32[32,256]{1,0:T(8,128)S(1)} %get-tuple-element.115), channel_id=1, source_target_pairs={{0,24},{1,25},{2,26},{3,27},{4,28},{5,29},{6,30},{7,31},{8,16},{9,... | collective-permute-start | bytes 98312 | tf_op jit(solution)/shard_map/ppermute | solution.py:20
  68.4 0.5 collective-permute-start.21
  68.8 3.5 %collective-permute-done.22.refs_2_ = f32[32,256]{1,0:T(8,128)S(1)} collective-permute-done((f32[32,256]{1,0:T(8,128)S(1)}, f32[32,256]{1,0:T(8,128)S(1)}, u32[]{:S(2)}, u32[]{:S(2)}) %collective-permute-start.22) | collective-permute-done | bytes 32800 | tf_op jit(solution)/shard_map/ppermute | solution.py:20
  72.3 0.9 collective-permute-done.21.refs_1_
  73.2 0.7 shard_map.112
  73.9 0.1 collective-permute-start.24
  74.0 0.7 collective-permute-start.25
  74.7 1.0 %shard_map.113 = (f32[32,1024]{1,0:T(8,128)S(1)}, f32[32,1024]{1,0:T(8,128)S(1)}, f32[32,128]{1,0:T(8,128)S(1)}, f32[1,128]{1,0:T(1,128)S(1)}) custom-call(bf16[32,256]{1,0:T(8,128)(2,1)S(1)} %get-tuple-element.120.top_ref, bf16[32,256]{1,0:T(8,128)(2,1)S(1)} %get-tuple-element.121.previous_ref, f32[32,1024]{1,0:T(8,128)S(1)} %get-tuple-element.118.refs_8_.local_ref, ...), custom_call_target="tpu_custom_call" | custom-call | flops 100000000 | bytes 279040 | tf_op jit(solution)/shard_map/pallas_call | solution.py:34
  75.7 1.0 %shard_map.114 = f32[32,128]{1,0:T(8,128)} custom-call(f32[32,1024]{1,0:T(8,128)S(1)} %get-tuple-element.125.acc_ref, f32[32,256]{1,0:T(8,128)S(1)} %collective-permute-done.24.near_ref, f32[32,256]{1,0:T(8,128)S(1)} %collective-permute-done.25.far_ref, bf16[3,1024,256]{2,1,0:T(8,128)(2,1)S(1)} %get-tuple-element.69.s3_ref, ...), custom_call_target="tpu_custom_call" | custom-call | flops 30000000 | bytes 16384 | tf_op jit(solution)/shard_map/pallas_call | solution.py:34
  76.7 7.8 %all-to-all-start = ((f32[32,1,128]{2,1,0:T(1,128)}), f32[32,1,128]{2,1,0:T(1,128)S(1)}, u32[]{:S(2)}, u32[]{:S(2)}) async-start(f32[32,1,128]{2,1,0:T(1,128)} %bitcast.1), calls=%async_computation | async-start | bytes 32768 | tf_op jit(solution)/shard_map/all_to_all | solution.py:504
  84.4 0.7 copy.11
  85.1 6.5 %all-to-all-done = f32[32,1,128]{2,1,0:T(1,128)S(1)} async-done(((f32[32,1,128]{2,1,0:T(1,128)}), f32[32,1,128]{2,1,0:T(1,128)S(1)}, u32[]{:S(2)}, u32[]{:S(2)}) %all-to-all-start) | async-done | bytes 16416 | tf_op jit(solution)/shard_map/all_to_all | solution.py:504
  91.6 0.7 shard_map.115
  (12 shorter events, 0.0 us)
Async XLA Ops:
  1.8 7.2 %collective-permute-start = (bf16[608,256]{1,0:T(8,128)(2,1)S(1)}, bf16[608,256]{1,0:T(8,128)(2,1)S(1)}, u32[]{:S(2)}, u32[]{:S(2)}) collective-permute-start(bf16[608,256]{1,0:T(8,128)(2,1)S(1)} %get-tuple-element.67), channel_id=1, source_target_pairs={{0,1},{1,0},{2,3},{3,2},{4,5},{5,4},{6,7},{7,6},{8,9},{9,8},{10,11... | collective-permute-start | bytes 933896 | tf_op jit(solution)/shard_map/ppermute | solution.py:20
  2.4 6.6 %collective-permute-start.4 = (bf16[256,256]{1,0:T(8,128)(2,1)S(1)}, bf16[256,256]{1,0:T(8,128)(2,1)S(1)}, u32[]{:S(2)}, u32[]{:S(2)}) collective-permute-start(bf16[256,256]{1,0:T(8,128)(2,1)S(1)} %get-tuple-element.72.chain_ref.own_ref.refs_11_.refs_14_), channel_id=1, source_target_pairs={{0,2},{1,3},{2,0},{3,1},{4,6},{5,7},{6,4},{7,5},{8,10},{9,11},{10,... | collective-permute-start | bytes 393224 | tf_op jit(solution)/shard_map/ppermute | solution.py:20
  9.0 1.3 %collective-permute-start.5 = (bf16[256,256]{1,0:T(8,128)(2,1)S(1)}, bf16[256,256]{1,0:T(8,128)(2,1)S(1)}, u32[]{:S(2)}, u32[]{:S(2)}) collective-permute-start(bf16[256,256]{1,0:T(8,128)(2,1)S(1)} %collective-permute-done.4.got_ref), channel_id=1, source_target_pairs={{0,1},{1,0},{2,3},{3,2},{4,5},{5,4},{6,7},{7,6},{8,9},{9,8},{10,11... | collective-permute-start | bytes 393224 | tf_op jit(solution)/shard_map/ppermute | solution.py:20
  11.2 5.6 %collective-permute-start.7 = (f32[128,256]{1,0:T(8,128)S(1)}, f32[128,256]{1,0:T(8,128)S(1)}, u32[]{:S(2)}, u32[]{:S(2)}) collective-permute-start(f32[128,256]{1,0:T(8,128)S(1)} %get-tuple-element.85), channel_id=1, source_target_pairs={{0,4},{1,5},{2,6},{3,7},{4,0},{5,1},{6,2},{7,3},{8,12},{9,13},{10,... | collective-permute-start | bytes 393224 | tf_op jit(solution)/shard_map/ppermute | solution.py:20
  16.8 1.3 %collective-permute-start.8 = (f32[128,256]{1,0:T(8,128)S(1)}, f32[128,256]{1,0:T(8,128)S(1)}, u32[]{:S(2)}, u32[]{:S(2)}) collective-permute-start(f32[128,256]{1,0:T(8,128)S(1)} %collective-permute-done.7.got_ref), channel_id=1, source_target_pairs={{0,1},{1,0},{2,3},{3,2},{4,5},{5,4},{6,7},{7,6},{8,9},{9,8},{10,11... | collective-permute-start | bytes 393224 | tf_op jit(solution)/shard_map/ppermute | solution.py:20
  16.8 9.9 %collective-permute-start.1 = (bf16[352,256]{1,0:T(8,128)(2,1)S(1)}, bf16[352,256]{1,0:T(8,128)(2,1)S(1)}, u32[]{:S(2)}, u32[]{:S(2)}) collective-permute-start(bf16[352,256]{1,0:T(8,128)(2,1)S(1)} %get-tuple-element.68), channel_id=1, source_target_pairs={{1,2},{3,4},{5,6},{7,8},{9,10},{11,12},{13,14},{15,16},{17,18},{19... | collective-permute-start | bytes 540680 | tf_op jit(solution)/shard_map/ppermute | solution.py:26
  18.8 9.8 %collective-permute-start.10 = (f32[128,256]{1,0:T(8,128)S(1)}, f32[128,256]{1,0:T(8,128)S(1)}, u32[]{:S(2)}, u32[]{:S(2)}) collective-permute-start(f32[128,256]{1,0:T(8,128)S(1)} %get-tuple-element.91), channel_id=1, source_target_pairs={{0,8},{1,9},{2,10},{3,11},{4,12},{5,13},{6,14},{7,15},{8,0},{9,1},... | collective-permute-start | bytes 393224 | tf_op jit(solution)/shard_map/ppermute | solution.py:20
  27.7 1.3 %collective-permute-start.2 = (f32[64,256]{1,0:T(8,128)S(1)}, f32[64,256]{1,0:T(8,128)S(1)}, u32[]{:S(2)}, u32[]{:S(2)}) collective-permute-start(f32[64,256]{1,0:T(8,128)S(1)} %get-tuple-element.74.both_ref), channel_id=1, source_target_pairs={{0,1},{1,0},{2,3},{3,2},{4,5},{5,4},{6,7},{7,6},{8,9},{9,8},{10,11... | collective-permute-start | bytes 196616 | tf_op jit(solution)/shard_map/ppermute | solution.py:20
  28.6 10.5 %collective-permute-start.11 = (f32[128,256]{1,0:T(8,128)S(1)}, f32[128,256]{1,0:T(8,128)S(1)}, u32[]{:S(2)}, u32[]{:S(2)}) collective-permute-start(f32[128,256]{1,0:T(8,128)S(1)} %collective-permute-done.10.got_ref), channel_id=1, source_target_pairs={{0,1},{1,0},{2,3},{3,2},{4,5},{5,4},{6,7},{7,6},{8,9},{9,8},{10,11... | collective-permute-start | bytes 393224 | tf_op jit(solution)/shard_map/ppermute | solution.py:20
  29.2 3.9 %collective-permute-start.3 = (f32[32,256]{1,0:T(8,128)S(1)}, f32[32,256]{1,0:T(8,128)S(1)}, u32[]{:S(2)}, u32[]{:S(2)}) collective-permute-start(f32[32,256]{1,0:T(8,128)S(1)} %get-tuple-element.76.total_ref), channel_id=1, source_target_pairs={{0,2},{1,3},{2,0},{3,1},{4,6},{5,7},{6,4},{7,5},{8,10},{9,11},{10,... | collective-permute-start | bytes 98312 | tf_op jit(solution)/shard_map/ppermute | solution.py:20
  33.3 4.0 %collective-permute-start.6 = (f32[32,256]{1,0:T(8,128)S(1)}, f32[32,256]{1,0:T(8,128)S(1)}, u32[]{:S(2)}, u32[]{:S(2)}) collective-permute-start(f32[32,256]{1,0:T(8,128)S(1)} %get-tuple-element.81.total_ref), channel_id=1, source_target_pairs={{0,4},{1,5},{2,6},{3,7},{4,0},{5,1},{6,2},{7,3},{8,12},{9,13},{10,... | collective-permute-start | bytes 98312 | tf_op jit(solution)/shard_map/ppermute | solution.py:20
  37.6 4.0 %collective-permute-start.9 = (f32[32,256]{1,0:T(8,128)S(1)}, f32[32,256]{1,0:T(8,128)S(1)}, u32[]{:S(2)}, u32[]{:S(2)}) collective-permute-start(f32[32,256]{1,0:T(8,128)S(1)} %get-tuple-element.87.total_ref), channel_id=1, source_target_pairs={{0,8},{1,9},{2,10},{3,11},{4,12},{5,13},{6,14},{7,15},{8,0},{9,1},... | collective-permute-start | bytes 98312 | tf_op jit(solution)/shard_map/ppermute | solution.py:20
  38.5 6.0 %collective-permute-start.13 = (f32[32,256]{1,0:T(8,128)S(1)}, f32[32,256]{1,0:T(8,128)S(1)}, u32[]{:S(2)}, u32[]{:S(2)}) collective-permute-start(f32[32,256]{1,0:T(8,128)S(1)} %get-tuple-element.96), channel_id=1, source_target_pairs={{1,2},{3,4},{5,6},{7,8},{9,10},{11,12},{13,14},{15,16},{17,18},{19... | collective-permute-start | bytes 98312 | tf_op jit(solution)/shard_map/ppermute | solution.py:26
  41.8 5.7 %collective-permute-start.12 = (f32[32,256]{1,0:T(8,128)S(1)}, f32[32,256]{1,0:T(8,128)S(1)}, u32[]{:S(2)}, u32[]{:S(2)}) collective-permute-start(f32[32,256]{1,0:T(8,128)S(1)} %get-tuple-element.93), channel_id=1, source_target_pairs={{0,16},{1,17},{2,18},{3,19},{4,20},{5,21},{6,22},{7,23},{8,24},{9,... | collective-permute-start | bytes 98312 | tf_op jit(solution)/shard_map/ppermute | solution.py:20
  48.2 1.8 %collective-permute-start.14 = (f32[32,256]{1,0:T(8,128)S(1)}, f32[32,256]{1,0:T(8,128)S(1)}, u32[]{:S(2)}, u32[]{:S(2)}) collective-permute-start(f32[32,256]{1,0:T(8,128)S(1)} %get-tuple-element.108), channel_id=1, source_target_pairs={{0,1},{1,0},{2,3},{3,2},{4,5},{5,4},{6,7},{7,6},{8,9},{9,8},{10,11... | collective-permute-start | bytes 98312 | tf_op jit(solution)/shard_map/ppermute | solution.py:20
  48.4 1.7 %collective-permute-start.15 = (f32[32,256]{1,0:T(8,128)S(1)}, f32[32,256]{1,0:T(8,128)S(1)}, u32[]{:S(2)}, u32[]{:S(2)}) collective-permute-start(f32[32,256]{1,0:T(8,128)S(1)} %get-tuple-element.109), channel_id=1, source_target_pairs={{1,2},{3,4},{5,6},{7,8},{9,10},{11,12},{13,14},{15,16},{17,18},{19... | collective-permute-start | bytes 98312 | tf_op jit(solution)/shard_map/ppermute | solution.py:26
  50.9 4.9 %collective-permute-start.16 = (f32[64,256]{1,0:T(8,128)S(1)}, f32[64,256]{1,0:T(8,128)S(1)}, u32[]{:S(2)}, u32[]{:S(2)}) collective-permute-start(f32[64,256]{1,0:T(8,128)S(1)} %get-tuple-element.110.both_ref), channel_id=1, source_target_pairs={{0,1},{1,0},{2,3},{3,2},{4,5},{5,4},{6,7},{7,6},{8,9},{9,8},{10,11... | collective-permute-start | bytes 196616 | tf_op jit(solution)/shard_map/ppermute | solution.py:20
  56.1 4.9 %collective-permute-start.17 = (f32[32,256]{1,0:T(8,128)S(1)}, f32[32,256]{1,0:T(8,128)S(1)}, u32[]{:S(2)}, u32[]{:S(2)}) collective-permute-start(f32[32,256]{1,0:T(8,128)S(1)} %get-tuple-element.111.total_ref), channel_id=1, source_target_pairs={{0,2},{1,3},{2,0},{3,1},{4,6},{5,7},{6,4},{7,5},{8,10},{9,11},{10,... | collective-permute-start | bytes 98312 | tf_op jit(solution)/shard_map/ppermute | solution.py:20
  58.0 4.8 %collective-permute-start.19 = (f32[32,256]{1,0:T(8,128)S(1)}, f32[32,256]{1,0:T(8,128)S(1)}, u32[]{:S(2)}, u32[]{:S(2)}) collective-permute-start(f32[32,256]{1,0:T(8,128)S(1)} %get-tuple-element.112.carried_ref), channel_id=1, source_target_pairs={{0,6},{1,7},{2,4},{3,5},{4,2},{5,3},{6,0},{7,1},{8,14},{9,15},{10,... | collective-permute-start | bytes 98312 | tf_op jit(solution)/shard_map/ppermute | solution.py:20
  59.9 3.9 %collective-permute-start.18 = (f32[32,256]{1,0:T(8,128)S(1)}, f32[32,256]{1,0:T(8,128)S(1)}, u32[]{:S(2)}, u32[]{:S(2)}) collective-permute-start(f32[32,256]{1,0:T(8,128)S(1)} %get-tuple-element.112.carried_ref), channel_id=1, source_target_pairs={{0,4},{1,5},{2,6},{3,7},{4,0},{5,1},{6,2},{7,3},{8,12},{9,13},{10,... | collective-permute-start | bytes 98312 | tf_op jit(solution)/shard_map/ppermute | solution.py:20
  60.4 8.5 %collective-permute-start.23 = (f32[32,256]{1,0:T(8,128)S(1)}, f32[32,256]{1,0:T(8,128)S(1)}, u32[]{:S(2)}, u32[]{:S(2)}) collective-permute-start(f32[32,256]{1,0:T(8,128)S(1)} %get-tuple-element.117), channel_id=1, source_target_pairs={{1,2},{3,4},{5,6},{7,8},{9,10},{11,12},{13,14},{15,16},{17,18},{19... | collective-permute-start | bytes 98312 | tf_op jit(solution)/shard_map/ppermute | solution.py:26
  64.5 4.3 %collective-permute-start.20 = (f32[32,256]{1,0:T(8,128)S(1)}, f32[32,256]{1,0:T(8,128)S(1)}, u32[]{:S(2)}, u32[]{:S(2)}) collective-permute-start(f32[32,256]{1,0:T(8,128)S(1)} %get-tuple-element.114), channel_id=1, source_target_pairs={{0,8},{1,9},{2,10},{3,11},{4,12},{5,13},{6,14},{7,15},{8,0},{9,1},... | collective-permute-start | bytes 98312 | tf_op jit(solution)/shard_map/ppermute | solution.py:20
  66.6 5.7 %collective-permute-start.22 = (f32[32,256]{1,0:T(8,128)S(1)}, f32[32,256]{1,0:T(8,128)S(1)}, u32[]{:S(2)}, u32[]{:S(2)}) collective-permute-start(f32[32,256]{1,0:T(8,128)S(1)} %get-tuple-element.115), channel_id=1, source_target_pairs={{0,24},{1,25},{2,26},{3,27},{4,28},{5,29},{6,30},{7,31},{8,16},{9,... | collective-permute-start | bytes 98312 | tf_op jit(solution)/shard_map/ppermute | solution.py:20
  68.4 4.8 %collective-permute-start.21 = (f32[32,256]{1,0:T(8,128)S(1)}, f32[32,256]{1,0:T(8,128)S(1)}, u32[]{:S(2)}, u32[]{:S(2)}) collective-permute-start(f32[32,256]{1,0:T(8,128)S(1)} %get-tuple-element.115), channel_id=1, source_target_pairs={{0,16},{1,17},{2,18},{3,19},{4,20},{5,21},{6,22},{7,23},{8,24},{9,... | collective-permute-start | bytes 98312 | tf_op jit(solution)/shard_map/ppermute | solution.py:20
  73.9 1.8 %collective-permute-start.24 = (f32[32,256]{1,0:T(8,128)S(1)}, f32[32,256]{1,0:T(8,128)S(1)}, u32[]{:S(2)}, u32[]{:S(2)}) collective-permute-start(f32[32,256]{1,0:T(8,128)S(1)} %get-tuple-element.126), channel_id=1, source_target_pairs={{0,1},{1,0},{2,3},{3,2},{4,5},{5,4},{6,7},{7,6},{8,9},{9,8},{10,11... | collective-permute-start | bytes 98312 | tf_op jit(solution)/shard_map/ppermute | solution.py:20
  74.0 1.7 %collective-permute-start.25 = (f32[32,256]{1,0:T(8,128)S(1)}, f32[32,256]{1,0:T(8,128)S(1)}, u32[]{:S(2)}, u32[]{:S(2)}) collective-permute-start(f32[32,256]{1,0:T(8,128)S(1)} %get-tuple-element.127), channel_id=1, source_target_pairs={{1,2},{3,4},{5,6},{7,8},{9,10},{11,12},{13,14},{15,16},{17,18},{19... | collective-permute-start | bytes 98312 | tf_op jit(solution)/shard_map/ppermute | solution.py:26
  76.7 14.9 %all-to-all-start = ((f32[32,1,128]{2,1,0:T(1,128)}), f32[32,1,128]{2,1,0:T(1,128)S(1)}, u32[]{:S(2)}, u32[]{:S(2)}) async-start(f32[32,1,128]{2,1,0:T(1,128)} %bitcast.1), calls=%async_computation | async-start | bytes 32768 | tf_op jit(solution)/shard_map/all_to_all | solution.py:504

commit v3 on v2

--- a/solution.py
+++ b/solution.py
@@ -126,12 +126,12 @@
         ref[j, rows, :] = part
 
 
-def first_local_kernel(b_hbm, x_hbm, d_hbm, s_hbm, p_hbm, z_hbm, u_hbm, l_hbm, acc_ref, b_ref, x_ref, d3_ref, s3_ref, p3_ref, z_ref, u_ref, l_ref):
+def first_local_kernel(b_hbm, x_hbm, d_hbm, s_hbm, p_hbm, acc_ref, b_ref, x_ref, d3_ref, s3_ref, p3_ref):
     width = d_hbm.shape[1]
 
     def work(d_ref, s_ref, p_ref, sems):
         copies = gather_copies(
-            [(x_hbm, x_ref), (d_hbm, d_ref), (s_hbm, s_ref), (p_hbm, p_ref), (b_hbm, b_ref), (z_hbm, z_ref), (u_hbm, u_ref), (l_hbm, l_ref)],
+            [(x_hbm, x_ref), (d_hbm, d_ref), (s_hbm, s_ref), (p_hbm, p_ref), (b_hbm, b_ref)],
             sems,
         )
         for copy in copies[:2]:
@@ -141,11 +141,9 @@
                 split_store(target, pl.ds(k * width, width), source[k * width : (k + 1) * width, :])
             copies[copy].wait()
         local_part(b_ref, x_ref, d3_ref, s3_ref, p3_ref, acc_ref)
-        for copy in copies[5:]:
-            copy.wait()
 
     mat = pltpu.VMEM(d_hbm.shape, F32)
-    pl.run_scoped(work, mat, mat, mat, pltpu.SemaphoreType.DMA((8,)))
+    pl.run_scoped(work, mat, mat, mat, pltpu.SemaphoreType.DMA((5,)))
 
 
 def local_part(b_ref, x_ref, d3_ref, s3_ref, p3_ref, acc_ref):
@@ -422,11 +420,9 @@
     )
     near = exchange(near_pack, 1)
     far = across(far_pack)
-    acc, right_sides, solution, d3, s3, p3, local_inverse, upper_spikes, lower_spikes = kernel_call(
-        first_local_kernel,
-        [wide, wide, wide, big, big, big, (local_inverse.shape, BF16), (upper_spikes.shape, BF16), (lower_spikes.shape, BF16)],
-        *((a,) for a in (right_sides, initial, diag_blocks, sub_blocks, super_blocks, local_inverse, upper_spikes, lower_spikes)),
-        micros=3,
+    acc, right_sides, solution, d3, s3, p3 = kernel_call(
+        first_local_kernel, [wide, wide, wide, big, big, big],
+        *((a,) for a in (right_sides, initial, diag_blocks, sub_blocks, super_blocks)), micros=3,
     )
     before, after, mix = kernel_call(mix_kernel, [low_square, low_square, triple], near, far, chain)
 

time: 92.5 us -> 92.6 us (level)
  no operation moved by 1% of the time
where the time goes in v3:
time: 92.6 us; the launch traced here: 92.3 us
  starting transfers between devices  39.4 us (43%)
  waiting for transfers between devices  36.3 us (39%)
  Pallas kernels  15 us (16%)
    ppermute x21, waiting for transfers between devices, exchange(): return lax.ppermute(values, AXIS, [(i, i ^ distance) for i in range(count)])  29.8 us
    ppermute x21, starting transfers between devices, exchange(): return lax.ppermute(values, AXIS, [(i, i ^ distance) for i in range(count)])  28.4 us
    pallas_call x20, Pallas kernels, kernel_call(): pl.pallas_call(kernel, in_specs=specs, out_specs=[pl.BlockSpec(memory_spa...  14.3 us
    all_to_all x1, starting transfers between devices, body(): gathered = lax.all_to_all(mine, AXIS, 0, 0, tiled=True)  7.76 us
    all_to_all x1, waiting for transfers between devices, body(): gathered = lax.all_to_all(mine, AXIS, 0, 0, tiled=True)  6.52 us
    ppermute x5, starting transfers between devices, across(): return lax.ppermute(values, AXIS, pairs + [(b, a) for a, b in pairs])  3.28 us
  transfers between devices with their start and end apart: 27, of which 16 were waited for; matrix products, arithmetic and copies ran while one was open for 1% of the time, Pallas kernels for 10%

profile of v3, /device:TPU:0, one launch (start us, length us, event | category | flops | bytes accessed | tf_op | source)
XLA Modules:
  0.0 92.3 jit_solution(13527749833817695288)
XLA Ops:
  0.6 1.2 %shard_map.96 = (bf16[608,256]{1,0:T(8,128)(2,1)S(1)}, bf16[352,256]{1,0:T(8,128)(2,1)S(1)}, bf16[256,256]{1,0:T(8,128)(2,1)S(1)}) custom-call(f32[32,1024]{1,0:T(8,128)} %x_hbm.3, bf16[256,1024]{1,0:T(8,128)(2,1)} %u_ref.3, bf16[256,1024]{1,0:T(8,128)(2,1)} %l_ref.3), custom_call_target="tpu_custom_call" | custom-call | flops 30000000 | bytes 622592 | tf_op jit(solution)/shard_map/pallas_call | solution.py:34
  1.8 0.6 collective-permute-start
  2.4 2.6 %collective-permute-start.4 = (bf16[256,256]{1,0:T(8,128)(2,1)S(1)}, bf16[256,256]{1,0:T(8,128)(2,1)S(1)}, u32[]{:S(2)}, u32[]{:S(2)}) collective-permute-start(bf16[256,256]{1,0:T(8,128)(2,1)S(1)} %get-tuple-element.68.chain_ref.own_ref.refs_11_.refs_14_), channel_id=1, source_target_pairs={{0,2},{1,3},{2,0},{3,1},{4,6},{5,7},{6,4},{7,5},{8,10},{9,11},{10,... | collective-permute-start | bytes 393224 | tf_op jit(solution)/shard_map/ppermute | solution.py:20
  4.9 4.1 %collective-permute-done.4.got_ref = bf16[256,256]{1,0:T(8,128)(2,1)S(1)} collective-permute-done((bf16[256,256]{1,0:T(8,128)(2,1)S(1)}, bf16[256,256]{1,0:T(8,128)(2,1)S(1)}, u32[]{:S(2)}, u32[]{:S(2)}) %collective-permute-start.4) | collective-permute-done | bytes 131104 | tf_op jit(solution)/shard_map/ppermute | solution.py:20
  9.0 0.3 shard_map.99
  9.3 1.1 %collective-permute-done.5.twin_ref = bf16[256,256]{1,0:T(8,128)(2,1)S(1)} collective-permute-done((bf16[256,256]{1,0:T(8,128)(2,1)S(1)}, bf16[256,256]{1,0:T(8,128)(2,1)S(1)}, u32[]{:S(2)}, u32[]{:S(2)}) %collective-permute-start.5) | collective-permute-done | bytes 131104 | tf_op jit(solution)/shard_map/ppermute | solution.py:20
  10.4 0.8 shard_map.101
  11.2 1.8 %collective-permute-start.7 = (f32[128,256]{1,0:T(8,128)S(1)}, f32[128,256]{1,0:T(8,128)S(1)}, u32[]{:S(2)}, u32[]{:S(2)}) collective-permute-start(f32[128,256]{1,0:T(8,128)S(1)} %get-tuple-element.81), channel_id=1, source_target_pairs={{0,4},{1,5},{2,6},{3,7},{4,0},{5,1},{6,2},{7,3},{8,12},{9,13},{10,... | collective-permute-start | bytes 393224 | tf_op jit(solution)/shard_map/ppermute | solution.py:20
  13.0 3.8 %collective-permute-done.7.got_ref = f32[128,256]{1,0:T(8,128)S(1)} collective-permute-done((f32[128,256]{1,0:T(8,128)S(1)}, f32[128,256]{1,0:T(8,128)S(1)}, u32[]{:S(2)}, u32[]{:S(2)}) %collective-permute-start.7) | collective-permute-done | bytes 131104 | tf_op jit(solution)/shard_map/ppermute | solution.py:20
  16.8 0.7 collective-permute-start.1
  17.5 0.7 collective-permute-done.8.twin_ref
  18.2 0.6 shard_map.103
  18.8 4.9 %collective-permute-start.10 = (f32[128,256]{1,0:T(8,128)S(1)}, f32[128,256]{1,0:T(8,128)S(1)}, u32[]{:S(2)}, u32[]{:S(2)}) collective-permute-start(f32[128,256]{1,0:T(8,128)S(1)} %get-tuple-element.87), channel_id=1, source_target_pairs={{0,8},{1,9},{2,10},{3,11},{4,12},{5,13},{6,14},{7,15},{8,0},{9,1},... | collective-permute-start | bytes 393224 | tf_op jit(solution)/shard_map/ppermute | solution.py:20
  23.7 2.9 %shard_map.95 = (f32[32,1024]{1,0:T(8,128)S(1)}, f32[32,1024]{1,0:T(8,128)S(1)}, f32[32,1024]{1,0:T(8,128)S(1)}, bf16[3,1024,256]{2,1,0:T(8,128)(2,1)S(1)}, bf16...) custom-call(f32[32,1024]{1,0:T(8,128)} %b_hbm.1, f32[32,1024]{1,0:T(8,128)} %x_hbm.3, f32[1024,256]{1,0:T(8,128)} %d_hbm.1, ...), custom_call_target="tpu_custom_call" | custom-call | flops 300000000 | bytes 5111808 | tf_op jit(solution)/shard_map/pallas_call | solution.py:34
  26.7 0.0 collective-permute-done.1.far_ref
  26.7 0.2 shard_map.97
  26.9 0.8 shard_map.98
  27.7 0.1 collective-permute-start.2
  27.8 0.8 collective-permute-done.10.got_ref
  28.6 0.4 collective-permute-done.2.got_ref.refs_3_
  29.0 0.1 shard_map.100
  29.2 1.0 %collective-permute-start.3 = (f32[32,256]{1,0:T(8,128)S(1)}, f32[32,256]{1,0:T(8,128)S(1)}, u32[]{:S(2)}, u32[]{:S(2)}) collective-permute-start(f32[32,256]{1,0:T(8,128)S(1)} %get-tuple-element.72.total_ref), channel_id=1, source_target_pairs={{0,2},{1,3},{2,0},{3,1},{4,6},{5,7},{6,4},{7,5},{8,10},{9,11},{10,... | collective-permute-start | bytes 98312 | tf_op jit(solution)/shard_map/ppermute | solution.py:20
  30.2 2.9 %collective-permute-done.3.got_ref = f32[32,256]{1,0:T(8,128)S(1)} collective-permute-done((f32[32,256]{1,0:T(8,128)S(1)}, f32[32,256]{1,0:T(8,128)S(1)}, u32[]{:S(2)}, u32[]{:S(2)}) %collective-permute-start.3) | collective-permute-done | bytes 32800 | tf_op jit(solution)/shard_map/ppermute | solution.py:20
  33.1 0.2 shard_map.102
  33.4 1.1 %collective-permute-start.6 = (f32[32,256]{1,0:T(8,128)S(1)}, f32[32,256]{1,0:T(8,128)S(1)}, u32[]{:S(2)}, u32[]{:S(2)}) collective-permute-start(f32[32,256]{1,0:T(8,128)S(1)} %get-tuple-element.77.total_ref), channel_id=1, source_target_pairs={{0,4},{1,5},{2,6},{3,7},{4,0},{5,1},{6,2},{7,3},{8,12},{9,13},{10,... | collective-permute-start | bytes 98312 | tf_op jit(solution)/shard_map/ppermute | solution.py:20
  34.5 2.9 %collective-permute-done.6.got_ref = f32[32,256]{1,0:T(8,128)S(1)} collective-permute-done((f32[32,256]{1,0:T(8,128)S(1)}, f32[32,256]{1,0:T(8,128)S(1)}, u32[]{:S(2)}, u32[]{:S(2)}) %collective-permute-start.6) | collective-permute-done | bytes 32800 | tf_op jit(solution)/shard_map/ppermute | solution.py:20
  37.4 0.2 shard_map.104
  37.6 0.9 collective-permute-start.9
  38.5 0.7 collective-permute-start.13
  39.2 0.4 shard_map.105
  39.6 2.0 %collective-permute-done.9.got_ref = f32[32,256]{1,0:T(8,128)S(1)} collective-permute-done((f32[32,256]{1,0:T(8,128)S(1)}, f32[32,256]{1,0:T(8,128)S(1)}, u32[]{:S(2)}, u32[]{:S(2)}) %collective-permute-start.9) | collective-permute-done | bytes 32800 | tf_op jit(solution)/shard_map/ppermute | solution.py:20
  41.6 0.2 shard_map.106
  41.8 2.6 %collective-permute-start.12 = (f32[32,256]{1,0:T(8,128)S(1)}, f32[32,256]{1,0:T(8,128)S(1)}, u32[]{:S(2)}, u32[]{:S(2)}) collective-permute-start(f32[32,256]{1,0:T(8,128)S(1)} %get-tuple-element.89), channel_id=1, source_target_pairs={{0,16},{1,17},{2,18},{3,19},{4,20},{5,21},{6,22},{7,23},{8,24},{9,... | collective-permute-start | bytes 98312 | tf_op jit(solution)/shard_map/ppermute | solution.py:20
  44.5 3.1 %collective-permute-done.12.refs_0_ = f32[32,256]{1,0:T(8,128)S(1)} collective-permute-done((f32[32,256]{1,0:T(8,128)S(1)}, f32[32,256]{1,0:T(8,128)S(1)}, u32[]{:S(2)}, u32[]{:S(2)}) %collective-permute-start.12) | collective-permute-done | bytes 32800 | tf_op jit(solution)/shard_map/ppermute | solution.py:20
  47.6 0.7 shard_map.107
  48.3 0.2 collective-permute-start.14
  48.5 0.7 collective-permute-start.15
  49.1 1.0 %shard_map.108 = (f32[32,1024]{1,0:T(8,128)S(1)}, f32[32,1024]{1,0:T(8,128)S(1)}) custom-call(bf16[32,256]{1,0:T(8,128)(2,1)S(1)} %get-tuple-element.97.top_ref, bf16[32,256]{1,0:T(8,128)(2,1)S(1)} %get-tuple-element.98.previous_ref, f32[32,1024]{1,0:T(8,128)S(1)} %get-tuple-element.93.refs_5_.local_ref, f32[32,1024]{1,0:T(8,128)S(1)} %get-tuple-element.94.refs_6_.x_ref, ...), custom_call_target="tpu_custom_call" | custom-call | flops 100000000 | bytes 262144 | tf_op jit(solution)/shard_map/pallas_call | solution.py:34
  50.1 0.0 collective-permute-done.14.near_ref
  50.1 0.8 shard_map.109
  50.9 4.0 %collective-permute-start.16 = (f32[64,256]{1,0:T(8,128)S(1)}, f32[64,256]{1,0:T(8,128)S(1)}, u32[]{:S(2)}, u32[]{:S(2)}) collective-permute-start(f32[64,256]{1,0:T(8,128)S(1)} %get-tuple-element.104.both_ref), channel_id=1, source_target_pairs={{0,1},{1,0},{2,3},{3,2},{4,5},{5,4},{6,7},{7,6},{8,9},{9,8},{10,11... | collective-permute-start | bytes 196616 | tf_op jit(solution)/shard_map/ppermute | solution.py:20
  54.9 0.9 collective-permute-done.16.got_ref.refs_6_
  55.8 0.3 shard_map.110
  56.1 1.9 %collective-permute-start.17 = (f32[32,256]{1,0:T(8,128)S(1)}, f32[32,256]{1,0:T(8,128)S(1)}, u32[]{:S(2)}, u32[]{:S(2)}) collective-permute-start(f32[32,256]{1,0:T(8,128)S(1)} %get-tuple-element.105.total_ref), channel_id=1, source_target_pairs={{0,2},{1,3},{2,0},{3,1},{4,6},{5,7},{6,4},{7,5},{8,10},{9,11},{10,... | collective-permute-start | bytes 98312 | tf_op jit(solution)/shard_map/ppermute | solution.py:20
  58.0 1.9 %collective-permute-start.19 = (f32[32,256]{1,0:T(8,128)S(1)}, f32[32,256]{1,0:T(8,128)S(1)}, u32[]{:S(2)}, u32[]{:S(2)}) collective-permute-start(f32[32,256]{1,0:T(8,128)S(1)} %get-tuple-element.106.carried_ref), channel_id=1, source_target_pairs={{0,6},{1,7},{2,4},{3,5},{4,2},{5,3},{6,0},{7,1},{8,14},{9,15},{10,... | collective-permute-start | bytes 98312 | tf_op jit(solution)/shard_map/ppermute | solution.py:20
  59.9 0.5 collective-permute-start.18
  60.4 0.7 collective-permute-start.23
  61.1 1.8 %collective-permute-done.19.cross_ref = f32[32,256]{1,0:T(8,128)S(1)} collective-permute-done((f32[32,256]{1,0:T(8,128)S(1)}, f32[32,256]{1,0:T(8,128)S(1)}, u32[]{:S(2)}, u32[]{:S(2)}) %collective-permute-start.19) | collective-permute-done | bytes 32800 | tf_op jit(solution)/shard_map/ppermute | solution.py:20
  62.9 1.0 %collective-permute-done.18.low_ref = f32[32,256]{1,0:T(8,128)S(1)} collective-permute-done((f32[32,256]{1,0:T(8,128)S(1)}, f32[32,256]{1,0:T(8,128)S(1)}, u32[]{:S(2)}, u32[]{:S(2)}) %collective-permute-start.18) | collective-permute-done | bytes 32800 | tf_op jit(solution)/shard_map/ppermute | solution.py:20
  63.9 0.7 shard_map.111
  64.6 2.1 %collective-permute-start.20 = (f32[32,256]{1,0:T(8,128)S(1)}, f32[32,256]{1,0:T(8,128)S(1)}, u32[]{:S(2)}, u32[]{:S(2)}) collective-permute-start(f32[32,256]{1,0:T(8,128)S(1)} %get-tuple-element.108), channel_id=1, source_target_pairs={{0,8},{1,9},{2,10},{3,11},{4,12},{5,13},{6,14},{7,15},{8,0},{9,1},... | collective-permute-start | bytes 98312 | tf_op jit(solution)/shard_map/ppermute | solution.py:20
  66.7 1.8 %collective-permute-start.22 = (f32[32,256]{1,0:T(8,128)S(1)}, f32[32,256]{1,0:T(8,128)S(1)}, u32[]{:S(2)}, u32[]{:S(2)}) collective-permute-start(f32[32,256]{1,0:T(8,128)S(1)} %get-tuple-element.109), channel_id=1, source_target_pairs={{0,24},{1,25},{2,26},{3,27},{4,28},{5,29},{6,30},{7,31},{8,16},{9,... | collective-permute-start | bytes 98312 | tf_op jit(solution)/shard_map/ppermute | solution.py:20
  68.4 0.5 collective-permute-start.21
  68.9 3.5 %collective-permute-done.22.refs_2_ = f32[32,256]{1,0:T(8,128)S(1)} collective-permute-done((f32[32,256]{1,0:T(8,128)S(1)}, f32[32,256]{1,0:T(8,128)S(1)}, u32[]{:S(2)}, u32[]{:S(2)}) %collective-permute-start.22) | collective-permute-done | bytes 32800 | tf_op jit(solution)/shard_map/ppermute | solution.py:20
  72.4 0.9 collective-permute-done.21.refs_1_
  73.2 0.7 shard_map.112
  74.0 0.1 collective-permute-start.24
  74.1 0.7 collective-permute-start.25
  74.7 1.0 %shard_map.113 = (f32[32,1024]{1,0:T(8,128)S(1)}, f32[32,1024]{1,0:T(8,128)S(1)}, f32[32,128]{1,0:T(8,128)S(1)}, f32[1,128]{1,0:T(1,128)S(1)}) custom-call(bf16[32,256]{1,0:T(8,128)(2,1)S(1)} %get-tuple-element.114.top_ref, bf16[32,256]{1,0:T(8,128)(2,1)S(1)} %get-tuple-element.115.previous_ref, f32[32,1024]{1,0:T(8,128)S(1)} %get-tuple-element.112.refs_8_.local_ref, ...), custom_call_target="tpu_custom_call" | custom-call | flops 100000000 | bytes 279040 | tf_op jit(solution)/shard_map/pallas_call | solution.py:34
  75.8 1.0 %shard_map.114 = f32[32,128]{1,0:T(8,128)} custom-call(f32[32,1024]{1,0:T(8,128)S(1)} %get-tuple-element.119.acc_ref, f32[32,256]{1,0:T(8,128)S(1)} %collective-permute-done.24.near_ref, f32[32,256]{1,0:T(8,128)S(1)} %collective-permute-done.25.far_ref, bf16[3,1024,256]{2,1,0:T(8,128)(2,1)S(1)} %get-tuple-element.66.s3_ref, ...), custom_call_target="tpu_custom_call" | custom-call | flops 30000000 | bytes 16384 | tf_op jit(solution)/shard_map/pallas_call | solution.py:34
  76.7 7.8 %all-to-all-start = ((f32[32,1,128]{2,1,0:T(1,128)}), f32[32,1,128]{2,1,0:T(1,128)S(1)}, u32[]{:S(2)}, u32[]{:S(2)}) async-start(f32[32,1,128]{2,1,0:T(1,128)} %bitcast.1), calls=%async_computation | async-start | bytes 32768 | tf_op jit(solution)/shard_map/all_to_all | solution.py:500
  84.5 0.7 copy.11
  85.1 6.5 %all-to-all-done = f32[32,1,128]{2,1,0:T(1,128)S(1)} async-done(((f32[32,1,128]{2,1,0:T(1,128)}), f32[32,1,128]{2,1,0:T(1,128)S(1)}, u32[]{:S(2)}, u32[]{:S(2)}) %all-to-all-start) | async-done | bytes 16416 | tf_op jit(solution)/shard_map/all_to_all | solution.py:500
  91.7 0.7 shard_map.115
  (18 shorter events, 0.1 us)
Async XLA Ops:
  1.8 7.2 %collective-permute-start = (bf16[608,256]{1,0:T(8,128)(2,1)S(1)}, bf16[608,256]{1,0:T(8,128)(2,1)S(1)}, u32[]{:S(2)}, u32[]{:S(2)}) collective-permute-start(bf16[608,256]{1,0:T(8,128)(2,1)S(1)} %get-tuple-element.64), channel_id=1, source_target_pairs={{0,1},{1,0},{2,3},{3,2},{4,5},{5,4},{6,7},{7,6},{8,9},{9,8},{10,11... | collective-permute-start | bytes 933896 | tf_op jit(solution)/shard_map/ppermute | solution.py:20
  2.4 6.6 %collective-permute-start.4 = (bf16[256,256]{1,0:T(8,128)(2,1)S(1)}, bf16[256,256]{1,0:T(8,128)(2,1)S(1)}, u32[]{:S(2)}, u32[]{:S(2)}) collective-permute-start(bf16[256,256]{1,0:T(8,128)(2,1)S(1)} %get-tuple-element.68.chain_ref.own_ref.refs_11_.refs_14_), channel_id=1, source_target_pairs={{0,2},{1,3},{2,0},{3,1},{4,6},{5,7},{6,4},{7,5},{8,10},{9,11},{10,... | collective-permute-start | bytes 393224 | tf_op jit(solution)/shard_map/ppermute | solution.py:20
  9.0 1.3 %collective-permute-start.5 = (bf16[256,256]{1,0:T(8,128)(2,1)S(1)}, bf16[256,256]{1,0:T(8,128)(2,1)S(1)}, u32[]{:S(2)}, u32[]{:S(2)}) collective-permute-start(bf16[256,256]{1,0:T(8,128)(2,1)S(1)} %collective-permute-done.4.got_ref), channel_id=1, source_target_pairs={{0,1},{1,0},{2,3},{3,2},{4,5},{5,4},{6,7},{7,6},{8,9},{9,8},{10,11... | collective-permute-start | bytes 393224 | tf_op jit(solution)/shard_map/ppermute | solution.py:20
  11.2 5.6 %collective-permute-start.7 = (f32[128,256]{1,0:T(8,128)S(1)}, f32[128,256]{1,0:T(8,128)S(1)}, u32[]{:S(2)}, u32[]{:S(2)}) collective-permute-start(f32[128,256]{1,0:T(8,128)S(1)} %get-tuple-element.81), channel_id=1, source_target_pairs={{0,4},{1,5},{2,6},{3,7},{4,0},{5,1},{6,2},{7,3},{8,12},{9,13},{10,... | collective-permute-start | bytes 393224 | tf_op jit(solution)/shard_map/ppermute | solution.py:20
  16.8 1.3 %collective-permute-start.8 = (f32[128,256]{1,0:T(8,128)S(1)}, f32[128,256]{1,0:T(8,128)S(1)}, u32[]{:S(2)}, u32[]{:S(2)}) collective-permute-start(f32[128,256]{1,0:T(8,128)S(1)} %collective-permute-done.7.got_ref), channel_id=1, source_target_pairs={{0,1},{1,0},{2,3},{3,2},{4,5},{5,4},{6,7},{7,6},{8,9},{9,8},{10,11... | collective-permute-start | bytes 393224 | tf_op jit(solution)/shard_map/ppermute | solution.py:20
  16.8 9.9 %collective-permute-start.1 = (bf16[352,256]{1,0:T(8,128)(2,1)S(1)}, bf16[352,256]{1,0:T(8,128)(2,1)S(1)}, u32[]{:S(2)}, u32[]{:S(2)}) collective-permute-start(bf16[352,256]{1,0:T(8,128)(2,1)S(1)} %get-tuple-element.65), channel_id=1, source_target_pairs={{1,2},{3,4},{5,6},{7,8},{9,10},{11,12},{13,14},{15,16},{17,18},{19... | collective-permute-start | bytes 540680 | tf_op jit(solution)/shard_map/ppermute | solution.py:26
  18.8 8.1 %copy-start.2 = (bf16[1024,1024]{1,0:T(8,128)(2,1)S(1)}, bf16[1024,1024]{1,0:T(8,128)(2,1)}, u32[]{:S(2)}) copy-start(bf16[1024,1024]{1,0:T(8,128)(2,1)} %z_ref.3) | copy-start | bytes 6291460
  18.8 9.8 %collective-permute-start.10 = (f32[128,256]{1,0:T(8,128)S(1)}, f32[128,256]{1,0:T(8,128)S(1)}, u32[]{:S(2)}, u32[]{:S(2)}) collective-permute-start(f32[128,256]{1,0:T(8,128)S(1)} %get-tuple-element.87), channel_id=1, source_target_pairs={{0,8},{1,9},{2,10},{3,11},{4,12},{5,13},{6,14},{7,15},{8,0},{9,1},... | collective-permute-start | bytes 393224 | tf_op jit(solution)/shard_map/ppermute | solution.py:20
  27.7 1.3 %collective-permute-start.2 = (f32[64,256]{1,0:T(8,128)S(1)}, f32[64,256]{1,0:T(8,128)S(1)}, u32[]{:S(2)}, u32[]{:S(2)}) collective-permute-start(f32[64,256]{1,0:T(8,128)S(1)} %get-tuple-element.70.both_ref), channel_id=1, source_target_pairs={{0,1},{1,0},{2,3},{3,2},{4,5},{5,4},{6,7},{7,6},{8,9},{9,8},{10,11... | collective-permute-start | bytes 196616 | tf_op jit(solution)/shard_map/ppermute | solution.py:20
  28.6 10.6 %collective-permute-start.11 = (f32[128,256]{1,0:T(8,128)S(1)}, f32[128,256]{1,0:T(8,128)S(1)}, u32[]{:S(2)}, u32[]{:S(2)}) collective-permute-start(f32[128,256]{1,0:T(8,128)S(1)} %collective-permute-done.10.got_ref), channel_id=1, source_target_pairs={{0,1},{1,0},{2,3},{3,2},{4,5},{5,4},{6,7},{7,6},{8,9},{9,8},{10,11... | collective-permute-start | bytes 393224 | tf_op jit(solution)/shard_map/ppermute | solution.py:20
  29.2 3.9 %collective-permute-start.3 = (f32[32,256]{1,0:T(8,128)S(1)}, f32[32,256]{1,0:T(8,128)S(1)}, u32[]{:S(2)}, u32[]{:S(2)}) collective-permute-start(f32[32,256]{1,0:T(8,128)S(1)} %get-tuple-element.72.total_ref), channel_id=1, source_target_pairs={{0,2},{1,3},{2,0},{3,1},{4,6},{5,7},{6,4},{7,5},{8,10},{9,11},{10,... | collective-permute-start | bytes 98312 | tf_op jit(solution)/shard_map/ppermute | solution.py:20
  33.4 14.2 %copy-start = (bf16[256,1024]{1,0:T(8,128)(2,1)S(1)}, bf16[256,1024]{1,0:T(8,128)(2,1)}, u32[]{:S(2)}) copy-start(bf16[256,1024]{1,0:T(8,128)(2,1)} %u_ref.3) | copy-start | bytes 1572868
  33.4 14.2 %copy-start.1 = (bf16[256,1024]{1,0:T(8,128)(2,1)S(1)}, bf16[256,1024]{1,0:T(8,128)(2,1)}, u32[]{:S(2)}) copy-start(bf16[256,1024]{1,0:T(8,128)(2,1)} %l_ref.3) | copy-start | bytes 1572868
  33.4 4.0 %collective-permute-start.6 = (f32[32,256]{1,0:T(8,128)S(1)}, f32[32,256]{1,0:T(8,128)S(1)}, u32[]{:S(2)}, u32[]{:S(2)}) collective-permute-start(f32[32,256]{1,0:T(8,128)S(1)} %get-tuple-element.77.total_ref), channel_id=1, source_target_pairs={{0,4},{1,5},{2,6},{3,7},{4,0},{5,1},{6,2},{7,3},{8,12},{9,13},{10,... | collective-permute-start | bytes 98312 | tf_op jit(solution)/shard_map/ppermute | solution.py:20
  37.6 4.0 %collective-permute-start.9 = (f32[32,256]{1,0:T(8,128)S(1)}, f32[32,256]{1,0:T(8,128)S(1)}, u32[]{:S(2)}, u32[]{:S(2)}) collective-permute-start(f32[32,256]{1,0:T(8,128)S(1)} %get-tuple-element.83.total_ref), channel_id=1, source_target_pairs={{0,8},{1,9},{2,10},{3,11},{4,12},{5,13},{6,14},{7,15},{8,0},{9,1},... | collective-permute-start | bytes 98312 | tf_op jit(solution)/shard_map/ppermute | solution.py:20
  38.5 6.0 %collective-permute-start.13 = (f32[32,256]{1,0:T(8,128)S(1)}, f32[32,256]{1,0:T(8,128)S(1)}, u32[]{:S(2)}, u32[]{:S(2)}) collective-permute-start(f32[32,256]{1,0:T(8,128)S(1)} %get-tuple-element.92), channel_id=1, source_target_pairs={{1,2},{3,4},{5,6},{7,8},{9,10},{11,12},{13,14},{15,16},{17,18},{19... | collective-permute-start | bytes 98312 | tf_op jit(solution)/shard_map/ppermute | solution.py:26
  41.8 5.7 %collective-permute-start.12 = (f32[32,256]{1,0:T(8,128)S(1)}, f32[32,256]{1,0:T(8,128)S(1)}, u32[]{:S(2)}, u32[]{:S(2)}) collective-permute-start(f32[32,256]{1,0:T(8,128)S(1)} %get-tuple-element.89), channel_id=1, source_target_pairs={{0,16},{1,17},{2,18},{3,19},{4,20},{5,21},{6,22},{7,23},{8,24},{9,... | collective-permute-start | bytes 98312 | tf_op jit(solution)/shard_map/ppermute | solution.py:20
  48.3 1.8 %collective-permute-start.14 = (f32[32,256]{1,0:T(8,128)S(1)}, f32[32,256]{1,0:T(8,128)S(1)}, u32[]{:S(2)}, u32[]{:S(2)}) collective-permute-start(f32[32,256]{1,0:T(8,128)S(1)} %get-tuple-element.102), channel_id=1, source_target_pairs={{0,1},{1,0},{2,3},{3,2},{4,5},{5,4},{6,7},{7,6},{8,9},{9,8},{10,11... | collective-permute-start | bytes 98312 | tf_op jit(solution)/shard_map/ppermute | solution.py:20
  48.5 1.7 %collective-permute-start.15 = (f32[32,256]{1,0:T(8,128)S(1)}, f32[32,256]{1,0:T(8,128)S(1)}, u32[]{:S(2)}, u32[]{:S(2)}) collective-permute-start(f32[32,256]{1,0:T(8,128)S(1)} %get-tuple-element.103), channel_id=1, source_target_pairs={{1,2},{3,4},{5,6},{7,8},{9,10},{11,12},{13,14},{15,16},{17,18},{19... | collective-permute-start | bytes 98312 | tf_op jit(solution)/shard_map/ppermute | solution.py:26
  50.9 4.9 %collective-permute-start.16 = (f32[64,256]{1,0:T(8,128)S(1)}, f32[64,256]{1,0:T(8,128)S(1)}, u32[]{:S(2)}, u32[]{:S(2)}) collective-permute-start(f32[64,256]{1,0:T(8,128)S(1)} %get-tuple-element.104.both_ref), channel_id=1, source_target_pairs={{0,1},{1,0},{2,3},{3,2},{4,5},{5,4},{6,7},{7,6},{8,9},{9,8},{10,11... | collective-permute-start | bytes 196616 | tf_op jit(solution)/shard_map/ppermute | solution.py:20
  56.1 4.9 %collective-permute-start.17 = (f32[32,256]{1,0:T(8,128)S(1)}, f32[32,256]{1,0:T(8,128)S(1)}, u32[]{:S(2)}, u32[]{:S(2)}) collective-permute-start(f32[32,256]{1,0:T(8,128)S(1)} %get-tuple-element.105.total_ref), channel_id=1, source_target_pairs={{0,2},{1,3},{2,0},{3,1},{4,6},{5,7},{6,4},{7,5},{8,10},{9,11},{10,... | collective-permute-start | bytes 98312 | tf_op jit(solution)/shard_map/ppermute | solution.py:20
  58.0 4.8 %collective-permute-start.19 = (f32[32,256]{1,0:T(8,128)S(1)}, f32[32,256]{1,0:T(8,128)S(1)}, u32[]{:S(2)}, u32[]{:S(2)}) collective-permute-start(f32[32,256]{1,0:T(8,128)S(1)} %get-tuple-element.106.carried_ref), channel_id=1, source_target_pairs={{0,6},{1,7},{2,4},{3,5},{4,2},{5,3},{6,0},{7,1},{8,14},{9,15},{10,... | collective-permute-start | bytes 98312 | tf_op jit(solution)/shard_map/ppermute | solution.py:20
  59.9 3.9 %collective-permute-start.18 = (f32[32,256]{1,0:T(8,128)S(1)}, f32[32,256]{1,0:T(8,128)S(1)}, u32[]{:S(2)}, u32[]{:S(2)}) collective-permute-start(f32[32,256]{1,0:T(8,128)S(1)} %get-tuple-element.106.carried_ref), channel_id=1, source_target_pairs={{0,4},{1,5},{2,6},{3,7},{4,0},{5,1},{6,2},{7,3},{8,12},{9,13},{10,... | collective-permute-start | bytes 98312 | tf_op jit(solution)/shard_map/ppermute | solution.py:20
  60.4 8.5 %collective-permute-start.23 = (f32[32,256]{1,0:T(8,128)S(1)}, f32[32,256]{1,0:T(8,128)S(1)}, u32[]{:S(2)}, u32[]{:S(2)}) collective-permute-start(f32[32,256]{1,0:T(8,128)S(1)} %get-tuple-element.111), channel_id=1, source_target_pairs={{1,2},{3,4},{5,6},{7,8},{9,10},{11,12},{13,14},{15,16},{17,18},{19... | collective-permute-start | bytes 98312 | tf_op jit(solution)/shard_map/ppermute | solution.py:26
  64.6 4.3 %collective-permute-start.20 = (f32[32,256]{1,0:T(8,128)S(1)}, f32[32,256]{1,0:T(8,128)S(1)}, u32[]{:S(2)}, u32[]{:S(2)}) collective-permute-start(f32[32,256]{1,0:T(8,128)S(1)} %get-tuple-element.108), channel_id=1, source_target_pairs={{0,8},{1,9},{2,10},{3,11},{4,12},{5,13},{6,14},{7,15},{8,0},{9,1},... | collective-permute-start | bytes 98312 | tf_op jit(solution)/shard_map/ppermute | solution.py:20
  66.7 5.7 %collective-permute-start.22 = (f32[32,256]{1,0:T(8,128)S(1)}, f32[32,256]{1,0:T(8,128)S(1)}, u32[]{:S(2)}, u32[]{:S(2)}) collective-permute-start(f32[32,256]{1,0:T(8,128)S(1)} %get-tuple-element.109), channel_id=1, source_target_pairs={{0,24},{1,25},{2,26},{3,27},{4,28},{5,29},{6,30},{7,31},{8,16},{9,... | collective-permute-start | bytes 98312 | tf_op jit(solution)/shard_map/ppermute | solution.py:20
  68.4 4.8 %collective-permute-start.21 = (f32[32,256]{1,0:T(8,128)S(1)}, f32[32,256]{1,0:T(8,128)S(1)}, u32[]{:S(2)}, u32[]{:S(2)}) collective-permute-start(f32[32,256]{1,0:T(8,128)S(1)} %get-tuple-element.109), channel_id=1, source_target_pairs={{0,16},{1,17},{2,18},{3,19},{4,20},{5,21},{6,22},{7,23},{8,24},{9,... | collective-permute-start | bytes 98312 | tf_op jit(solution)/shard_map/ppermute | solution.py:20
  74.0 1.8 %collective-permute-start.24 = (f32[32,256]{1,0:T(8,128)S(1)}, f32[32,256]{1,0:T(8,128)S(1)}, u32[]{:S(2)}, u32[]{:S(2)}) collective-permute-start(f32[32,256]{1,0:T(8,128)S(1)} %get-tuple-element.120), channel_id=1, source_target_pairs={{0,1},{1,0},{2,3},{3,2},{4,5},{5,4},{6,7},{7,6},{8,9},{9,8},{10,11... | collective-permute-start | bytes 98312 | tf_op jit(solution)/shard_map/ppermute | solution.py:20
  74.1 1.7 %collective-permute-start.25 = (f32[32,256]{1,0:T(8,128)S(1)}, f32[32,256]{1,0:T(8,128)S(1)}, u32[]{:S(2)}, u32[]{:S(2)}) collective-permute-start(f32[32,256]{1,0:T(8,128)S(1)} %get-tuple-element.121), channel_id=1, source_target_pairs={{1,2},{3,4},{5,6},{7,8},{9,10},{11,12},{13,14},{15,16},{17,18},{19... | collective-permute-start | bytes 98312 | tf_op jit(solution)/shard_map/ppermute | solution.py:26
  76.7 14.9 %all-to-all-start = ((f32[32,1,128]{2,1,0:T(1,128)}), f32[32,1,128]{2,1,0:T(1,128)S(1)}, u32[]{:S(2)}, u32[]{:S(2)}) async-start(f32[32,1,128]{2,1,0:T(1,128)} %bitcast.1), calls=%async_computation | async-start | bytes 32768 | tf_op jit(solution)/shard_map/all_to_all | solution.py:500

commit v4 on v2

--- a/solution.py
+++ b/solution.py
@@ -126,40 +126,52 @@
         ref[j, rows, :] = part
 
 
-def first_local_kernel(b_hbm, x_hbm, d_hbm, s_hbm, p_hbm, z_hbm, u_hbm, l_hbm, acc_ref, b_ref, x_ref, d3_ref, s3_ref, p3_ref, z_ref, u_ref, l_ref):
+def first_local_kernel(
+    b_hbm, x_hbm, d_hbm, s_hbm, p_hbm, z_hbm, u_hbm, l_hbm, acc_ref, b_ref, x_ref, d3_ref, s3_ref, p3_ref, z_ref, u_ref, l_ref
+):
     width = d_hbm.shape[1]
+    blocks = d_hbm.shape[0] // width
 
     def work(d_ref, s_ref, p_ref, sems):
-        copies = gather_copies(
-            [(x_hbm, x_ref), (d_hbm, d_ref), (s_hbm, s_ref), (p_hbm, p_ref), (b_hbm, b_ref), (z_hbm, z_ref), (u_hbm, u_ref), (l_hbm, l_ref)],
-            sems,
-        )
-        for copy in copies[:2]:
+        pairs = [(x_hbm, x_ref), (b_hbm, b_ref)]
+        for k in range(blocks):
+            rows = pl.ds(k * width, width)
+            pairs += [(a.at[rows, :], v.at[rows, :]) for a, v in ((d_hbm, d_ref), (s_hbm, s_ref), (p_hbm, p_ref))]
+        pairs += [(z_hbm, z_ref), (u_hbm, u_ref), (l_hbm, l_ref)]
+        copies = gather_copies(pairs, sems)
+        copies[0].wait()
+        copies[1].wait()
+        for k in range(blocks):
+            for j, (source, target) in enumerate(((d_ref, d3_ref), (s_ref, s3_ref), (p_ref, p3_ref))):
+                copies[2 + 3 * k + j].wait()
+                split_store(target, pl.ds(k * width, width), source[k * width : (k + 1) * width, :])
+            local_block(k, b_ref, x_ref, d3_ref, s3_ref, p3_ref, acc_ref)
+        for copy in copies[-3:]:
             copy.wait()
-        for source, target, copy in ((d_ref, d3_ref, 2), (s_ref, s3_ref, 3), (p_ref, p3_ref, 4)):
-            for k in range(d_ref.shape[0] // width):
-                split_store(target, pl.ds(k * width, width), source[k * width : (k + 1) * width, :])
-            copies[copy].wait()
-        local_part(b_ref, x_ref, d3_ref, s3_ref, p3_ref, acc_ref)
-        for copy in copies[5:]:
-            copy.wait()
 
     mat = pltpu.VMEM(d_hbm.shape, F32)
-    pl.run_scoped(work, mat, mat, mat, pltpu.SemaphoreType.DMA((8,)))
-
-
-def local_part(b_ref, x_ref, d3_ref, s3_ref, p3_ref, acc_ref):
+    pl.run_scoped(work, mat, mat, mat, pltpu.SemaphoreType.DMA((5 + 3 * blocks,)))
+
+
+def local_block(k, b_ref, x_ref, d3_ref, s3_ref, p3_ref, acc_ref):
     width = d3_ref.shape[2]
     last = d3_ref.shape[1] // width - 1
-    x = [split3(x_ref[:, k * width : (k + 1) * width]) for k in range(last + 1)]
-    for k in range(last + 1):
-        rows = pl.ds(k * width, width)
-        part = times_split(x[k], *(d3_ref[j, rows, :] for j in range(3)))
-        if k > 0:
-            part = part + times_split(x[k - 1], *(s3_ref[j, rows, :] for j in range(3)))
-        if k < last:
-            part = part + times_split(x[k + 1], *(p3_ref[j, rows, :] for j in range(3)))
-        acc_ref[:, k * width : (k + 1) * width] = b_ref[:, k * width : (k + 1) * width] - part
+    rows = pl.ds(k * width, width)
+
+    def term(i, ref):
+        return times_split(split3(x_ref[:, i * width : (i + 1) * width]), *(ref[j, rows, :] for j in range(3)))
+
+    part = term(k, d3_ref)
+    if k > 0:
+        part = part + term(k - 1, s3_ref)
+    if k < last:
+        part = part + term(k + 1, p3_ref)
+    acc_ref[:, k * width : (k + 1) * width] = b_ref[:, k * width : (k + 1) * width] - part
+
+
+def local_part(b_ref, x_ref, d3_ref, s3_ref, p3_ref, acc_ref):
+    for k in range(d3_ref.shape[1] // d3_ref.shape[2]):
+        local_block(k, b_ref, x_ref, d3_ref, s3_ref, p3_ref, acc_ref)
 
 
 def choose(condition, left, right):
@@ -274,14 +286,14 @@
 def static_kernel(whole_ref, got_ref, twin_ref, prefix_ref, *outs, level):
     even = is_even()
     got, twin = got_ref[...], twin_ref[...]
-    other = jnp.concatenate([jnp.where(even, got, twin), jnp.where(even, twin, got)], 0)
+    other = jnp.concatenate([jnp.where(even, twin, got), jnp.where(even, got, twin)], 0)
     next_level(level, whole_ref[...], other, parts_of(prefix_ref), *outs)
 
 
 def chip_kernel(whole_ref, got_ref, twin_ref, prefix_ref, *outs):
     even = is_even()
     got, twin = got_ref[...], twin_ref[...]
-    other = dot(choose(even, got, twin), choose(even, twin, got))
+    other = dot(choose(even, twin, got), choose(even, got, twin))
     next_level(1, whole_ref[...], other, parts_of(prefix_ref), *outs)
 
 
@@ -430,11 +442,14 @@
     )
     before, after, mix = kernel_call(mix_kernel, [low_square, low_square, triple], near, far, chain)
 
+    def swap(values, distance):
+        return exchange(values, distance | 1)
+
     second, prefix, whole = kernel_call(pair_kernel, [low_square, triple, square], chain, near)
     seconds, reaches = [second], [None, prefix]
     for level in range(1, levels - 1):
-        got = exchange(chain if level == 1 else piece, 1 << level)
-        twin = exchange(got, 1)
+        got = swap(chain if level == 1 else piece, 1 << level)
+        twin = swap(got, 1)
         kernel = chip_kernel if level == 1 else functools.partial(static_kernel, level=level)
         second, prefix, *rest = kernel_call(
             kernel, [triple, triple] + [square, half] * (level < levels - 2), whole, got, twin, prefix, micros=1
@@ -451,7 +466,7 @@
             acc, near, far, s3, p3, local_inverse, mix, micros=0.8,
         )
         norms.append(norm)
-        swapped = exchange(both, 1)
+        swapped = swap(both, 1)
         far_top = across(own_top)
         groups = [(0, 1)]
         while sum(groups[-1]) < levels:
@@ -466,25 +481,25 @@
                 kernel = level0_wide_kernel if after_size == 2 else level0_kernel
                 total, carry, *more = kernel_call(kernel, outs, both, swapped, seconds[0], *following)
             elif size_of == 1:
-                got = exchange(total, 1 << level)
+                got = swap(total, 1 << level)
                 total, carry, *more = kernel_call(
                     functools.partial(level_kernel, level=level), outs, total, got, carry, reaches[level], seconds[level]
                 )
             else:
                 step = 1 << level
-                got = exchange(total, step)
-                low = exchange(carried, 2 * step)
-                cross = exchange(carried, 3 * step)
+                got = swap(total, step)
+                low = swap(carried, 2 * step)
+                cross = swap(carried, 3 * step)
                 total, carry, *more = kernel_call(
                     functools.partial(wide_kernel, level=level), outs, total, carried, got, low, cross, carry,
                     reaches[level], reaches[level + 1], seconds[level], seconds[level + 1], *following,
                 )
             carried = more[0] if more else None
         level, size_of = groups[-1]
-        gots = [exchange(total, 1 << level)]
+        gots = [swap(total, 1 << level)]
         if size_of == 2:
-            gots.append(exchange(carried, 2 << level))
-            gots.append(exchange(carried, 3 << level))
+            gots.append(swap(carried, 2 << level))
+            gots.append(swap(carried, 3 << level))
         top, previous, near, far = kernel_call(
             functools.partial(tips_kernel, level=level, wide=size_of == 2), [low_tip, low_tip, tip, tip],
             *gots, *reaches[level : level + size_of], carry, swapped, far_top, local, solution, upper_spikes, lower_spikes,

time: 92.5 us -> 90.9 us (0.983)
  waiting for transfers between devices: 36.3 us -> 31.5 us
  starting transfers between devices: 39.4 us -> 42.3 us
    ppermute x21, waiting for transfers between devices: 29.8 us -> 25 us  [exchange(): return lax.ppermute(values, AXIS, [(i, i ^ distance) for i in range(count)])]
    ppermute x21, starting transfers between devices: 28.4 us -> 31.9 us  [exchange(): return lax.ppermute(values, AXIS, [(i, i ^ distance) for i in range(count)])]
  transfers between devices with their start and end apart: 27 -> 27, of which waited for: 16 -> 15; matrix products, arithmetic and copies ran while one was open for 1% -> 1% of each run, Pallas kernels for 10% -> 10%
where the time goes in v4:
time: 90.9 us; the launch traced here: 90.7 us
  starting transfers between devices  42.3 us (47%)
  waiting for transfers between devices  31.5 us (35%)
  Pallas kernels  15.4 us (17%)
    ppermute x21, starting transfers between devices, exchange(): return lax.ppermute(values, AXIS, [(i, i ^ distance) for i in range(count)])  31.9 us
    ppermute x21, waiting for transfers between devices, exchange(): return lax.ppermute(values, AXIS, [(i, i ^ distance) for i in range(count)])  25 us
    pallas_call x20, Pallas kernels, kernel_call(): pl.pallas_call(kernel, in_specs=specs, out_specs=[pl.BlockSpec(memory_spa...  14.7 us
    all_to_all x1, starting transfers between devices, body(): gathered = lax.all_to_all(mine, AXIS, 0, 0, tiled=True)  7.16 us
    all_to_all x1, waiting for transfers between devices, body(): gathered = lax.all_to_all(mine, AXIS, 0, 0, tiled=True)  6.51 us
    ppermute x5, starting transfers between devices, across(): return lax.ppermute(values, AXIS, pairs + [(b, a) for a, b in pairs])  3.28 us
  transfers between devices with their start and end apart: 27, of which 15 were waited for; matrix products, arithmetic and copies ran while one was open for 1% of the time, Pallas kernels for 10%

profile of v4, /device:TPU:0, one launch (start us, length us, event | category | flops | bytes accessed | tf_op | source)
XLA Modules:
  0.0 90.7 jit_solution(6569563366352817513)
XLA Ops:
  0.6 1.2 %shard_map.96 = (bf16[608,256]{1,0:T(8,128)(2,1)S(1)}, bf16[352,256]{1,0:T(8,128)(2,1)S(1)}, bf16[256,256]{1,0:T(8,128)(2,1)S(1)}) custom-call(f32[32,1024]{1,0:T(8,128)} %x_hbm.3, bf16[256,1024]{1,0:T(8,128)(2,1)} %u_hbm.3, bf16[256,1024]{1,0:T(8,128)(2,1)} %l_hbm.3), custom_call_target="tpu_custom_call" | custom-call | flops 30000000 | bytes 622592 | tf_op jit(solution)/shard_map/pallas_call | solution.py:34
  1.8 0.6 collective-permute-start
  2.4 2.6 %collective-permute-start.4 = (bf16[256,256]{1,0:T(8,128)(2,1)S(1)}, bf16[256,256]{1,0:T(8,128)(2,1)S(1)}, u32[]{:S(2)}, u32[]{:S(2)}) collective-permute-start(bf16[256,256]{1,0:T(8,128)(2,1)S(1)} %get-tuple-element.72.chain_ref.own_ref.refs_11_.refs_14_), channel_id=1, source_target_pairs={{0,3},{1,2},{2,1},{3,0},{4,7},{5,6},{6,5},{7,4},{8,11},{9,10},{10,... | collective-permute-start | bytes 393224 | tf_op jit(solution)/shard_map/ppermute | solution.py:20
  5.0 3.8 %collective-permute-done.4.got_ref = bf16[256,256]{1,0:T(8,128)(2,1)S(1)} collective-permute-done((bf16[256,256]{1,0:T(8,128)(2,1)S(1)}, bf16[256,256]{1,0:T(8,128)(2,1)S(1)}, u32[]{:S(2)}, u32[]{:S(2)}) %collective-permute-start.4) | collective-permute-done | bytes 131104 | tf_op jit(solution)/shard_map/ppermute | solution.py:20
  8.8 0.1 collective-permute-start.5
  8.9 0.3 shard_map.99
  9.1 1.0 %collective-permute-done.5.twin_ref = bf16[256,256]{1,0:T(8,128)(2,1)S(1)} collective-permute-done((bf16[256,256]{1,0:T(8,128)(2,1)S(1)}, bf16[256,256]{1,0:T(8,128)(2,1)S(1)}, u32[]{:S(2)}, u32[]{:S(2)}) %collective-permute-start.5) | collective-permute-done | bytes 131104 | tf_op jit(solution)/shard_map/ppermute | solution.py:20
  10.1 0.8 shard_map.101
  10.9 1.5 %collective-permute-start.7 = (f32[128,256]{1,0:T(8,128)S(1)}, f32[128,256]{1,0:T(8,128)S(1)}, u32[]{:S(2)}, u32[]{:S(2)}) collective-permute-start(f32[128,256]{1,0:T(8,128)S(1)} %get-tuple-element.85), channel_id=1, source_target_pairs={{0,5},{1,4},{2,7},{3,6},{4,1},{5,0},{6,3},{7,2},{8,13},{9,12},{10,... | collective-permute-start | bytes 393224 | tf_op jit(solution)/shard_map/ppermute | solution.py:20
  12.4 4.0 %collective-permute-done.7.got_ref = f32[128,256]{1,0:T(8,128)S(1)} collective-permute-done((f32[128,256]{1,0:T(8,128)S(1)}, f32[128,256]{1,0:T(8,128)S(1)}, u32[]{:S(2)}, u32[]{:S(2)}) %collective-permute-start.7) | collective-permute-done | bytes 131104 | tf_op jit(solution)/shard_map/ppermute | solution.py:20
  16.4 0.1 collective-permute-start.8
  16.6 0.7 collective-permute-start.1
  17.3 0.5 collective-permute-done.8.twin_ref
  17.8 0.6 shard_map.103
  18.4 3.5 %collective-permute-start.10 = (f32[128,256]{1,0:T(8,128)S(1)}, f32[128,256]{1,0:T(8,128)S(1)}, u32[]{:S(2)}, u32[]{:S(2)}) collective-permute-start(f32[128,256]{1,0:T(8,128)S(1)} %get-tuple-element.91), channel_id=1, source_target_pairs={{0,9},{1,8},{2,11},{3,10},{4,13},{5,12},{6,15},{7,14},{8,1},{9,0},... | collective-permute-start | bytes 393224 | tf_op jit(solution)/shard_map/ppermute | solution.py:20
  21.9 3.3 %shard_map.95 = (f32[32,1024]{1,0:T(8,128)S(1)}, f32[32,1024]{1,0:T(8,128)S(1)}, f32[32,1024]{1,0:T(8,128)S(1)}, bf16[3,1024,256]{2,1,0:T(8,128)(2,1)S(1)}, bf16...) custom-call(f32[32,1024]{1,0:T(8,128)} %b_hbm.1, ...), custom_call_target="tpu_custom_call" | custom-call | flops 300000000 | bytes 8257536 | tf_op jit(solution)/shard_map/pallas_call | solution.py:34
  25.3 0.2 shard_map.97
  25.5 0.8 shard_map.98
  26.3 1.1 %collective-permute-start.2 = (f32[64,256]{1,0:T(8,128)S(1)}, f32[64,256]{1,0:T(8,128)S(1)}, u32[]{:S(2)}, u32[]{:S(2)}) collective-permute-start(f32[64,256]{1,0:T(8,128)S(1)} %get-tuple-element.74.both_ref), channel_id=1, source_target_pairs={{0,1},{1,0},{2,3},{3,2},{4,5},{5,4},{6,7},{7,6},{8,9},{9,8},{10,11... | collective-permute-start | bytes 196616 | tf_op jit(solution)/shard_map/ppermute | solution.py:20
  27.4 0.4 collective-permute-start.11
  27.8 0.5 collective-permute-done.2.got_ref.refs_3_
  28.3 0.1 shard_map.100
  28.4 1.2 %collective-permute-start.3 = (f32[32,256]{1,0:T(8,128)S(1)}, f32[32,256]{1,0:T(8,128)S(1)}, u32[]{:S(2)}, u32[]{:S(2)}) collective-permute-start(f32[32,256]{1,0:T(8,128)S(1)} %get-tuple-element.76.total_ref), channel_id=1, source_target_pairs={{0,3},{1,2},{2,1},{3,0},{4,7},{5,6},{6,5},{7,4},{8,11},{9,10},{10,... | collective-permute-start | bytes 98312 | tf_op jit(solution)/shard_map/ppermute | solution.py:20
  29.6 2.1 %collective-permute-done.3.got_ref = f32[32,256]{1,0:T(8,128)S(1)} collective-permute-done((f32[32,256]{1,0:T(8,128)S(1)}, f32[32,256]{1,0:T(8,128)S(1)}, u32[]{:S(2)}, u32[]{:S(2)}) %collective-permute-start.3) | collective-permute-done | bytes 32800 | tf_op jit(solution)/shard_map/ppermute | solution.py:20
  31.8 0.2 shard_map.102
  32.0 1.2 %collective-permute-start.6 = (f32[32,256]{1,0:T(8,128)S(1)}, f32[32,256]{1,0:T(8,128)S(1)}, u32[]{:S(2)}, u32[]{:S(2)}) collective-permute-start(f32[32,256]{1,0:T(8,128)S(1)} %get-tuple-element.81.total_ref), channel_id=1, source_target_pairs={{0,5},{1,4},{2,7},{3,6},{4,1},{5,0},{6,3},{7,2},{8,13},{9,12},{10,... | collective-permute-start | bytes 98312 | tf_op jit(solution)/shard_map/ppermute | solution.py:20
  33.2 2.2 %collective-permute-done.6.got_ref = f32[32,256]{1,0:T(8,128)S(1)} collective-permute-done((f32[32,256]{1,0:T(8,128)S(1)}, f32[32,256]{1,0:T(8,128)S(1)}, u32[]{:S(2)}, u32[]{:S(2)}) %collective-permute-start.6) | collective-permute-done | bytes 32800 | tf_op jit(solution)/shard_map/ppermute | solution.py:20
  35.4 0.2 shard_map.104
  35.6 0.9 collective-permute-start.9
  36.5 0.7 collective-permute-start.13
  37.2 0.4 shard_map.105
  37.7 1.4 %collective-permute-done.9.got_ref = f32[32,256]{1,0:T(8,128)S(1)} collective-permute-done((f32[32,256]{1,0:T(8,128)S(1)}, f32[32,256]{1,0:T(8,128)S(1)}, u32[]{:S(2)}, u32[]{:S(2)}) %collective-permute-start.9) | collective-permute-done | bytes 32800 | tf_op jit(solution)/shard_map/ppermute | solution.py:20
  39.0 0.2 shard_map.106
  39.3 4.2 %collective-permute-start.12 = (f32[32,256]{1,0:T(8,128)S(1)}, f32[32,256]{1,0:T(8,128)S(1)}, u32[]{:S(2)}, u32[]{:S(2)}) collective-permute-start(f32[32,256]{1,0:T(8,128)S(1)} %get-tuple-element.93), channel_id=1, source_target_pairs={{0,17},{1,16},{2,19},{3,18},{4,21},{5,20},{6,23},{7,22},{8,25},{9,... | collective-permute-start | bytes 98312 | tf_op jit(solution)/shard_map/ppermute | solution.py:20
  43.5 1.6 %collective-permute-done.12.refs_0_ = f32[32,256]{1,0:T(8,128)S(1)} collective-permute-done((f32[32,256]{1,0:T(8,128)S(1)}, f32[32,256]{1,0:T(8,128)S(1)}, u32[]{:S(2)}, u32[]{:S(2)}) %collective-permute-start.12) | collective-permute-done | bytes 32800 | tf_op jit(solution)/shard_map/ppermute | solution.py:20
  45.1 0.7 shard_map.107
  45.8 0.5 collective-permute-start.14
  46.3 0.7 collective-permute-start.15
  46.9 1.0 %shard_map.108 = (f32[32,1024]{1,0:T(8,128)S(1)}, f32[32,1024]{1,0:T(8,128)S(1)}) custom-call(bf16[32,256]{1,0:T(8,128)(2,1)S(1)} %get-tuple-element.103.top_ref, bf16[32,256]{1,0:T(8,128)(2,1)S(1)} %get-tuple-element.104.previous_ref, f32[32,1024]{1,0:T(8,128)S(1)} %get-tuple-element.97.refs_5_.local_ref, f32[32,1024]{1,0:T(8,128)S(1)} %get-tuple-element.98.refs_6_.x_ref, ...), custom_call_target="tpu_custom_call" | custom-call | flops 100000000 | bytes 262144 | tf_op jit(solution)/shard_map/pallas_call | solution.py:34
  47.9 0.0 collective-permute-done.14.near_ref
  48.0 0.8 shard_map.109
  48.8 3.7 %collective-permute-start.16 = (f32[64,256]{1,0:T(8,128)S(1)}, f32[64,256]{1,0:T(8,128)S(1)}, u32[]{:S(2)}, u32[]{:S(2)}) collective-permute-start(f32[64,256]{1,0:T(8,128)S(1)} %get-tuple-element.110.both_ref), channel_id=1, source_target_pairs={{0,1},{1,0},{2,3},{3,2},{4,5},{5,4},{6,7},{7,6},{8,9},{9,8},{10,11... | collective-permute-start | bytes 196616 | tf_op jit(solution)/shard_map/ppermute | solution.py:20
  52.4 0.9 collective-permute-done.16.got_ref.refs_6_
  53.3 0.3 shard_map.110
  53.6 2.5 %collective-permute-start.17 = (f32[32,256]{1,0:T(8,128)S(1)}, f32[32,256]{1,0:T(8,128)S(1)}, u32[]{:S(2)}, u32[]{:S(2)}) collective-permute-start(f32[32,256]{1,0:T(8,128)S(1)} %get-tuple-element.111.total_ref), channel_id=1, source_target_pairs={{0,3},{1,2},{2,1},{3,0},{4,7},{5,6},{6,5},{7,4},{8,11},{9,10},{10,... | collective-permute-start | bytes 98312 | tf_op jit(solution)/shard_map/ppermute | solution.py:20
  56.1 1.9 %collective-permute-start.19 = (f32[32,256]{1,0:T(8,128)S(1)}, f32[32,256]{1,0:T(8,128)S(1)}, u32[]{:S(2)}, u32[]{:S(2)}) collective-permute-start(f32[32,256]{1,0:T(8,128)S(1)} %get-tuple-element.112.carried_ref), channel_id=1, source_target_pairs={{0,7},{1,6},{2,5},{3,4},{4,3},{5,2},{6,1},{7,0},{8,15},{9,14},{10,... | collective-permute-start | bytes 98312 | tf_op jit(solution)/shard_map/ppermute | solution.py:20
  58.1 0.7 collective-permute-start.23
  58.8 1.6 %collective-permute-done.19.cross_ref = f32[32,256]{1,0:T(8,128)S(1)} collective-permute-done((f32[32,256]{1,0:T(8,128)S(1)}, f32[32,256]{1,0:T(8,128)S(1)}, u32[]{:S(2)}, u32[]{:S(2)}) %collective-permute-start.19) | collective-permute-done | bytes 32800 | tf_op jit(solution)/shard_map/ppermute | solution.py:20
  60.4 1.0 %collective-permute-done.18.low_ref = f32[32,256]{1,0:T(8,128)S(1)} collective-permute-done((f32[32,256]{1,0:T(8,128)S(1)}, f32[32,256]{1,0:T(8,128)S(1)}, u32[]{:S(2)}, u32[]{:S(2)}) %collective-permute-start.18) | collective-permute-done | bytes 32800 | tf_op jit(solution)/shard_map/ppermute | solution.py:20
  61.4 0.7 shard_map.111
  62.2 2.2 %collective-permute-start.20 = (f32[32,256]{1,0:T(8,128)S(1)}, f32[32,256]{1,0:T(8,128)S(1)}, u32[]{:S(2)}, u32[]{:S(2)}) collective-permute-start(f32[32,256]{1,0:T(8,128)S(1)} %get-tuple-element.114), channel_id=1, source_target_pairs={{0,9},{1,8},{2,11},{3,10},{4,13},{5,12},{6,15},{7,14},{8,1},{9,0},... | collective-permute-start | bytes 98312 | tf_op jit(solution)/shard_map/ppermute | solution.py:20
  64.4 3.5 %collective-permute-start.22 = (f32[32,256]{1,0:T(8,128)S(1)}, f32[32,256]{1,0:T(8,128)S(1)}, u32[]{:S(2)}, u32[]{:S(2)}) collective-permute-start(f32[32,256]{1,0:T(8,128)S(1)} %get-tuple-element.115), channel_id=1, source_target_pairs={{0,25},{1,24},{2,27},{3,26},{4,29},{5,28},{6,31},{7,30},{8,17},{9,... | collective-permute-start | bytes 98312 | tf_op jit(solution)/shard_map/ppermute | solution.py:20
  68.0 2.0 %collective-permute-done.22.refs_2_ = f32[32,256]{1,0:T(8,128)S(1)} collective-permute-done((f32[32,256]{1,0:T(8,128)S(1)}, f32[32,256]{1,0:T(8,128)S(1)}, u32[]{:S(2)}, u32[]{:S(2)}) %collective-permute-start.22) | collective-permute-done | bytes 32800 | tf_op jit(solution)/shard_map/ppermute | solution.py:20
  69.9 2.2 %collective-permute-done.21.refs_1_ = f32[32,256]{1,0:T(8,128)S(1)} collective-permute-done((f32[32,256]{1,0:T(8,128)S(1)}, f32[32,256]{1,0:T(8,128)S(1)}, u32[]{:S(2)}, u32[]{:S(2)}) %collective-permute-start.21) | collective-permute-done | bytes 32800 | tf_op jit(solution)/shard_map/ppermute | solution.py:20
  72.2 0.7 shard_map.112
  72.9 0.1 collective-permute-start.24
  73.0 0.7 collective-permute-start.25
  73.7 1.0 %shard_map.113 = (f32[32,1024]{1,0:T(8,128)S(1)}, f32[32,1024]{1,0:T(8,128)S(1)}, f32[32,128]{1,0:T(8,128)S(1)}, f32[1,128]{1,0:T(1,128)S(1)}) custom-call(bf16[32,256]{1,0:T(8,128)(2,1)S(1)} %get-tuple-element.120.top_ref, bf16[32,256]{1,0:T(8,128)(2,1)S(1)} %get-tuple-element.121.previous_ref, f32[32,1024]{1,0:T(8,128)S(1)} %get-tuple-element.118.refs_8_.local_ref, ...), custom_call_target="tpu_custom_call" | custom-call | flops 100000000 | bytes 279040 | tf_op jit(solution)/shard_map/pallas_call | solution.py:34
  74.7 0.0 collective-permute-done.24.near_ref
  74.7 1.0 %shard_map.114 = f32[32,128]{1,0:T(8,128)} custom-call(f32[32,1024]{1,0:T(8,128)S(1)} %get-tuple-element.125.acc_ref, f32[32,256]{1,0:T(8,128)S(1)} %collective-permute-done.24.near_ref, f32[32,256]{1,0:T(8,128)S(1)} %collective-permute-done.25.far_ref, bf16[3,1024,256]{2,1,0:T(8,128)(2,1)S(1)} %get-tuple-element.69.s3_ref, ...), custom_call_target="tpu_custom_call" | custom-call | flops 30000000 | bytes 16384 | tf_op jit(solution)/shard_map/pallas_call | solution.py:34
  75.7 7.2 %all-to-all-start = ((f32[32,1,128]{2,1,0:T(1,128)}), f32[32,1,128]{2,1,0:T(1,128)S(1)}, u32[]{:S(2)}, u32[]{:S(2)}) async-start(f32[32,1,128]{2,1,0:T(1,128)} %bitcast.1), calls=%async_computation | async-start | bytes 32768 | tf_op jit(solution)/shard_map/all_to_all | solution.py:519
  82.8 0.7 copy.11
  83.5 6.5 %all-to-all-done = f32[32,1,128]{2,1,0:T(1,128)S(1)} async-done(((f32[32,1,128]{2,1,0:T(1,128)}), f32[32,1,128]{2,1,0:T(1,128)S(1)}, u32[]{:S(2)}, u32[]{:S(2)}) %all-to-all-start) | async-done | bytes 16416 | tf_op jit(solution)/shard_map/all_to_all | solution.py:519
  90.0 0.7 shard_map.115
  (12 shorter events, 0.0 us)
Async XLA Ops:
  1.8 7.1 %collective-permute-start = (bf16[608,256]{1,0:T(8,128)(2,1)S(1)}, bf16[608,256]{1,0:T(8,128)(2,1)S(1)}, u32[]{:S(2)}, u32[]{:S(2)}) collective-permute-start(bf16[608,256]{1,0:T(8,128)(2,1)S(1)} %get-tuple-element.67), channel_id=1, source_target_pairs={{0,1},{1,0},{2,3},{3,2},{4,5},{5,4},{6,7},{7,6},{8,9},{9,8},{10,11... | collective-permute-start | bytes 933896 | tf_op jit(solution)/shard_map/ppermute | solution.py:20
  2.4 6.4 %collective-permute-start.4 = (bf16[256,256]{1,0:T(8,128)(2,1)S(1)}, bf16[256,256]{1,0:T(8,128)(2,1)S(1)}, u32[]{:S(2)}, u32[]{:S(2)}) collective-permute-start(bf16[256,256]{1,0:T(8,128)(2,1)S(1)} %get-tuple-element.72.chain_ref.own_ref.refs_11_.refs_14_), channel_id=1, source_target_pairs={{0,3},{1,2},{2,1},{3,0},{4,7},{5,6},{6,5},{7,4},{8,11},{9,10},{10,... | collective-permute-start | bytes 393224 | tf_op jit(solution)/shard_map/ppermute | solution.py:20
  8.8 1.3 %collective-permute-start.5 = (bf16[256,256]{1,0:T(8,128)(2,1)S(1)}, bf16[256,256]{1,0:T(8,128)(2,1)S(1)}, u32[]{:S(2)}, u32[]{:S(2)}) collective-permute-start(bf16[256,256]{1,0:T(8,128)(2,1)S(1)} %collective-permute-done.4.got_ref), channel_id=1, source_target_pairs={{0,1},{1,0},{2,3},{3,2},{4,5},{5,4},{6,7},{7,6},{8,9},{9,8},{10,11... | collective-permute-start | bytes 393224 | tf_op jit(solution)/shard_map/ppermute | solution.py:20
  10.9 5.5 %collective-permute-start.7 = (f32[128,256]{1,0:T(8,128)S(1)}, f32[128,256]{1,0:T(8,128)S(1)}, u32[]{:S(2)}, u32[]{:S(2)}) collective-permute-start(f32[128,256]{1,0:T(8,128)S(1)} %get-tuple-element.85), channel_id=1, source_target_pairs={{0,5},{1,4},{2,7},{3,6},{4,1},{5,0},{6,3},{7,2},{8,13},{9,12},{10,... | collective-permute-start | bytes 393224 | tf_op jit(solution)/shard_map/ppermute | solution.py:20
  16.4 1.3 %collective-permute-start.8 = (f32[128,256]{1,0:T(8,128)S(1)}, f32[128,256]{1,0:T(8,128)S(1)}, u32[]{:S(2)}, u32[]{:S(2)}) collective-permute-start(f32[128,256]{1,0:T(8,128)S(1)} %collective-permute-done.7.got_ref), channel_id=1, source_target_pairs={{0,1},{1,0},{2,3},{3,2},{4,5},{5,4},{6,7},{7,6},{8,9},{9,8},{10,11... | collective-permute-start | bytes 393224 | tf_op jit(solution)/shard_map/ppermute | solution.py:20
  16.6 8.7 %collective-permute-start.1 = (bf16[352,256]{1,0:T(8,128)(2,1)S(1)}, bf16[352,256]{1,0:T(8,128)(2,1)S(1)}, u32[]{:S(2)}, u32[]{:S(2)}) collective-permute-start(bf16[352,256]{1,0:T(8,128)(2,1)S(1)} %get-tuple-element.68), channel_id=1, source_target_pairs={{1,2},{3,4},{5,6},{7,8},{9,10},{11,12},{13,14},{15,16},{17,18},{19... | collective-permute-start | bytes 540680 | tf_op jit(solution)/shard_map/ppermute | solution.py:26
  18.4 8.9 %collective-permute-start.10 = (f32[128,256]{1,0:T(8,128)S(1)}, f32[128,256]{1,0:T(8,128)S(1)}, u32[]{:S(2)}, u32[]{:S(2)}) collective-permute-start(f32[128,256]{1,0:T(8,128)S(1)} %get-tuple-element.91), channel_id=1, source_target_pairs={{0,9},{1,8},{2,11},{3,10},{4,13},{5,12},{6,15},{7,14},{8,1},{9,0},... | collective-permute-start | bytes 393224 | tf_op jit(solution)/shard_map/ppermute | solution.py:20
  26.3 2.0 %collective-permute-start.2 = (f32[64,256]{1,0:T(8,128)S(1)}, f32[64,256]{1,0:T(8,128)S(1)}, u32[]{:S(2)}, u32[]{:S(2)}) collective-permute-start(f32[64,256]{1,0:T(8,128)S(1)} %get-tuple-element.74.both_ref), channel_id=1, source_target_pairs={{0,1},{1,0},{2,3},{3,2},{4,5},{5,4},{6,7},{7,6},{8,9},{9,8},{10,11... | collective-permute-start | bytes 196616 | tf_op jit(solution)/shard_map/ppermute | solution.py:20
  27.4 9.8 %collective-permute-start.11 = (f32[128,256]{1,0:T(8,128)S(1)}, f32[128,256]{1,0:T(8,128)S(1)}, u32[]{:S(2)}, u32[]{:S(2)}) collective-permute-start(f32[128,256]{1,0:T(8,128)S(1)} %collective-permute-done.10.got_ref), channel_id=1, source_target_pairs={{0,1},{1,0},{2,3},{3,2},{4,5},{5,4},{6,7},{7,6},{8,9},{9,8},{10,11... | collective-permute-start | bytes 393224 | tf_op jit(solution)/shard_map/ppermute | solution.py:20
  28.4 3.4 %collective-permute-start.3 = (f32[32,256]{1,0:T(8,128)S(1)}, f32[32,256]{1,0:T(8,128)S(1)}, u32[]{:S(2)}, u32[]{:S(2)}) collective-permute-start(f32[32,256]{1,0:T(8,128)S(1)} %get-tuple-element.76.total_ref), channel_id=1, source_target_pairs={{0,3},{1,2},{2,1},{3,0},{4,7},{5,6},{6,5},{7,4},{8,11},{9,10},{10,... | collective-permute-start | bytes 98312 | tf_op jit(solution)/shard_map/ppermute | solution.py:20
  32.0 3.4 %collective-permute-start.6 = (f32[32,256]{1,0:T(8,128)S(1)}, f32[32,256]{1,0:T(8,128)S(1)}, u32[]{:S(2)}, u32[]{:S(2)}) collective-permute-start(f32[32,256]{1,0:T(8,128)S(1)} %get-tuple-element.81.total_ref), channel_id=1, source_target_pairs={{0,5},{1,4},{2,7},{3,6},{4,1},{5,0},{6,3},{7,2},{8,13},{9,12},{10,... | collective-permute-start | bytes 98312 | tf_op jit(solution)/shard_map/ppermute | solution.py:20
  35.6 3.4 %collective-permute-start.9 = (f32[32,256]{1,0:T(8,128)S(1)}, f32[32,256]{1,0:T(8,128)S(1)}, u32[]{:S(2)}, u32[]{:S(2)}) collective-permute-start(f32[32,256]{1,0:T(8,128)S(1)} %get-tuple-element.87.total_ref), channel_id=1, source_target_pairs={{0,9},{1,8},{2,11},{3,10},{4,13},{5,12},{6,15},{7,14},{8,1},{9,0},... | collective-permute-start | bytes 98312 | tf_op jit(solution)/shard_map/ppermute | solution.py:20
  36.5 7.0 %collective-permute-start.13 = (f32[32,256]{1,0:T(8,128)S(1)}, f32[32,256]{1,0:T(8,128)S(1)}, u32[]{:S(2)}, u32[]{:S(2)}) collective-permute-start(f32[32,256]{1,0:T(8,128)S(1)} %get-tuple-element.96), channel_id=1, source_target_pairs={{1,2},{3,4},{5,6},{7,8},{9,10},{11,12},{13,14},{15,16},{17,18},{19... | collective-permute-start | bytes 98312 | tf_op jit(solution)/shard_map/ppermute | solution.py:26
  39.3 5.8 %collective-permute-start.12 = (f32[32,256]{1,0:T(8,128)S(1)}, f32[32,256]{1,0:T(8,128)S(1)}, u32[]{:S(2)}, u32[]{:S(2)}) collective-permute-start(f32[32,256]{1,0:T(8,128)S(1)} %get-tuple-element.93), channel_id=1, source_target_pairs={{0,17},{1,16},{2,19},{3,18},{4,21},{5,20},{6,23},{7,22},{8,25},{9,... | collective-permute-start | bytes 98312 | tf_op jit(solution)/shard_map/ppermute | solution.py:20
  45.8 2.2 %collective-permute-start.14 = (f32[32,256]{1,0:T(8,128)S(1)}, f32[32,256]{1,0:T(8,128)S(1)}, u32[]{:S(2)}, u32[]{:S(2)}) collective-permute-start(f32[32,256]{1,0:T(8,128)S(1)} %get-tuple-element.108), channel_id=1, source_target_pairs={{0,1},{1,0},{2,3},{3,2},{4,5},{5,4},{6,7},{7,6},{8,9},{9,8},{10,11... | collective-permute-start | bytes 98312 | tf_op jit(solution)/shard_map/ppermute | solution.py:20
  46.3 1.7 %collective-permute-start.15 = (f32[32,256]{1,0:T(8,128)S(1)}, f32[32,256]{1,0:T(8,128)S(1)}, u32[]{:S(2)}, u32[]{:S(2)}) collective-permute-start(f32[32,256]{1,0:T(8,128)S(1)} %get-tuple-element.109), channel_id=1, source_target_pairs={{1,2},{3,4},{5,6},{7,8},{9,10},{11,12},{13,14},{15,16},{17,18},{19... | collective-permute-start | bytes 98312 | tf_op jit(solution)/shard_map/ppermute | solution.py:26
  48.8 4.6 %collective-permute-start.16 = (f32[64,256]{1,0:T(8,128)S(1)}, f32[64,256]{1,0:T(8,128)S(1)}, u32[]{:S(2)}, u32[]{:S(2)}) collective-permute-start(f32[64,256]{1,0:T(8,128)S(1)} %get-tuple-element.110.both_ref), channel_id=1, source_target_pairs={{0,1},{1,0},{2,3},{3,2},{4,5},{5,4},{6,7},{7,6},{8,9},{9,8},{10,11... | collective-permute-start | bytes 196616 | tf_op jit(solution)/shard_map/ppermute | solution.py:20
  53.6 5.1 %collective-permute-start.17 = (f32[32,256]{1,0:T(8,128)S(1)}, f32[32,256]{1,0:T(8,128)S(1)}, u32[]{:S(2)}, u32[]{:S(2)}) collective-permute-start(f32[32,256]{1,0:T(8,128)S(1)} %get-tuple-element.111.total_ref), channel_id=1, source_target_pairs={{0,3},{1,2},{2,1},{3,0},{4,7},{5,6},{6,5},{7,4},{8,11},{9,10},{10,... | collective-permute-start | bytes 98312 | tf_op jit(solution)/shard_map/ppermute | solution.py:20
  56.1 4.3 %collective-permute-start.19 = (f32[32,256]{1,0:T(8,128)S(1)}, f32[32,256]{1,0:T(8,128)S(1)}, u32[]{:S(2)}, u32[]{:S(2)}) collective-permute-start(f32[32,256]{1,0:T(8,128)S(1)} %get-tuple-element.112.carried_ref), channel_id=1, source_target_pairs={{0,7},{1,6},{2,5},{3,4},{4,3},{5,2},{6,1},{7,0},{8,15},{9,14},{10,... | collective-permute-start | bytes 98312 | tf_op jit(solution)/shard_map/ppermute | solution.py:20
  58.1 3.4 %collective-permute-start.18 = (f32[32,256]{1,0:T(8,128)S(1)}, f32[32,256]{1,0:T(8,128)S(1)}, u32[]{:S(2)}, u32[]{:S(2)}) collective-permute-start(f32[32,256]{1,0:T(8,128)S(1)} %get-tuple-element.112.carried_ref), channel_id=1, source_target_pairs={{0,5},{1,4},{2,7},{3,6},{4,1},{5,0},{6,3},{7,2},{8,13},{9,12},{10,... | collective-permute-start | bytes 98312 | tf_op jit(solution)/shard_map/ppermute | solution.py:20
  58.1 9.9 %collective-permute-start.23 = (f32[32,256]{1,0:T(8,128)S(1)}, f32[32,256]{1,0:T(8,128)S(1)}, u32[]{:S(2)}, u32[]{:S(2)}) collective-permute-start(f32[32,256]{1,0:T(8,128)S(1)} %get-tuple-element.117), channel_id=1, source_target_pairs={{1,2},{3,4},{5,6},{7,8},{9,10},{11,12},{13,14},{15,16},{17,18},{19... | collective-permute-start | bytes 98312 | tf_op jit(solution)/shard_map/ppermute | solution.py:26
  62.2 5.8 %collective-permute-start.20 = (f32[32,256]{1,0:T(8,128)S(1)}, f32[32,256]{1,0:T(8,128)S(1)}, u32[]{:S(2)}, u32[]{:S(2)}) collective-permute-start(f32[32,256]{1,0:T(8,128)S(1)} %get-tuple-element.114), channel_id=1, source_target_pairs={{0,9},{1,8},{2,11},{3,10},{4,13},{5,12},{6,15},{7,14},{8,1},{9,0},... | collective-permute-start | bytes 98312 | tf_op jit(solution)/shard_map/ppermute | solution.py:20
  64.4 5.5 %collective-permute-start.22 = (f32[32,256]{1,0:T(8,128)S(1)}, f32[32,256]{1,0:T(8,128)S(1)}, u32[]{:S(2)}, u32[]{:S(2)}) collective-permute-start(f32[32,256]{1,0:T(8,128)S(1)} %get-tuple-element.115), channel_id=1, source_target_pairs={{0,25},{1,24},{2,27},{3,26},{4,29},{5,28},{6,31},{7,30},{8,17},{9,... | collective-permute-start | bytes 98312 | tf_op jit(solution)/shard_map/ppermute | solution.py:20
  67.9 4.2 %collective-permute-start.21 = (f32[32,256]{1,0:T(8,128)S(1)}, f32[32,256]{1,0:T(8,128)S(1)}, u32[]{:S(2)}, u32[]{:S(2)}) collective-permute-start(f32[32,256]{1,0:T(8,128)S(1)} %get-tuple-element.115), channel_id=1, source_target_pairs={{0,17},{1,16},{2,19},{3,18},{4,21},{5,20},{6,23},{7,22},{8,25},{9,... | collective-permute-start | bytes 98312 | tf_op jit(solution)/shard_map/ppermute | solution.py:20
  72.9 1.8 %collective-permute-start.24 = (f32[32,256]{1,0:T(8,128)S(1)}, f32[32,256]{1,0:T(8,128)S(1)}, u32[]{:S(2)}, u32[]{:S(2)}) collective-permute-start(f32[32,256]{1,0:T(8,128)S(1)} %get-tuple-element.126), channel_id=1, source_target_pairs={{0,1},{1,0},{2,3},{3,2},{4,5},{5,4},{6,7},{7,6},{8,9},{9,8},{10,11... | collective-permute-start | bytes 98312 | tf_op jit(solution)/shard_map/ppermute | solution.py:20
  73.0 1.7 %collective-permute-start.25 = (f32[32,256]{1,0:T(8,128)S(1)}, f32[32,256]{1,0:T(8,128)S(1)}, u32[]{:S(2)}, u32[]{:S(2)}) collective-permute-start(f32[32,256]{1,0:T(8,128)S(1)} %get-tuple-element.127), channel_id=1, source_target_pairs={{1,2},{3,4},{5,6},{7,8},{9,10},{11,12},{13,14},{15,16},{17,18},{19... | collective-permute-start | bytes 98312 | tf_op jit(solution)/shard_map/ppermute | solution.py:26
  75.7 14.3 %all-to-all-start = ((f32[32,1,128]{2,1,0:T(1,128)}), f32[32,1,128]{2,1,0:T(1,128)S(1)}, u32[]{:S(2)}, u32[]{:S(2)}) async-start(f32[32,1,128]{2,1,0:T(1,128)} %bitcast.1), calls=%async_computation | async-start | bytes 32768 | tf_op jit(solution)/shard_map/all_to_all | solution.py:519

commit v5 on v2

--- a/solution.py
+++ b/solution.py
@@ -274,14 +274,14 @@
 def static_kernel(whole_ref, got_ref, twin_ref, prefix_ref, *outs, level):
     even = is_even()
     got, twin = got_ref[...], twin_ref[...]
-    other = jnp.concatenate([jnp.where(even, got, twin), jnp.where(even, twin, got)], 0)
+    other = jnp.concatenate([jnp.where(even, twin, got), jnp.where(even, got, twin)], 0)
     next_level(level, whole_ref[...], other, parts_of(prefix_ref), *outs)
 
 
 def chip_kernel(whole_ref, got_ref, twin_ref, prefix_ref, *outs):
     even = is_even()
     got, twin = got_ref[...], twin_ref[...]
-    other = dot(choose(even, got, twin), choose(even, twin, got))
+    other = dot(choose(even, twin, got), choose(even, got, twin))
     next_level(1, whole_ref[...], other, parts_of(prefix_ref), *outs)
 
 
@@ -430,11 +430,14 @@
     )
     before, after, mix = kernel_call(mix_kernel, [low_square, low_square, triple], near, far, chain)
 
+    def swap(values, distance):
+        return exchange(values, distance | 1)
+
     second, prefix, whole = kernel_call(pair_kernel, [low_square, triple, square], chain, near)
     seconds, reaches = [second], [None, prefix]
     for level in range(1, levels - 1):
-        got = exchange(chain if level == 1 else piece, 1 << level)
-        twin = exchange(got, 1)
+        got = swap(chain if level == 1 else piece, 1 << level)
+        twin = swap(got, 1)
         kernel = chip_kernel if level == 1 else functools.partial(static_kernel, level=level)
         second, prefix, *rest = kernel_call(
             kernel, [triple, triple] + [square, half] * (level < levels - 2), whole, got, twin, prefix, micros=1
@@ -451,12 +454,12 @@
             acc, near, far, s3, p3, local_inverse, mix, micros=0.8,
         )
         norms.append(norm)
-        swapped = exchange(both, 1)
+        swapped = swap(both, 1)
         far_top = across(own_top)
         groups = [(0, 1)]
         while sum(groups[-1]) < levels:
             level = sum(groups[-1])
-            groups.append((level, 2 if turn > 0 and level + 2 <= levels else 1))
+            groups.append((level, 2 if (turn > 0 or level == 1) and level + 2 <= levels else 1))
         carried = None
         for i, (level, size_of) in enumerate(groups[:-1]):
             after_size = groups[i + 1][1]
@@ -466,25 +469,25 @@
                 kernel = level0_wide_kernel if after_size == 2 else level0_kernel
                 total, carry, *more = kernel_call(kernel, outs, both, swapped, seconds[0], *following)
             elif size_of == 1:
-                got = exchange(total, 1 << level)
+                got = swap(total, 1 << level)
                 total, carry, *more = kernel_call(
                     functools.partial(level_kernel, level=level), outs, total, got, carry, reaches[level], seconds[level]
                 )
             else:
                 step = 1 << level
-                got = exchange(total, step)
-                low = exchange(carried, 2 * step)
-                cross = exchange(carried, 3 * step)
+                got = swap(total, step)
+                low = swap(carried, 2 * step)
+                cross = swap(carried, 3 * step)
                 total, carry, *more = kernel_call(
                     functools.partial(wide_kernel, level=level), outs, total, carried, got, low, cross, carry,
                     reaches[level], reaches[level + 1], seconds[level], seconds[level + 1], *following,
                 )
             carried = more[0] if more else None
         level, size_of = groups[-1]
-        gots = [exchange(total, 1 << level)]
+        gots = [swap(total, 1 << level)]
         if size_of == 2:
-            gots.append(exchange(carried, 2 << level))
-            gots.append(exchange(carried, 3 << level))
+            gots.append(swap(carried, 2 << level))
+            gots.append(swap(carried, 3 << level))
         top, previous, near, far = kernel_call(
             functools.partial(tips_kernel, level=level, wide=size_of == 2), [low_tip, low_tip, tip, tip],
             *gots, *reaches[level : level + size_of], carry, swapped, far_top, local, solution, upper_spikes, lower_spikes,

time: 92.5 us -> 91.3 us (0.987)
  waiting for transfers between devices: 36.3 us -> 31.9 us
  starting transfers between devices: 39.4 us -> 42.4 us
    ppermute x21 -> x22, waiting for transfers between devices: 29.8 us -> 25.3 us  [exchange(): return lax.ppermute(values, AXIS, [(i, i ^ distance) for i in range(count)])]
    ppermute x21 -> x22, starting transfers between devices: 28.4 us -> 31.7 us  [exchange(): return lax.ppermute(values, AXIS, [(i, i ^ distance) for i in range(count)])]
    pallas_call x20 -> x19, Pallas kernels: 14.4 us -> 14.6 us  [kernel_call(): pl.pallas_call(kernel, in_specs=specs, out_specs=[pl.BlockSpec(memory_spa...]
  transfers between devices with their start and end apart: 27 -> 28, of which waited for: 16 -> 17; matrix products, arithmetic and copies ran while one was open for 1% -> 1% of each run, Pallas kernels for 10% -> 10%
where the time goes in v5:
time: 91.3 us; the launch traced here: 91 us
  starting transfers between devices  42.4 us (46%)
  waiting for transfers between devices  31.9 us (35%)
  Pallas kernels  15.3 us (17%)
    ppermute x22, starting transfers between devices, exchange(): return lax.ppermute(values, AXIS, [(i, i ^ distance) for i in range(count)])  31.7 us
    ppermute x22, waiting for transfers between devices, exchange(): return lax.ppermute(values, AXIS, [(i, i ^ distance) for i in range(count)])  25.3 us
    pallas_call x19, Pallas kernels, kernel_call(): pl.pallas_call(kernel, in_specs=specs, out_specs=[pl.BlockSpec(memory_spa...  14.6 us
    all_to_all x1, starting transfers between devices, body(): gathered = lax.all_to_all(mine, AXIS, 0, 0, tiled=True)  7.39 us
    all_to_all x1, waiting for transfers between devices, body(): gathered = lax.all_to_all(mine, AXIS, 0, 0, tiled=True)  6.51 us
    ppermute x5, starting transfers between devices, across(): return lax.ppermute(values, AXIS, pairs + [(b, a) for a, b in pairs])  3.26 us
  transfers between devices with their start and end apart: 28, of which 17 were waited for; matrix products, arithmetic and copies ran while one was open for 1% of the time, Pallas kernels for 10%

profile of v5, /device:TPU:0, one launch (start us, length us, event | category | flops | bytes accessed | tf_op | source)
XLA Modules:
  0.0 91.0 jit_solution(3547960098609975189)
XLA Ops:
  0.6 1.2 %shard_map.96 = (bf16[608,256]{1,0:T(8,128)(2,1)S(1)}, bf16[352,256]{1,0:T(8,128)(2,1)S(1)}, bf16[256,256]{1,0:T(8,128)(2,1)S(1)}) custom-call(f32[32,1024]{1,0:T(8,128)} %x_hbm.3, bf16[256,1024]{1,0:T(8,128)(2,1)} %u_hbm.3, bf16[256,1024]{1,0:T(8,128)(2,1)} %l_hbm.3), custom_call_target="tpu_custom_call" | custom-call | flops 30000000 | bytes 622592 | tf_op jit(solution)/shard_map/pallas_call | solution.py:34
  1.8 0.6 collective-permute-start
  2.4 2.6 %collective-permute-start.3 = (bf16[256,256]{1,0:T(8,128)(2,1)S(1)}, bf16[256,256]{1,0:T(8,128)(2,1)S(1)}, u32[]{:S(2)}, u32[]{:S(2)}) collective-permute-start(bf16[256,256]{1,0:T(8,128)(2,1)S(1)} %get-tuple-element.71.chain_ref.own_ref.refs_11_.refs_14_), channel_id=1, source_target_pairs={{0,3},{1,2},{2,1},{3,0},{4,7},{5,6},{6,5},{7,4},{8,11},{9,10},{10,... | collective-permute-start | bytes 393224 | tf_op jit(solution)/shard_map/ppermute | solution.py:20
  5.0 3.8 %collective-permute-done.3.got_ref = bf16[256,256]{1,0:T(8,128)(2,1)S(1)} collective-permute-done((bf16[256,256]{1,0:T(8,128)(2,1)S(1)}, bf16[256,256]{1,0:T(8,128)(2,1)S(1)}, u32[]{:S(2)}, u32[]{:S(2)}) %collective-permute-start.3) | collective-permute-done | bytes 131104 | tf_op jit(solution)/shard_map/ppermute | solution.py:20
  8.8 0.1 collective-permute-start.4
  8.9 0.3 shard_map.99
  9.1 1.0 %collective-permute-done.4.twin_ref = bf16[256,256]{1,0:T(8,128)(2,1)S(1)} collective-permute-done((bf16[256,256]{1,0:T(8,128)(2,1)S(1)}, bf16[256,256]{1,0:T(8,128)(2,1)S(1)}, u32[]{:S(2)}, u32[]{:S(2)}) %collective-permute-start.4) | collective-permute-done | bytes 131104 | tf_op jit(solution)/shard_map/ppermute | solution.py:20
  10.1 0.8 shard_map.100
  10.9 1.5 %collective-permute-start.8 = (f32[128,256]{1,0:T(8,128)S(1)}, f32[128,256]{1,0:T(8,128)S(1)}, u32[]{:S(2)}, u32[]{:S(2)}) collective-permute-start(f32[128,256]{1,0:T(8,128)S(1)} %get-tuple-element.83), channel_id=1, source_target_pairs={{0,5},{1,4},{2,7},{3,6},{4,1},{5,0},{6,3},{7,2},{8,13},{9,12},{10,... | collective-permute-start | bytes 393224 | tf_op jit(solution)/shard_map/ppermute | solution.py:20
  12.4 4.0 %collective-permute-done.8.got_ref = f32[128,256]{1,0:T(8,128)S(1)} collective-permute-done((f32[128,256]{1,0:T(8,128)S(1)}, f32[128,256]{1,0:T(8,128)S(1)}, u32[]{:S(2)}, u32[]{:S(2)}) %collective-permute-start.8) | collective-permute-done | bytes 131104 | tf_op jit(solution)/shard_map/ppermute | solution.py:20
  16.4 0.1 collective-permute-start.9
  16.6 0.7 collective-permute-start.1
  17.3 0.5 collective-permute-done.9.twin_ref
  17.8 0.6 shard_map.102
  18.4 3.5 %collective-permute-start.11 = (f32[128,256]{1,0:T(8,128)S(1)}, f32[128,256]{1,0:T(8,128)S(1)}, u32[]{:S(2)}, u32[]{:S(2)}) collective-permute-start(f32[128,256]{1,0:T(8,128)S(1)} %get-tuple-element.89), channel_id=1, source_target_pairs={{0,9},{1,8},{2,11},{3,10},{4,13},{5,12},{6,15},{7,14},{8,1},{9,0},... | collective-permute-start | bytes 393224 | tf_op jit(solution)/shard_map/ppermute | solution.py:20
  21.9 3.0 %shard_map.95 = (f32[32,1024]{1,0:T(8,128)S(1)}, f32[32,1024]{1,0:T(8,128)S(1)}, f32[32,1024]{1,0:T(8,128)S(1)}, bf16[3,1024,256]{2,1,0:T(8,128)(2,1)S(1)}, bf16...) custom-call(f32[32,1024]{1,0:T(8,128)} %b_hbm.1, ...), custom_call_target="tpu_custom_call" | custom-call | flops 300000000 | bytes 8257536 | tf_op jit(solution)/shard_map/pallas_call | solution.py:34
  24.9 0.2 shard_map.97
  25.2 0.4 collective-permute-done.11.got_ref
  25.6 2.2 %collective-permute-start.12 = (f32[128,256]{1,0:T(8,128)S(1)}, f32[128,256]{1,0:T(8,128)S(1)}, u32[]{:S(2)}, u32[]{:S(2)}) collective-permute-start(f32[128,256]{1,0:T(8,128)S(1)} %collective-permute-done.11.got_ref), channel_id=1, source_target_pairs={{0,1},{1,0},{2,3},{3,2},{4,5},{5,4},{6,7},{7,6},{8,9},{9,8},{10,11... | collective-permute-start | bytes 393224 | tf_op jit(solution)/shard_map/ppermute | solution.py:20
  27.8 0.8 shard_map.98
  28.6 1.2 %collective-permute-done.2.got_ref.refs_3_ = f32[64,256]{1,0:T(8,128)S(1)} collective-permute-done((f32[64,256]{1,0:T(8,128)S(1)}, f32[64,256]{1,0:T(8,128)S(1)}, u32[]{:S(2)}, u32[]{:S(2)}) %collective-permute-start.2) | collective-permute-done | bytes 65568 | tf_op jit(solution)/shard_map/ppermute | solution.py:20
  29.9 0.3 shard_map.101
  30.2 0.1 collective-permute-start.5
  30.3 1.2 %collective-permute-start.7 = (f32[32,256]{1,0:T(8,128)S(1)}, f32[32,256]{1,0:T(8,128)S(1)}, u32[]{:S(2)}, u32[]{:S(2)}) collective-permute-start(f32[32,256]{1,0:T(8,128)S(1)} %get-tuple-element.79.carried_ref), channel_id=1, source_target_pairs={{0,7},{1,6},{2,5},{3,4},{4,3},{5,2},{6,1},{7,0},{8,15},{9,14},{10,... | collective-permute-start | bytes 98312 | tf_op jit(solution)/shard_map/ppermute | solution.py:20
  31.5 1.8 %collective-permute-start.6 = (f32[32,256]{1,0:T(8,128)S(1)}, f32[32,256]{1,0:T(8,128)S(1)}, u32[]{:S(2)}, u32[]{:S(2)}) collective-permute-start(f32[32,256]{1,0:T(8,128)S(1)} %get-tuple-element.79.carried_ref), channel_id=1, source_target_pairs={{0,5},{1,4},{2,7},{3,6},{4,1},{5,0},{6,3},{7,2},{8,13},{9,12},{10,... | collective-permute-start | bytes 98312 | tf_op jit(solution)/shard_map/ppermute | solution.py:20
  33.2 0.4 collective-permute-done.5.got_ref
  33.6 1.0 %collective-permute-done.7.cross_ref = f32[32,256]{1,0:T(8,128)S(1)} collective-permute-done((f32[32,256]{1,0:T(8,128)S(1)}, f32[32,256]{1,0:T(8,128)S(1)}, u32[]{:S(2)}, u32[]{:S(2)}) %collective-permute-start.7) | collective-permute-done | bytes 32800 | tf_op jit(solution)/shard_map/ppermute | solution.py:20
  34.6 0.9 %collective-permute-done.6.low_ref = f32[32,256]{1,0:T(8,128)S(1)} collective-permute-done((f32[32,256]{1,0:T(8,128)S(1)}, f32[32,256]{1,0:T(8,128)S(1)}, u32[]{:S(2)}, u32[]{:S(2)}) %collective-permute-start.6) | collective-permute-done | bytes 32800 | tf_op jit(solution)/shard_map/ppermute | solution.py:20
  35.6 0.5 shard_map.103
  36.1 1.0 %collective-permute-start.10 = (f32[32,256]{1,0:T(8,128)S(1)}, f32[32,256]{1,0:T(8,128)S(1)}, u32[]{:S(2)}, u32[]{:S(2)}) collective-permute-start(f32[32,256]{1,0:T(8,128)S(1)} %get-tuple-element.85.total_ref), channel_id=1, source_target_pairs={{0,9},{1,8},{2,11},{3,10},{4,13},{5,12},{6,15},{7,14},{8,1},{9,0},... | collective-permute-start | bytes 98312 | tf_op jit(solution)/shard_map/ppermute | solution.py:20
  37.1 0.7 collective-permute-start.14
  37.8 0.4 shard_map.104
  38.2 1.3 %collective-permute-done.10.got_ref = f32[32,256]{1,0:T(8,128)S(1)} collective-permute-done((f32[32,256]{1,0:T(8,128)S(1)}, f32[32,256]{1,0:T(8,128)S(1)}, u32[]{:S(2)}, u32[]{:S(2)}) %collective-permute-start.10) | collective-permute-done | bytes 32800 | tf_op jit(solution)/shard_map/ppermute | solution.py:20
  39.5 0.2 shard_map.105
  39.8 3.6 %collective-permute-start.13 = (f32[32,256]{1,0:T(8,128)S(1)}, f32[32,256]{1,0:T(8,128)S(1)}, u32[]{:S(2)}, u32[]{:S(2)}) collective-permute-start(f32[32,256]{1,0:T(8,128)S(1)} %get-tuple-element.91), channel_id=1, source_target_pairs={{0,17},{1,16},{2,19},{3,18},{4,21},{5,20},{6,23},{7,22},{8,25},{9,... | collective-permute-start | bytes 98312 | tf_op jit(solution)/shard_map/ppermute | solution.py:20
  43.4 1.6 %collective-permute-done.13.refs_0_ = f32[32,256]{1,0:T(8,128)S(1)} collective-permute-done((f32[32,256]{1,0:T(8,128)S(1)}, f32[32,256]{1,0:T(8,128)S(1)}, u32[]{:S(2)}, u32[]{:S(2)}) %collective-permute-start.13) | collective-permute-done | bytes 32800 | tf_op jit(solution)/shard_map/ppermute | solution.py:20
  45.0 0.7 shard_map.106
  45.7 0.7 collective-permute-start.15
  46.3 0.7 collective-permute-start.16
  47.0 1.0 %shard_map.107 = (f32[32,1024]{1,0:T(8,128)S(1)}, f32[32,1024]{1,0:T(8,128)S(1)}) custom-call(bf16[32,256]{1,0:T(8,128)(2,1)S(1)} %get-tuple-element.101.top_ref, bf16[32,256]{1,0:T(8,128)(2,1)S(1)} %get-tuple-element.102.previous_ref, f32[32,1024]{1,0:T(8,128)S(1)} %get-tuple-element.95.refs_5_.local_ref, f32[32,1024]{1,0:T(8,128)S(1)} %get-tuple-element.96.refs_6_.x_ref, ...), custom_call_target="tpu_custom_call" | custom-call | flops 100000000 | bytes 262144 | tf_op jit(solution)/shard_map/pallas_call | solution.py:34
  48.0 0.8 shard_map.108
  48.8 4.3 %collective-permute-start.17 = (f32[64,256]{1,0:T(8,128)S(1)}, f32[64,256]{1,0:T(8,128)S(1)}, u32[]{:S(2)}, u32[]{:S(2)}) collective-permute-start(f32[64,256]{1,0:T(8,128)S(1)} %get-tuple-element.108.both_ref), channel_id=1, source_target_pairs={{0,1},{1,0},{2,3},{3,2},{4,5},{5,4},{6,7},{7,6},{8,9},{9,8},{10,11... | collective-permute-start | bytes 196616 | tf_op jit(solution)/shard_map/ppermute | solution.py:20
  53.1 0.9 collective-permute-done.17.got_ref.refs_6_
  54.0 0.3 shard_map.109
  54.3 2.9 %collective-permute-start.18 = (f32[32,256]{1,0:T(8,128)S(1)}, f32[32,256]{1,0:T(8,128)S(1)}, u32[]{:S(2)}, u32[]{:S(2)}) collective-permute-start(f32[32,256]{1,0:T(8,128)S(1)} %get-tuple-element.109.total_ref), channel_id=1, source_target_pairs={{0,3},{1,2},{2,1},{3,0},{4,7},{5,6},{6,5},{7,4},{8,11},{9,10},{10,... | collective-permute-start | bytes 98312 | tf_op jit(solution)/shard_map/ppermute | solution.py:20
  57.2 1.1 %collective-permute-start.20 = (f32[32,256]{1,0:T(8,128)S(1)}, f32[32,256]{1,0:T(8,128)S(1)}, u32[]{:S(2)}, u32[]{:S(2)}) collective-permute-start(f32[32,256]{1,0:T(8,128)S(1)} %get-tuple-element.110.carried_ref), channel_id=1, source_target_pairs={{0,7},{1,6},{2,5},{3,4},{4,3},{5,2},{6,1},{7,0},{8,15},{9,14},{10,... | collective-permute-start | bytes 98312 | tf_op jit(solution)/shard_map/ppermute | solution.py:20
  58.3 0.3 collective-permute-start.19
  58.6 0.7 collective-permute-start.24
  59.2 2.3 %collective-permute-done.20.cross_ref = f32[32,256]{1,0:T(8,128)S(1)} collective-permute-done((f32[32,256]{1,0:T(8,128)S(1)}, f32[32,256]{1,0:T(8,128)S(1)}, u32[]{:S(2)}, u32[]{:S(2)}) %collective-permute-start.20) | collective-permute-done | bytes 32800 | tf_op jit(solution)/shard_map/ppermute | solution.py:20
  61.5 1.0 %collective-permute-done.19.low_ref = f32[32,256]{1,0:T(8,128)S(1)} collective-permute-done((f32[32,256]{1,0:T(8,128)S(1)}, f32[32,256]{1,0:T(8,128)S(1)}, u32[]{:S(2)}, u32[]{:S(2)}) %collective-permute-start.19) | collective-permute-done | bytes 32800 | tf_op jit(solution)/shard_map/ppermute | solution.py:20
  62.5 0.7 shard_map.110
  63.2 0.6 collective-permute-start.21
  63.8 3.5 %collective-permute-start.23 = (f32[32,256]{1,0:T(8,128)S(1)}, f32[32,256]{1,0:T(8,128)S(1)}, u32[]{:S(2)}, u32[]{:S(2)}) collective-permute-start(f32[32,256]{1,0:T(8,128)S(1)} %get-tuple-element.113), channel_id=1, source_target_pairs={{0,25},{1,24},{2,27},{3,26},{4,29},{5,28},{6,31},{7,30},{8,17},{9,... | collective-permute-start | bytes 98312 | tf_op jit(solution)/shard_map/ppermute | solution.py:20
  67.4 2.0 %collective-permute-done.23.refs_2_ = f32[32,256]{1,0:T(8,128)S(1)} collective-permute-done((f32[32,256]{1,0:T(8,128)S(1)}, f32[32,256]{1,0:T(8,128)S(1)}, u32[]{:S(2)}, u32[]{:S(2)}) %collective-permute-start.23) | collective-permute-done | bytes 32800 | tf_op jit(solution)/shard_map/ppermute | solution.py:20
  69.4 2.8 %collective-permute-done.22.refs_1_ = f32[32,256]{1,0:T(8,128)S(1)} collective-permute-done((f32[32,256]{1,0:T(8,128)S(1)}, f32[32,256]{1,0:T(8,128)S(1)}, u32[]{:S(2)}, u32[]{:S(2)}) %collective-permute-start.22) | collective-permute-done | bytes 32800 | tf_op jit(solution)/shard_map/ppermute | solution.py:20
  72.2 0.7 shard_map.111
  73.0 0.2 collective-permute-start.25
  73.1 0.7 collective-permute-start.26
  73.8 1.0 %shard_map.112 = (f32[32,1024]{1,0:T(8,128)S(1)}, f32[32,1024]{1,0:T(8,128)S(1)}, f32[32,128]{1,0:T(8,128)S(1)}, f32[1,128]{1,0:T(1,128)S(1)}) custom-call(bf16[32,256]{1,0:T(8,128)(2,1)S(1)} %get-tuple-element.118.top_ref, bf16[32,256]{1,0:T(8,128)(2,1)S(1)} %get-tuple-element.119.previous_ref, f32[32,1024]{1,0:T(8,128)S(1)} %get-tuple-element.116.refs_8_.local_ref, ...), custom_call_target="tpu_custom_call" | custom-call | flops 100000000 | bytes 279040 | tf_op jit(solution)/shard_map/pallas_call | solution.py:34
  74.8 1.0 %shard_map.113 = f32[32,128]{1,0:T(8,128)} custom-call(f32[32,1024]{1,0:T(8,128)S(1)} %get-tuple-element.123.acc_ref, f32[32,256]{1,0:T(8,128)S(1)} %collective-permute-done.25.near_ref, f32[32,256]{1,0:T(8,128)S(1)} %collective-permute-done.26.far_ref, bf16[3,1024,256]{2,1,0:T(8,128)(2,1)S(1)} %get-tuple-element.68.s3_ref, ...), custom_call_target="tpu_custom_call" | custom-call | flops 30000000 | bytes 16384 | tf_op jit(solution)/shard_map/pallas_call | solution.py:34
  75.8 7.4 %all-to-all-start = ((f32[32,1,128]{2,1,0:T(1,128)}), f32[32,1,128]{2,1,0:T(1,128)S(1)}, u32[]{:S(2)}, u32[]{:S(2)}) async-start(f32[32,1,128]{2,1,0:T(1,128)} %bitcast.1), calls=%async_computation | async-start | bytes 32768 | tf_op jit(solution)/shard_map/all_to_all | solution.py:507
  83.2 0.7 copy.11
  83.9 6.5 %all-to-all-done = f32[32,1,128]{2,1,0:T(1,128)S(1)} async-done(((f32[32,1,128]{2,1,0:T(1,128)}), f32[32,1,128]{2,1,0:T(1,128)S(1)}, u32[]{:S(2)}, u32[]{:S(2)}) %all-to-all-start) | async-done | bytes 16416 | tf_op jit(solution)/shard_map/all_to_all | solution.py:507
  90.4 0.7 shard_map.114
  (13 shorter events, 0.1 us)
Async XLA Ops:
  1.8 7.1 %collective-permute-start = (bf16[608,256]{1,0:T(8,128)(2,1)S(1)}, bf16[608,256]{1,0:T(8,128)(2,1)S(1)}, u32[]{:S(2)}, u32[]{:S(2)}) collective-permute-start(bf16[608,256]{1,0:T(8,128)(2,1)S(1)} %get-tuple-element.66), channel_id=1, source_target_pairs={{0,1},{1,0},{2,3},{3,2},{4,5},{5,4},{6,7},{7,6},{8,9},{9,8},{10,11... | collective-permute-start | bytes 933896 | tf_op jit(solution)/shard_map/ppermute | solution.py:20
  2.4 6.4 %collective-permute-start.3 = (bf16[256,256]{1,0:T(8,128)(2,1)S(1)}, bf16[256,256]{1,0:T(8,128)(2,1)S(1)}, u32[]{:S(2)}, u32[]{:S(2)}) collective-permute-start(bf16[256,256]{1,0:T(8,128)(2,1)S(1)} %get-tuple-element.71.chain_ref.own_ref.refs_11_.refs_14_), channel_id=1, source_target_pairs={{0,3},{1,2},{2,1},{3,0},{4,7},{5,6},{6,5},{7,4},{8,11},{9,10},{10,... | collective-permute-start | bytes 393224 | tf_op jit(solution)/shard_map/ppermute | solution.py:20
  8.8 1.3 %collective-permute-start.4 = (bf16[256,256]{1,0:T(8,128)(2,1)S(1)}, bf16[256,256]{1,0:T(8,128)(2,1)S(1)}, u32[]{:S(2)}, u32[]{:S(2)}) collective-permute-start(bf16[256,256]{1,0:T(8,128)(2,1)S(1)} %collective-permute-done.3.got_ref), channel_id=1, source_target_pairs={{0,1},{1,0},{2,3},{3,2},{4,5},{5,4},{6,7},{7,6},{8,9},{9,8},{10,11... | collective-permute-start | bytes 393224 | tf_op jit(solution)/shard_map/ppermute | solution.py:20
  10.9 5.5 %collective-permute-start.8 = (f32[128,256]{1,0:T(8,128)S(1)}, f32[128,256]{1,0:T(8,128)S(1)}, u32[]{:S(2)}, u32[]{:S(2)}) collective-permute-start(f32[128,256]{1,0:T(8,128)S(1)} %get-tuple-element.83), channel_id=1, source_target_pairs={{0,5},{1,4},{2,7},{3,6},{4,1},{5,0},{6,3},{7,2},{8,13},{9,12},{10,... | collective-permute-start | bytes 393224 | tf_op jit(solution)/shard_map/ppermute | solution.py:20
  16.4 1.3 %collective-permute-start.9 = (f32[128,256]{1,0:T(8,128)S(1)}, f32[128,256]{1,0:T(8,128)S(1)}, u32[]{:S(2)}, u32[]{:S(2)}) collective-permute-start(f32[128,256]{1,0:T(8,128)S(1)} %collective-permute-done.8.got_ref), channel_id=1, source_target_pairs={{0,1},{1,0},{2,3},{3,2},{4,5},{5,4},{6,7},{7,6},{8,9},{9,8},{10,11... | collective-permute-start | bytes 393224 | tf_op jit(solution)/shard_map/ppermute | solution.py:20
  16.6 8.3 %collective-permute-start.1 = (bf16[352,256]{1,0:T(8,128)(2,1)S(1)}, bf16[352,256]{1,0:T(8,128)(2,1)S(1)}, u32[]{:S(2)}, u32[]{:S(2)}) collective-permute-start(bf16[352,256]{1,0:T(8,128)(2,1)S(1)} %get-tuple-element.67), channel_id=1, source_target_pairs={{1,2},{3,4},{5,6},{7,8},{9,10},{11,12},{13,14},{15,16},{17,18},{19... | collective-permute-start | bytes 540680 | tf_op jit(solution)/shard_map/ppermute | solution.py:26
  18.4 7.1 %collective-permute-start.11 = (f32[128,256]{1,0:T(8,128)S(1)}, f32[128,256]{1,0:T(8,128)S(1)}, u32[]{:S(2)}, u32[]{:S(2)}) collective-permute-start(f32[128,256]{1,0:T(8,128)S(1)} %get-tuple-element.89), channel_id=1, source_target_pairs={{0,9},{1,8},{2,11},{3,10},{4,13},{5,12},{6,15},{7,14},{8,1},{9,0},... | collective-permute-start | bytes 393224 | tf_op jit(solution)/shard_map/ppermute | solution.py:20
  25.6 12.2 %collective-permute-start.12 = (f32[128,256]{1,0:T(8,128)S(1)}, f32[128,256]{1,0:T(8,128)S(1)}, u32[]{:S(2)}, u32[]{:S(2)}) collective-permute-start(f32[128,256]{1,0:T(8,128)S(1)} %collective-permute-done.11.got_ref), channel_id=1, source_target_pairs={{0,1},{1,0},{2,3},{3,2},{4,5},{5,4},{6,7},{7,6},{8,9},{9,8},{10,11... | collective-permute-start | bytes 393224 | tf_op jit(solution)/shard_map/ppermute | solution.py:20
  28.5 1.3 %collective-permute-start.2 = (f32[64,256]{1,0:T(8,128)S(1)}, f32[64,256]{1,0:T(8,128)S(1)}, u32[]{:S(2)}, u32[]{:S(2)}) collective-permute-start(f32[64,256]{1,0:T(8,128)S(1)} %get-tuple-element.73.both_ref), channel_id=1, source_target_pairs={{0,1},{1,0},{2,3},{3,2},{4,5},{5,4},{6,7},{7,6},{8,9},{9,8},{10,11... | collective-permute-start | bytes 196616 | tf_op jit(solution)/shard_map/ppermute | solution.py:20
  30.2 3.4 %collective-permute-start.5 = (f32[32,256]{1,0:T(8,128)S(1)}, f32[32,256]{1,0:T(8,128)S(1)}, u32[]{:S(2)}, u32[]{:S(2)}) collective-permute-start(f32[32,256]{1,0:T(8,128)S(1)} %get-tuple-element.78.total_ref), channel_id=1, source_target_pairs={{0,3},{1,2},{2,1},{3,0},{4,7},{5,6},{6,5},{7,4},{8,11},{9,10},{10,... | collective-permute-start | bytes 98312 | tf_op jit(solution)/shard_map/ppermute | solution.py:20
  30.3 4.3 %collective-permute-start.7 = (f32[32,256]{1,0:T(8,128)S(1)}, f32[32,256]{1,0:T(8,128)S(1)}, u32[]{:S(2)}, u32[]{:S(2)}) collective-permute-start(f32[32,256]{1,0:T(8,128)S(1)} %get-tuple-element.79.carried_ref), channel_id=1, source_target_pairs={{0,7},{1,6},{2,5},{3,4},{4,3},{5,2},{6,1},{7,0},{8,15},{9,14},{10,... | collective-permute-start | bytes 98312 | tf_op jit(solution)/shard_map/ppermute | solution.py:20
  31.5 4.1 %collective-permute-start.6 = (f32[32,256]{1,0:T(8,128)S(1)}, f32[32,256]{1,0:T(8,128)S(1)}, u32[]{:S(2)}, u32[]{:S(2)}) collective-permute-start(f32[32,256]{1,0:T(8,128)S(1)} %get-tuple-element.79.carried_ref), channel_id=1, source_target_pairs={{0,5},{1,4},{2,7},{3,6},{4,1},{5,0},{6,3},{7,2},{8,13},{9,12},{10,... | collective-permute-start | bytes 98312 | tf_op jit(solution)/shard_map/ppermute | solution.py:20
  36.1 3.4 %collective-permute-start.10 = (f32[32,256]{1,0:T(8,128)S(1)}, f32[32,256]{1,0:T(8,128)S(1)}, u32[]{:S(2)}, u32[]{:S(2)}) collective-permute-start(f32[32,256]{1,0:T(8,128)S(1)} %get-tuple-element.85.total_ref), channel_id=1, source_target_pairs={{0,9},{1,8},{2,11},{3,10},{4,13},{5,12},{6,15},{7,14},{8,1},{9,0},... | collective-permute-start | bytes 98312 | tf_op jit(solution)/shard_map/ppermute | solution.py:20
  37.1 6.3 %collective-permute-start.14 = (f32[32,256]{1,0:T(8,128)S(1)}, f32[32,256]{1,0:T(8,128)S(1)}, u32[]{:S(2)}, u32[]{:S(2)}) collective-permute-start(f32[32,256]{1,0:T(8,128)S(1)} %get-tuple-element.94), channel_id=1, source_target_pairs={{1,2},{3,4},{5,6},{7,8},{9,10},{11,12},{13,14},{15,16},{17,18},{19... | collective-permute-start | bytes 98312 | tf_op jit(solution)/shard_map/ppermute | solution.py:26
  39.8 5.2 %collective-permute-start.13 = (f32[32,256]{1,0:T(8,128)S(1)}, f32[32,256]{1,0:T(8,128)S(1)}, u32[]{:S(2)}, u32[]{:S(2)}) collective-permute-start(f32[32,256]{1,0:T(8,128)S(1)} %get-tuple-element.91), channel_id=1, source_target_pairs={{0,17},{1,16},{2,19},{3,18},{4,21},{5,20},{6,23},{7,22},{8,25},{9,... | collective-permute-start | bytes 98312 | tf_op jit(solution)/shard_map/ppermute | solution.py:20
  45.7 2.3 %collective-permute-start.15 = (f32[32,256]{1,0:T(8,128)S(1)}, f32[32,256]{1,0:T(8,128)S(1)}, u32[]{:S(2)}, u32[]{:S(2)}) collective-permute-start(f32[32,256]{1,0:T(8,128)S(1)} %get-tuple-element.106), channel_id=1, source_target_pairs={{0,1},{1,0},{2,3},{3,2},{4,5},{5,4},{6,7},{7,6},{8,9},{9,8},{10,11... | collective-permute-start | bytes 98312 | tf_op jit(solution)/shard_map/ppermute | solution.py:20
  46.3 1.7 %collective-permute-start.16 = (f32[32,256]{1,0:T(8,128)S(1)}, f32[32,256]{1,0:T(8,128)S(1)}, u32[]{:S(2)}, u32[]{:S(2)}) collective-permute-start(f32[32,256]{1,0:T(8,128)S(1)} %get-tuple-element.107), channel_id=1, source_target_pairs={{1,2},{3,4},{5,6},{7,8},{9,10},{11,12},{13,14},{15,16},{17,18},{19... | collective-permute-start | bytes 98312 | tf_op jit(solution)/shard_map/ppermute | solution.py:26
  48.8 5.2 %collective-permute-start.17 = (f32[64,256]{1,0:T(8,128)S(1)}, f32[64,256]{1,0:T(8,128)S(1)}, u32[]{:S(2)}, u32[]{:S(2)}) collective-permute-start(f32[64,256]{1,0:T(8,128)S(1)} %get-tuple-element.108.both_ref), channel_id=1, source_target_pairs={{0,1},{1,0},{2,3},{3,2},{4,5},{5,4},{6,7},{7,6},{8,9},{9,8},{10,11... | collective-permute-start | bytes 196616 | tf_op jit(solution)/shard_map/ppermute | solution.py:20
  54.3 4.9 %collective-permute-start.18 = (f32[32,256]{1,0:T(8,128)S(1)}, f32[32,256]{1,0:T(8,128)S(1)}, u32[]{:S(2)}, u32[]{:S(2)}) collective-permute-start(f32[32,256]{1,0:T(8,128)S(1)} %get-tuple-element.109.total_ref), channel_id=1, source_target_pairs={{0,3},{1,2},{2,1},{3,0},{4,7},{5,6},{6,5},{7,4},{8,11},{9,10},{10,... | collective-permute-start | bytes 98312 | tf_op jit(solution)/shard_map/ppermute | solution.py:20
  57.2 4.3 %collective-permute-start.20 = (f32[32,256]{1,0:T(8,128)S(1)}, f32[32,256]{1,0:T(8,128)S(1)}, u32[]{:S(2)}, u32[]{:S(2)}) collective-permute-start(f32[32,256]{1,0:T(8,128)S(1)} %get-tuple-element.110.carried_ref), channel_id=1, source_target_pairs={{0,7},{1,6},{2,5},{3,4},{4,3},{5,2},{6,1},{7,0},{8,15},{9,14},{10,... | collective-permute-start | bytes 98312 | tf_op jit(solution)/shard_map/ppermute | solution.py:20
  58.3 4.2 %collective-permute-start.19 = (f32[32,256]{1,0:T(8,128)S(1)}, f32[32,256]{1,0:T(8,128)S(1)}, u32[]{:S(2)}, u32[]{:S(2)}) collective-permute-start(f32[32,256]{1,0:T(8,128)S(1)} %get-tuple-element.110.carried_ref), channel_id=1, source_target_pairs={{0,5},{1,4},{2,7},{3,6},{4,1},{5,0},{6,3},{7,2},{8,13},{9,12},{10,... | collective-permute-start | bytes 98312 | tf_op jit(solution)/shard_map/ppermute | solution.py:20
  58.6 8.8 %collective-permute-start.24 = (f32[32,256]{1,0:T(8,128)S(1)}, f32[32,256]{1,0:T(8,128)S(1)}, u32[]{:S(2)}, u32[]{:S(2)}) collective-permute-start(f32[32,256]{1,0:T(8,128)S(1)} %get-tuple-element.115), channel_id=1, source_target_pairs={{1,2},{3,4},{5,6},{7,8},{9,10},{11,12},{13,14},{15,16},{17,18},{19... | collective-permute-start | bytes 98312 | tf_op jit(solution)/shard_map/ppermute | solution.py:26
  63.2 4.1 %collective-permute-start.21 = (f32[32,256]{1,0:T(8,128)S(1)}, f32[32,256]{1,0:T(8,128)S(1)}, u32[]{:S(2)}, u32[]{:S(2)}) collective-permute-start(f32[32,256]{1,0:T(8,128)S(1)} %get-tuple-element.112), channel_id=1, source_target_pairs={{0,9},{1,8},{2,11},{3,10},{4,13},{5,12},{6,15},{7,14},{8,1},{9,0},... | collective-permute-start | bytes 98312 | tf_op jit(solution)/shard_map/ppermute | solution.py:20
  63.8 5.6 %collective-permute-start.23 = (f32[32,256]{1,0:T(8,128)S(1)}, f32[32,256]{1,0:T(8,128)S(1)}, u32[]{:S(2)}, u32[]{:S(2)}) collective-permute-start(f32[32,256]{1,0:T(8,128)S(1)} %get-tuple-element.113), channel_id=1, source_target_pairs={{0,25},{1,24},{2,27},{3,26},{4,29},{5,28},{6,31},{7,30},{8,17},{9,... | collective-permute-start | bytes 98312 | tf_op jit(solution)/shard_map/ppermute | solution.py:20
  67.3 4.9 %collective-permute-start.22 = (f32[32,256]{1,0:T(8,128)S(1)}, f32[32,256]{1,0:T(8,128)S(1)}, u32[]{:S(2)}, u32[]{:S(2)}) collective-permute-start(f32[32,256]{1,0:T(8,128)S(1)} %get-tuple-element.113), channel_id=1, source_target_pairs={{0,17},{1,16},{2,19},{3,18},{4,21},{5,20},{6,23},{7,22},{8,25},{9,... | collective-permute-start | bytes 98312 | tf_op jit(solution)/shard_map/ppermute | solution.py:20
  73.0 1.8 %collective-permute-start.25 = (f32[32,256]{1,0:T(8,128)S(1)}, f32[32,256]{1,0:T(8,128)S(1)}, u32[]{:S(2)}, u32[]{:S(2)}) collective-permute-start(f32[32,256]{1,0:T(8,128)S(1)} %get-tuple-element.124), channel_id=1, source_target_pairs={{0,1},{1,0},{2,3},{3,2},{4,5},{5,4},{6,7},{7,6},{8,9},{9,8},{10,11... | collective-permute-start | bytes 98312 | tf_op jit(solution)/shard_map/ppermute | solution.py:20
  73.1 1.7 %collective-permute-start.26 = (f32[32,256]{1,0:T(8,128)S(1)}, f32[32,256]{1,0:T(8,128)S(1)}, u32[]{:S(2)}, u32[]{:S(2)}) collective-permute-start(f32[32,256]{1,0:T(8,128)S(1)} %get-tuple-element.125), channel_id=1, source_target_pairs={{1,2},{3,4},{5,6},{7,8},{9,10},{11,12},{13,14},{15,16},{17,18},{19... | collective-permute-start | bytes 98312 | tf_op jit(solution)/shard_map/ppermute | solution.py:26
  75.8 14.6 %all-to-all-start = ((f32[32,1,128]{2,1,0:T(1,128)}), f32[32,1,128]{2,1,0:T(1,128)S(1)}, u32[]{:S(2)}, u32[]{:S(2)}) async-start(f32[32,1,128]{2,1,0:T(1,128)} %bitcast.1), calls=%async_computation | async-start | bytes 32768 | tf_op jit(solution)/shard_map/all_to_all | solution.py:507

commit v6 on v5

--- a/solution.py
+++ b/solution.py
@@ -317,27 +317,31 @@
     sent_on(1, total_ref[...], next_ref, carried_ref)
 
 
-def level_kernel(total_ref, got_ref, carry_ref, reach_ref, second_ref, total_out, carry_out, *, level):
-    got = got_ref[...]
-    total_out[...] = merged(on_right(level), total_ref[...], got, parts_of(second_ref))
-    carry_out[...] = carry_ref[...] + carry_step(level, got, reach_ref)
-
-
-def wide_kernel(
-    total_ref, carried_ref, got_ref, low_ref, cross_ref, carry_ref, reach_ref, reach2_ref, second_ref, second2_ref,
-    *rest, level
-):
-    next_ref = rest[0] if len(rest) == 4 else None
-    total_out, carry_out = rest[-3:-1] if next_ref is not None else rest
+def level_kernel(total_ref, got_ref, second_ref, total_out, *, level):
+    total_out[...] = merged(on_right(level), total_ref[...], got_ref[...], parts_of(second_ref))
+
+
+def carry_kernel(got_ref, carry_ref, reach_ref, carry_out, *, level):
+    carry_out[...] = carry_ref[...] + carry_step(level, got_ref[...], reach_ref)
+
+
+def wide_kernel(total_ref, carried_ref, got_ref, low_ref, cross_ref, second_ref, second2_ref, *rest, level):
     right, right2 = on_right(level), on_right(level + 1)
     got, low = got_ref[...], low_ref[...] + cross_ref[...]
-    carry_out[...] = carry_ref[...] + carry_step(level, got, reach_ref) + carry_step(level + 1, low, reach2_ref)
     passed = times_split(split3(got), *parts_of(second_ref))
     pair = jnp.where(right, passed + total_ref[...], carried_ref[...] + got)
     total = merged(right2, pair, low, parts_of(second2_ref))
-    total_out[...] = total
-    if next_ref is not None:
-        sent_on(level + 2, total, next_ref, rest[-1])
+    if len(rest) == 1:
+        rest[0][...] = total
+    else:
+        next_ref, total_out, carried_out = rest
+        total_out[...] = total
+        sent_on(level + 2, total, next_ref, carried_out)
+
+
+def wide_carry_kernel(got_ref, low_ref, cross_ref, carry_ref, reach_ref, reach2_ref, carry_out, *, level):
+    step = carry_step(level, got_ref[...], reach_ref) + carry_step(level + 1, low_ref[...] + cross_ref[...], reach2_ref)
+    carry_out[...] = carry_ref[...] + step
 
 
 def tips_kernel(*refs, level, wide):
@@ -470,18 +474,23 @@
                 total, carry, *more = kernel_call(kernel, outs, both, swapped, seconds[0], *following)
             elif size_of == 1:
                 got = swap(total, 1 << level)
-                total, carry, *more = kernel_call(
-                    functools.partial(level_kernel, level=level), outs, total, got, carry, reaches[level], seconds[level]
+                total, *more = kernel_call(
+                    functools.partial(level_kernel, level=level), [tip], total, got, seconds[level]
                 )
+                carry = kernel_call(functools.partial(carry_kernel, level=level), [tip], got, carry, reaches[level])[0]
             else:
                 step = 1 << level
                 got = swap(total, step)
                 low = swap(carried, 2 * step)
                 cross = swap(carried, 3 * step)
-                total, carry, *more = kernel_call(
-                    functools.partial(wide_kernel, level=level), outs, total, carried, got, low, cross, carry,
-                    reaches[level], reaches[level + 1], seconds[level], seconds[level + 1], *following,
+                total, *more = kernel_call(
+                    functools.partial(wide_kernel, level=level), outs[1:], total, carried, got, low, cross,
+                    seconds[level], seconds[level + 1], *following,
                 )
+                carry = kernel_call(
+                    functools.partial(wide_carry_kernel, level=level), [tip],
+                    got, low, cross, carry, reaches[level], reaches[level + 1],
+                )[0]
             carried = more[0] if more else None
         level, size_of = groups[-1]
         gots = [swap(total, 1 << level)]

time: 91.3 us -> 91 us (level)
    pallas_call x19 -> x22, Pallas kernels: 14.6 us -> 15 us  [kernel_call(): pl.pallas_call(kernel, in_specs=specs, out_specs=[pl.BlockSpec(memory_spa...]
  transfers between devices with their start and end apart: 28 -> 28, of which waited for: 17 -> 17; matrix products, arithmetic and copies ran while one was open for 1% -> 1% of each run, Pallas kernels for 10% -> 11%
where the time goes in v6:
time: 91 us; the launch traced here: 90.8 us
  starting transfers between devices  42.4 us (47%)
  waiting for transfers between devices  31.1 us (34%)
  Pallas kernels  15.7 us (17%)
  between operations  0.93 us (1%)
    ppermute x22, starting transfers between devices, exchange(): return lax.ppermute(values, AXIS, [(i, i ^ distance) for i in range(count)])  31.7 us
    ppermute x22, waiting for transfers between devices, exchange(): return lax.ppermute(values, AXIS, [(i, i ^ distance) for i in range(count)])  24.6 us
    pallas_call x22, Pallas kernels, kernel_call(): pl.pallas_call(kernel, in_specs=specs, out_specs=[pl.BlockSpec(memory_spa...  15 us
    all_to_all x1, starting transfers between devices, body(): gathered = lax.all_to_all(mine, AXIS, 0, 0, tiled=True)  7.4 us
    all_to_all x1, waiting for transfers between devices, body(): gathered = lax.all_to_all(mine, AXIS, 0, 0, tiled=True)  6.52 us
    ppermute x5, starting transfers between devices, across(): return lax.ppermute(values, AXIS, pairs + [(b, a) for a, b in pairs])  3.26 us
  transfers between devices with their start and end apart: 28, of which 17 were waited for; matrix products, arithmetic and copies ran while one was open for 1% of the time, Pallas kernels for 11%

profile of v6, /device:TPU:0, one launch (start us, length us, event | category | flops | bytes accessed | tf_op | source)
XLA Modules:
  0.0 90.8 jit_solution(13270029553811219785)
XLA Ops:
  0.6 1.2 %shard_map.96 = (bf16[608,256]{1,0:T(8,128)(2,1)S(1)}, bf16[352,256]{1,0:T(8,128)(2,1)S(1)}, bf16[256,256]{1,0:T(8,128)(2,1)S(1)}) custom-call(f32[32,1024]{1,0:T(8,128)} %x_hbm.3, bf16[256,1024]{1,0:T(8,128)(2,1)} %u_hbm.3, bf16[256,1024]{1,0:T(8,128)(2,1)} %l_hbm.3), custom_call_target="tpu_custom_call" | custom-call | flops 30000000 | bytes 622592 | tf_op jit(solution)/shard_map/pallas_call | solution.py:34
  1.8 0.6 collective-permute-start
  2.4 2.6 %collective-permute-start.3 = (bf16[256,256]{1,0:T(8,128)(2,1)S(1)}, bf16[256,256]{1,0:T(8,128)(2,1)S(1)}, u32[]{:S(2)}, u32[]{:S(2)}) collective-permute-start(bf16[256,256]{1,0:T(8,128)(2,1)S(1)} %get-tuple-element.66.chain_ref.own_ref.refs_11_.refs_14_), channel_id=1, source_target_pairs={{0,3},{1,2},{2,1},{3,0},{4,7},{5,6},{6,5},{7,4},{8,11},{9,10},{10,... | collective-permute-start | bytes 393224 | tf_op jit(solution)/shard_map/ppermute | solution.py:20
  5.0 3.8 %collective-permute-done.3.got_ref = bf16[256,256]{1,0:T(8,128)(2,1)S(1)} collective-permute-done((bf16[256,256]{1,0:T(8,128)(2,1)S(1)}, bf16[256,256]{1,0:T(8,128)(2,1)S(1)}, u32[]{:S(2)}, u32[]{:S(2)}) %collective-permute-start.3) | collective-permute-done | bytes 131104 | tf_op jit(solution)/shard_map/ppermute | solution.py:20
  8.9 0.3 shard_map.99
  9.1 1.0 %collective-permute-done.4.twin_ref = bf16[256,256]{1,0:T(8,128)(2,1)S(1)} collective-permute-done((bf16[256,256]{1,0:T(8,128)(2,1)S(1)}, bf16[256,256]{1,0:T(8,128)(2,1)S(1)}, u32[]{:S(2)}, u32[]{:S(2)}) %collective-permute-start.4) | collective-permute-done | bytes 131104 | tf_op jit(solution)/shard_map/ppermute | solution.py:20
  10.1 0.8 shard_map.100
  10.9 1.5 %collective-permute-start.8 = (f32[128,256]{1,0:T(8,128)S(1)}, f32[128,256]{1,0:T(8,128)S(1)}, u32[]{:S(2)}, u32[]{:S(2)}) collective-permute-start(f32[128,256]{1,0:T(8,128)S(1)} %get-tuple-element.76), channel_id=1, source_target_pairs={{0,5},{1,4},{2,7},{3,6},{4,1},{5,0},{6,3},{7,2},{8,13},{9,12},{10,... | collective-permute-start | bytes 393224 | tf_op jit(solution)/shard_map/ppermute | solution.py:20
  12.4 4.0 %collective-permute-done.8.got_ref = f32[128,256]{1,0:T(8,128)S(1)} collective-permute-done((f32[128,256]{1,0:T(8,128)S(1)}, f32[128,256]{1,0:T(8,128)S(1)}, u32[]{:S(2)}, u32[]{:S(2)}) %collective-permute-start.8) | collective-permute-done | bytes 131104 | tf_op jit(solution)/shard_map/ppermute | solution.py:20
  16.6 0.7 collective-permute-start.1
  17.3 0.5 collective-permute-done.9.twin_ref
  17.8 0.6 shard_map.102
  18.4 3.5 %collective-permute-start.11 = (f32[128,256]{1,0:T(8,128)S(1)}, f32[128,256]{1,0:T(8,128)S(1)}, u32[]{:S(2)}, u32[]{:S(2)}) collective-permute-start(f32[128,256]{1,0:T(8,128)S(1)} %get-tuple-element.80), channel_id=1, source_target_pairs={{0,9},{1,8},{2,11},{3,10},{4,13},{5,12},{6,15},{7,14},{8,1},{9,0},... | collective-permute-start | bytes 393224 | tf_op jit(solution)/shard_map/ppermute | solution.py:20
  21.9 3.0 %shard_map.95 = (f32[32,1024]{1,0:T(8,128)S(1)}, f32[32,1024]{1,0:T(8,128)S(1)}, f32[32,1024]{1,0:T(8,128)S(1)}, bf16[3,1024,256]{2,1,0:T(8,128)(2,1)S(1)}, bf16...) custom-call(f32[32,1024]{1,0:T(8,128)} %b_hbm.1, ...), custom_call_target="tpu_custom_call" | custom-call | flops 300000000 | bytes 8257536 | tf_op jit(solution)/shard_map/pallas_call | solution.py:34
  24.9 0.2 shard_map.97
  25.2 0.4 collective-permute-done.11.got_ref
  25.6 2.2 %collective-permute-start.12 = (f32[128,256]{1,0:T(8,128)S(1)}, f32[128,256]{1,0:T(8,128)S(1)}, u32[]{:S(2)}, u32[]{:S(2)}) collective-permute-start(f32[128,256]{1,0:T(8,128)S(1)} %collective-permute-done.11.got_ref), channel_id=1, source_target_pairs={{0,1},{1,0},{2,3},{3,2},{4,5},{5,4},{6,7},{7,6},{8,9},{9,8},{10,11... | collective-permute-start | bytes 393224 | tf_op jit(solution)/shard_map/ppermute | solution.py:20
  27.8 0.8 shard_map.98
  28.6 1.2 %collective-permute-done.2.got_ref.refs_3_ = f32[64,256]{1,0:T(8,128)S(1)} collective-permute-done((f32[64,256]{1,0:T(8,128)S(1)}, f32[64,256]{1,0:T(8,128)S(1)}, u32[]{:S(2)}, u32[]{:S(2)}) %collective-permute-start.2) | collective-permute-done | bytes 65568 | tf_op jit(solution)/shard_map/ppermute | solution.py:20
  29.9 0.3 shard_map.101
  30.3 1.2 %collective-permute-start.7 = (f32[32,256]{1,0:T(8,128)S(1)}, f32[32,256]{1,0:T(8,128)S(1)}, u32[]{:S(2)}, u32[]{:S(2)}) collective-permute-start(f32[32,256]{1,0:T(8,128)S(1)} %get-tuple-element.74.carried_ref), channel_id=1, source_target_pairs={{0,7},{1,6},{2,5},{3,4},{4,3},{5,2},{6,1},{7,0},{8,15},{9,14},{10,... | collective-permute-start | bytes 98312 | tf_op jit(solution)/shard_map/ppermute | solution.py:20
  31.5 1.8 %collective-permute-start.6 = (f32[32,256]{1,0:T(8,128)S(1)}, f32[32,256]{1,0:T(8,128)S(1)}, u32[]{:S(2)}, u32[]{:S(2)}) collective-permute-start(f32[32,256]{1,0:T(8,128)S(1)} %get-tuple-element.74.carried_ref), channel_id=1, source_target_pairs={{0,5},{1,4},{2,7},{3,6},{4,1},{5,0},{6,3},{7,2},{8,13},{9,12},{10,... | collective-permute-start | bytes 98312 | tf_op jit(solution)/shard_map/ppermute | solution.py:20
  33.2 0.4 collective-permute-done.5.got_ref
  33.6 1.0 %collective-permute-done.7.cross_ref = f32[32,256]{1,0:T(8,128)S(1)} collective-permute-done((f32[32,256]{1,0:T(8,128)S(1)}, f32[32,256]{1,0:T(8,128)S(1)}, u32[]{:S(2)}, u32[]{:S(2)}) %collective-permute-start.7) | collective-permute-done | bytes 32800 | tf_op jit(solution)/shard_map/ppermute | solution.py:20
  34.6 0.9 %collective-permute-done.6.low_ref = f32[32,256]{1,0:T(8,128)S(1)} collective-permute-done((f32[32,256]{1,0:T(8,128)S(1)}, f32[32,256]{1,0:T(8,128)S(1)}, u32[]{:S(2)}, u32[]{:S(2)}) %collective-permute-start.6) | collective-permute-done | bytes 32800 | tf_op jit(solution)/shard_map/ppermute | solution.py:20
  35.6 0.4 shard_map.103.total_ref
  36.0 1.0 %collective-permute-start.10 = (f32[32,256]{1,0:T(8,128)S(1)}, f32[32,256]{1,0:T(8,128)S(1)}, u32[]{:S(2)}, u32[]{:S(2)}) collective-permute-start(f32[32,256]{1,0:T(8,128)S(1)} %shard_map.103.total_ref), channel_id=1, source_target_pairs={{0,9},{1,8},{2,11},{3,10},{4,13},{5,12},{6,15},{7,14},{8,1},{9,0},... | collective-permute-start | bytes 98312 | tf_op jit(solution)/shard_map/ppermute | solution.py:20
  37.0 0.7 collective-permute-start.14
  37.6 0.4 shard_map.104
  38.1 1.3 %collective-permute-done.10.got_ref = f32[32,256]{1,0:T(8,128)S(1)} collective-permute-done((f32[32,256]{1,0:T(8,128)S(1)}, f32[32,256]{1,0:T(8,128)S(1)}, u32[]{:S(2)}, u32[]{:S(2)}) %collective-permute-start.10) | collective-permute-done | bytes 32800 | tf_op jit(solution)/shard_map/ppermute | solution.py:20
  39.4 0.2 shard_map.105
  39.6 3.6 %collective-permute-start.13 = (f32[32,256]{1,0:T(8,128)S(1)}, f32[32,256]{1,0:T(8,128)S(1)}, u32[]{:S(2)}, u32[]{:S(2)}) collective-permute-start(f32[32,256]{1,0:T(8,128)S(1)} %shard_map.105), channel_id=1, source_target_pairs={{0,17},{1,16},{2,19},{3,18},{4,21},{5,20},{6,23},{7,22},{8,25},{9,... | collective-permute-start | bytes 98312 | tf_op jit(solution)/shard_map/ppermute | solution.py:20
  43.2 0.3 shard_map.106.carry_ref
  43.5 0.2 shard_map.107.refs_2_
  43.7 1.1 %collective-permute-done.13.refs_0_ = f32[32,256]{1,0:T(8,128)S(1)} collective-permute-done((f32[32,256]{1,0:T(8,128)S(1)}, f32[32,256]{1,0:T(8,128)S(1)}, u32[]{:S(2)}, u32[]{:S(2)}) %collective-permute-start.13) | collective-permute-done | bytes 32800 | tf_op jit(solution)/shard_map/ppermute | solution.py:20
  44.8 0.7 shard_map.108
  45.5 0.7 collective-permute-start.15
  46.2 0.7 collective-permute-start.16
  46.8 1.0 %shard_map.109 = (f32[32,1024]{1,0:T(8,128)S(1)}, f32[32,1024]{1,0:T(8,128)S(1)}) custom-call(bf16[32,256]{1,0:T(8,128)(2,1)S(1)} %get-tuple-element.92.top_ref, bf16[32,256]{1,0:T(8,128)(2,1)S(1)} %get-tuple-element.93.previous_ref, f32[32,1024]{1,0:T(8,128)S(1)} %get-tuple-element.86.refs_5_.local_ref, f32[32,1024]{1,0:T(8,128)S(1)} %get-tuple-element.87.refs_6_.x_ref, ...), custom_call_target="tpu_custom_call" | custom-call | flops 100000000 | bytes 262144 | tf_op jit(solution)/shard_map/pallas_call | solution.py:34
  47.8 0.8 shard_map.110
  48.6 4.3 %collective-permute-start.17 = (f32[64,256]{1,0:T(8,128)S(1)}, f32[64,256]{1,0:T(8,128)S(1)}, u32[]{:S(2)}, u32[]{:S(2)}) collective-permute-start(f32[64,256]{1,0:T(8,128)S(1)} %get-tuple-element.99.both_ref), channel_id=1, source_target_pairs={{0,1},{1,0},{2,3},{3,2},{4,5},{5,4},{6,7},{7,6},{8,9},{9,8},{10,11... | collective-permute-start | bytes 196616 | tf_op jit(solution)/shard_map/ppermute | solution.py:20
  52.9 0.9 collective-permute-done.17.got_ref.refs_6_
  53.8 0.3 shard_map.111
  54.1 3.0 %collective-permute-start.18 = (f32[32,256]{1,0:T(8,128)S(1)}, f32[32,256]{1,0:T(8,128)S(1)}, u32[]{:S(2)}, u32[]{:S(2)}) collective-permute-start(f32[32,256]{1,0:T(8,128)S(1)} %get-tuple-element.100.total_ref), channel_id=1, source_target_pairs={{0,3},{1,2},{2,1},{3,0},{4,7},{5,6},{6,5},{7,4},{8,11},{9,10},{10,... | collective-permute-start | bytes 98312 | tf_op jit(solution)/shard_map/ppermute | solution.py:20
  57.1 1.0 %collective-permute-start.20 = (f32[32,256]{1,0:T(8,128)S(1)}, f32[32,256]{1,0:T(8,128)S(1)}, u32[]{:S(2)}, u32[]{:S(2)}) collective-permute-start(f32[32,256]{1,0:T(8,128)S(1)} %get-tuple-element.101.carried_ref), channel_id=1, source_target_pairs={{0,7},{1,6},{2,5},{3,4},{4,3},{5,2},{6,1},{7,0},{8,15},{9,14},{10,... | collective-permute-start | bytes 98312 | tf_op jit(solution)/shard_map/ppermute | solution.py:20
  58.1 0.3 collective-permute-start.19
  58.4 0.7 collective-permute-start.24
  59.1 2.3 %collective-permute-done.20.cross_ref = f32[32,256]{1,0:T(8,128)S(1)} collective-permute-done((f32[32,256]{1,0:T(8,128)S(1)}, f32[32,256]{1,0:T(8,128)S(1)}, u32[]{:S(2)}, u32[]{:S(2)}) %collective-permute-start.20) | collective-permute-done | bytes 32800 | tf_op jit(solution)/shard_map/ppermute | solution.py:20
  61.4 1.0 %collective-permute-done.19.low_ref = f32[32,256]{1,0:T(8,128)S(1)} collective-permute-done((f32[32,256]{1,0:T(8,128)S(1)}, f32[32,256]{1,0:T(8,128)S(1)}, u32[]{:S(2)}, u32[]{:S(2)}) %collective-permute-start.19) | collective-permute-done | bytes 32800 | tf_op jit(solution)/shard_map/ppermute | solution.py:20
  62.4 0.6 shard_map.112
  63.0 0.6 collective-permute-start.21
  63.5 3.5 %collective-permute-start.23 = (f32[32,256]{1,0:T(8,128)S(1)}, f32[32,256]{1,0:T(8,128)S(1)}, u32[]{:S(2)}, u32[]{:S(2)}) collective-permute-start(f32[32,256]{1,0:T(8,128)S(1)} %get-tuple-element.103), channel_id=1, source_target_pairs={{0,25},{1,24},{2,27},{3,26},{4,29},{5,28},{6,31},{7,30},{8,17},{9,... | collective-permute-start | bytes 98312 | tf_op jit(solution)/shard_map/ppermute | solution.py:20
  67.1 0.3 shard_map.113.refs_5_
  67.4 1.8 %collective-permute-done.23.refs_2_ = f32[32,256]{1,0:T(8,128)S(1)} collective-permute-done((f32[32,256]{1,0:T(8,128)S(1)}, f32[32,256]{1,0:T(8,128)S(1)}, u32[]{:S(2)}, u32[]{:S(2)}) %collective-permute-start.23) | collective-permute-done | bytes 32800 | tf_op jit(solution)/shard_map/ppermute | solution.py:20
  69.1 2.8 %collective-permute-done.22.refs_1_ = f32[32,256]{1,0:T(8,128)S(1)} collective-permute-done((f32[32,256]{1,0:T(8,128)S(1)}, f32[32,256]{1,0:T(8,128)S(1)}, u32[]{:S(2)}, u32[]{:S(2)}) %collective-permute-start.22) | collective-permute-done | bytes 32800 | tf_op jit(solution)/shard_map/ppermute | solution.py:20
  71.9 0.7 shard_map.114
  72.7 0.2 collective-permute-start.25
  72.9 0.7 collective-permute-start.26
  73.5 1.0 %shard_map.115 = (f32[32,1024]{1,0:T(8,128)S(1)}, f32[32,1024]{1,0:T(8,128)S(1)}, f32[32,128]{1,0:T(8,128)S(1)}, f32[1,128]{1,0:T(1,128)S(1)}) custom-call(bf16[32,256]{1,0:T(8,128)(2,1)S(1)} %get-tuple-element.108.top_ref, bf16[32,256]{1,0:T(8,128)(2,1)S(1)} %get-tuple-element.109.previous_ref, f32[32,1024]{1,0:T(8,128)S(1)} %get-tuple-element.106.refs_8_.local_ref, ...), custom_call_target="tpu_custom_call" | custom-call | flops 100000000 | bytes 279040 | tf_op jit(solution)/shard_map/pallas_call | solution.py:34
  74.5 1.0 %shard_map.116 = f32[32,128]{1,0:T(8,128)} custom-call(f32[32,1024]{1,0:T(8,128)S(1)} %get-tuple-element.113.acc_ref, f32[32,256]{1,0:T(8,128)S(1)} %collective-permute-done.25.near_ref, f32[32,256]{1,0:T(8,128)S(1)} %collective-permute-done.26.far_ref, bf16[3,1024,256]{2,1,0:T(8,128)(2,1)S(1)} %get-tuple-element.63.s3_ref, ...), custom_call_target="tpu_custom_call" | custom-call | flops 30000000 | bytes 16384 | tf_op jit(solution)/shard_map/pallas_call | solution.py:34
  75.5 7.4 %all-to-all-start = ((f32[32,1,128]{2,1,0:T(1,128)}), f32[32,1,128]{2,1,0:T(1,128)S(1)}, u32[]{:S(2)}, u32[]{:S(2)}) async-start(f32[32,1,128]{2,1,0:T(1,128)} %bitcast.1), calls=%async_computation | async-start | bytes 32768 | tf_op jit(solution)/shard_map/all_to_all | solution.py:516
  82.9 0.7 copy.11
  83.6 6.5 %all-to-all-done = f32[32,1,128]{2,1,0:T(1,128)S(1)} async-done(((f32[32,1,128]{2,1,0:T(1,128)}), f32[32,1,128]{2,1,0:T(1,128)S(1)}, u32[]{:S(2)}, u32[]{:S(2)}) %all-to-all-start) | async-done | bytes 16416 | tf_op jit(solution)/shard_map/all_to_all | solution.py:516
  90.1 0.7 shard_map.117
  (16 shorter events, 0.5 us)
Async XLA Ops:
  1.8 7.1 %collective-permute-start = (bf16[608,256]{1,0:T(8,128)(2,1)S(1)}, bf16[608,256]{1,0:T(8,128)(2,1)S(1)}, u32[]{:S(2)}, u32[]{:S(2)}) collective-permute-start(bf16[608,256]{1,0:T(8,128)(2,1)S(1)} %get-tuple-element.61), channel_id=1, source_target_pairs={{0,1},{1,0},{2,3},{3,2},{4,5},{5,4},{6,7},{7,6},{8,9},{9,8},{10,11... | collective-permute-start | bytes 933896 | tf_op jit(solution)/shard_map/ppermute | solution.py:20
  2.4 6.4 %collective-permute-start.3 = (bf16[256,256]{1,0:T(8,128)(2,1)S(1)}, bf16[256,256]{1,0:T(8,128)(2,1)S(1)}, u32[]{:S(2)}, u32[]{:S(2)}) collective-permute-start(bf16[256,256]{1,0:T(8,128)(2,1)S(1)} %get-tuple-element.66.chain_ref.own_ref.refs_11_.refs_14_), channel_id=1, source_target_pairs={{0,3},{1,2},{2,1},{3,0},{4,7},{5,6},{6,5},{7,4},{8,11},{9,10},{10,... | collective-permute-start | bytes 393224 | tf_op jit(solution)/shard_map/ppermute | solution.py:20
  8.8 1.3 %collective-permute-start.4 = (bf16[256,256]{1,0:T(8,128)(2,1)S(1)}, bf16[256,256]{1,0:T(8,128)(2,1)S(1)}, u32[]{:S(2)}, u32[]{:S(2)}) collective-permute-start(bf16[256,256]{1,0:T(8,128)(2,1)S(1)} %collective-permute-done.3.got_ref), channel_id=1, source_target_pairs={{0,1},{1,0},{2,3},{3,2},{4,5},{5,4},{6,7},{7,6},{8,9},{9,8},{10,11... | collective-permute-start | bytes 393224 | tf_op jit(solution)/shard_map/ppermute | solution.py:20
  10.9 5.5 %collective-permute-start.8 = (f32[128,256]{1,0:T(8,128)S(1)}, f32[128,256]{1,0:T(8,128)S(1)}, u32[]{:S(2)}, u32[]{:S(2)}) collective-permute-start(f32[128,256]{1,0:T(8,128)S(1)} %get-tuple-element.76), channel_id=1, source_target_pairs={{0,5},{1,4},{2,7},{3,6},{4,1},{5,0},{6,3},{7,2},{8,13},{9,12},{10,... | collective-permute-start | bytes 393224 | tf_op jit(solution)/shard_map/ppermute | solution.py:20
  16.4 1.3 %collective-permute-start.9 = (f32[128,256]{1,0:T(8,128)S(1)}, f32[128,256]{1,0:T(8,128)S(1)}, u32[]{:S(2)}, u32[]{:S(2)}) collective-permute-start(f32[128,256]{1,0:T(8,128)S(1)} %collective-permute-done.8.got_ref), channel_id=1, source_target_pairs={{0,1},{1,0},{2,3},{3,2},{4,5},{5,4},{6,7},{7,6},{8,9},{9,8},{10,11... | collective-permute-start | bytes 393224 | tf_op jit(solution)/shard_map/ppermute | solution.py:20
  16.6 8.3 %collective-permute-start.1 = (bf16[352,256]{1,0:T(8,128)(2,1)S(1)}, bf16[352,256]{1,0:T(8,128)(2,1)S(1)}, u32[]{:S(2)}, u32[]{:S(2)}) collective-permute-start(bf16[352,256]{1,0:T(8,128)(2,1)S(1)} %get-tuple-element.62), channel_id=1, source_target_pairs={{1,2},{3,4},{5,6},{7,8},{9,10},{11,12},{13,14},{15,16},{17,18},{19... | collective-permute-start | bytes 540680 | tf_op jit(solution)/shard_map/ppermute | solution.py:26
  18.4 7.1 %collective-permute-start.11 = (f32[128,256]{1,0:T(8,128)S(1)}, f32[128,256]{1,0:T(8,128)S(1)}, u32[]{:S(2)}, u32[]{:S(2)}) collective-permute-start(f32[128,256]{1,0:T(8,128)S(1)} %get-tuple-element.80), channel_id=1, source_target_pairs={{0,9},{1,8},{2,11},{3,10},{4,13},{5,12},{6,15},{7,14},{8,1},{9,0},... | collective-permute-start | bytes 393224 | tf_op jit(solution)/shard_map/ppermute | solution.py:20
  25.6 12.0 %collective-permute-start.12 = (f32[128,256]{1,0:T(8,128)S(1)}, f32[128,256]{1,0:T(8,128)S(1)}, u32[]{:S(2)}, u32[]{:S(2)}) collective-permute-start(f32[128,256]{1,0:T(8,128)S(1)} %collective-permute-done.11.got_ref), channel_id=1, source_target_pairs={{0,1},{1,0},{2,3},{3,2},{4,5},{5,4},{6,7},{7,6},{8,9},{9,8},{10,11... | collective-permute-start | bytes 393224 | tf_op jit(solution)/shard_map/ppermute | solution.py:20
  28.5 1.3 %collective-permute-start.2 = (f32[64,256]{1,0:T(8,128)S(1)}, f32[64,256]{1,0:T(8,128)S(1)}, u32[]{:S(2)}, u32[]{:S(2)}) collective-permute-start(f32[64,256]{1,0:T(8,128)S(1)} %get-tuple-element.68.both_ref), channel_id=1, source_target_pairs={{0,1},{1,0},{2,3},{3,2},{4,5},{5,4},{6,7},{7,6},{8,9},{9,8},{10,11... | collective-permute-start | bytes 196616 | tf_op jit(solution)/shard_map/ppermute | solution.py:20
  30.2 3.4 %collective-permute-start.5 = (f32[32,256]{1,0:T(8,128)S(1)}, f32[32,256]{1,0:T(8,128)S(1)}, u32[]{:S(2)}, u32[]{:S(2)}) collective-permute-start(f32[32,256]{1,0:T(8,128)S(1)} %get-tuple-element.73.total_ref), channel_id=1, source_target_pairs={{0,3},{1,2},{2,1},{3,0},{4,7},{5,6},{6,5},{7,4},{8,11},{9,10},{10,... | collective-permute-start | bytes 98312 | tf_op jit(solution)/shard_map/ppermute | solution.py:20
  30.3 4.3 %collective-permute-start.7 = (f32[32,256]{1,0:T(8,128)S(1)}, f32[32,256]{1,0:T(8,128)S(1)}, u32[]{:S(2)}, u32[]{:S(2)}) collective-permute-start(f32[32,256]{1,0:T(8,128)S(1)} %get-tuple-element.74.carried_ref), channel_id=1, source_target_pairs={{0,7},{1,6},{2,5},{3,4},{4,3},{5,2},{6,1},{7,0},{8,15},{9,14},{10,... | collective-permute-start | bytes 98312 | tf_op jit(solution)/shard_map/ppermute | solution.py:20
  31.5 4.1 %collective-permute-start.6 = (f32[32,256]{1,0:T(8,128)S(1)}, f32[32,256]{1,0:T(8,128)S(1)}, u32[]{:S(2)}, u32[]{:S(2)}) collective-permute-start(f32[32,256]{1,0:T(8,128)S(1)} %get-tuple-element.74.carried_ref), channel_id=1, source_target_pairs={{0,5},{1,4},{2,7},{3,6},{4,1},{5,0},{6,3},{7,2},{8,13},{9,12},{10,... | collective-permute-start | bytes 98312 | tf_op jit(solution)/shard_map/ppermute | solution.py:20
  36.0 3.4 %collective-permute-start.10 = (f32[32,256]{1,0:T(8,128)S(1)}, f32[32,256]{1,0:T(8,128)S(1)}, u32[]{:S(2)}, u32[]{:S(2)}) collective-permute-start(f32[32,256]{1,0:T(8,128)S(1)} %shard_map.103.total_ref), channel_id=1, source_target_pairs={{0,9},{1,8},{2,11},{3,10},{4,13},{5,12},{6,15},{7,14},{8,1},{9,0},... | collective-permute-start | bytes 98312 | tf_op jit(solution)/shard_map/ppermute | solution.py:20
  37.0 6.7 %collective-permute-start.14 = (f32[32,256]{1,0:T(8,128)S(1)}, f32[32,256]{1,0:T(8,128)S(1)}, u32[]{:S(2)}, u32[]{:S(2)}) collective-permute-start(f32[32,256]{1,0:T(8,128)S(1)} %get-tuple-element.85), channel_id=1, source_target_pairs={{1,2},{3,4},{5,6},{7,8},{9,10},{11,12},{13,14},{15,16},{17,18},{19... | collective-permute-start | bytes 98312 | tf_op jit(solution)/shard_map/ppermute | solution.py:26
  39.6 5.2 %collective-permute-start.13 = (f32[32,256]{1,0:T(8,128)S(1)}, f32[32,256]{1,0:T(8,128)S(1)}, u32[]{:S(2)}, u32[]{:S(2)}) collective-permute-start(f32[32,256]{1,0:T(8,128)S(1)} %shard_map.105), channel_id=1, source_target_pairs={{0,17},{1,16},{2,19},{3,18},{4,21},{5,20},{6,23},{7,22},{8,25},{9,... | collective-permute-start | bytes 98312 | tf_op jit(solution)/shard_map/ppermute | solution.py:20
  45.5 2.3 %collective-permute-start.15 = (f32[32,256]{1,0:T(8,128)S(1)}, f32[32,256]{1,0:T(8,128)S(1)}, u32[]{:S(2)}, u32[]{:S(2)}) collective-permute-start(f32[32,256]{1,0:T(8,128)S(1)} %get-tuple-element.97), channel_id=1, source_target_pairs={{0,1},{1,0},{2,3},{3,2},{4,5},{5,4},{6,7},{7,6},{8,9},{9,8},{10,11... | collective-permute-start | bytes 98312 | tf_op jit(solution)/shard_map/ppermute | solution.py:20
  46.2 1.7 %collective-permute-start.16 = (f32[32,256]{1,0:T(8,128)S(1)}, f32[32,256]{1,0:T(8,128)S(1)}, u32[]{:S(2)}, u32[]{:S(2)}) collective-permute-start(f32[32,256]{1,0:T(8,128)S(1)} %get-tuple-element.98), channel_id=1, source_target_pairs={{1,2},{3,4},{5,6},{7,8},{9,10},{11,12},{13,14},{15,16},{17,18},{19... | collective-permute-start | bytes 98312 | tf_op jit(solution)/shard_map/ppermute | solution.py:26
  48.6 5.2 %collective-permute-start.17 = (f32[64,256]{1,0:T(8,128)S(1)}, f32[64,256]{1,0:T(8,128)S(1)}, u32[]{:S(2)}, u32[]{:S(2)}) collective-permute-start(f32[64,256]{1,0:T(8,128)S(1)} %get-tuple-element.99.both_ref), channel_id=1, source_target_pairs={{0,1},{1,0},{2,3},{3,2},{4,5},{5,4},{6,7},{7,6},{8,9},{9,8},{10,11... | collective-permute-start | bytes 196616 | tf_op jit(solution)/shard_map/ppermute | solution.py:20
  54.1 4.9 %collective-permute-start.18 = (f32[32,256]{1,0:T(8,128)S(1)}, f32[32,256]{1,0:T(8,128)S(1)}, u32[]{:S(2)}, u32[]{:S(2)}) collective-permute-start(f32[32,256]{1,0:T(8,128)S(1)} %get-tuple-element.100.total_ref), channel_id=1, source_target_pairs={{0,3},{1,2},{2,1},{3,0},{4,7},{5,6},{6,5},{7,4},{8,11},{9,10},{10,... | collective-permute-start | bytes 98312 | tf_op jit(solution)/shard_map/ppermute | solution.py:20
  57.1 4.3 %collective-permute-start.20 = (f32[32,256]{1,0:T(8,128)S(1)}, f32[32,256]{1,0:T(8,128)S(1)}, u32[]{:S(2)}, u32[]{:S(2)}) collective-permute-start(f32[32,256]{1,0:T(8,128)S(1)} %get-tuple-element.101.carried_ref), channel_id=1, source_target_pairs={{0,7},{1,6},{2,5},{3,4},{4,3},{5,2},{6,1},{7,0},{8,15},{9,14},{10,... | collective-permute-start | bytes 98312 | tf_op jit(solution)/shard_map/ppermute | solution.py:20
  58.1 4.2 %collective-permute-start.19 = (f32[32,256]{1,0:T(8,128)S(1)}, f32[32,256]{1,0:T(8,128)S(1)}, u32[]{:S(2)}, u32[]{:S(2)}) collective-permute-start(f32[32,256]{1,0:T(8,128)S(1)} %get-tuple-element.101.carried_ref), channel_id=1, source_target_pairs={{0,5},{1,4},{2,7},{3,6},{4,1},{5,0},{6,3},{7,2},{8,13},{9,12},{10,... | collective-permute-start | bytes 98312 | tf_op jit(solution)/shard_map/ppermute | solution.py:20
  58.4 8.9 %collective-permute-start.24 = (f32[32,256]{1,0:T(8,128)S(1)}, f32[32,256]{1,0:T(8,128)S(1)}, u32[]{:S(2)}, u32[]{:S(2)}) collective-permute-start(f32[32,256]{1,0:T(8,128)S(1)} %get-tuple-element.105), channel_id=1, source_target_pairs={{1,2},{3,4},{5,6},{7,8},{9,10},{11,12},{13,14},{15,16},{17,18},{19... | collective-permute-start | bytes 98312 | tf_op jit(solution)/shard_map/ppermute | solution.py:26
  63.0 4.4 %collective-permute-start.21 = (f32[32,256]{1,0:T(8,128)S(1)}, f32[32,256]{1,0:T(8,128)S(1)}, u32[]{:S(2)}, u32[]{:S(2)}) collective-permute-start(f32[32,256]{1,0:T(8,128)S(1)} %get-tuple-element.102), channel_id=1, source_target_pairs={{0,9},{1,8},{2,11},{3,10},{4,13},{5,12},{6,15},{7,14},{8,1},{9,0},... | collective-permute-start | bytes 98312 | tf_op jit(solution)/shard_map/ppermute | solution.py:20
  63.5 5.6 %collective-permute-start.23 = (f32[32,256]{1,0:T(8,128)S(1)}, f32[32,256]{1,0:T(8,128)S(1)}, u32[]{:S(2)}, u32[]{:S(2)}) collective-permute-start(f32[32,256]{1,0:T(8,128)S(1)} %get-tuple-element.103), channel_id=1, source_target_pairs={{0,25},{1,24},{2,27},{3,26},{4,29},{5,28},{6,31},{7,30},{8,17},{9,... | collective-permute-start | bytes 98312 | tf_op jit(solution)/shard_map/ppermute | solution.py:20
  67.1 4.9 %collective-permute-start.22 = (f32[32,256]{1,0:T(8,128)S(1)}, f32[32,256]{1,0:T(8,128)S(1)}, u32[]{:S(2)}, u32[]{:S(2)}) collective-permute-start(f32[32,256]{1,0:T(8,128)S(1)} %get-tuple-element.103), channel_id=1, source_target_pairs={{0,17},{1,16},{2,19},{3,18},{4,21},{5,20},{6,23},{7,22},{8,25},{9,... | collective-permute-start | bytes 98312 | tf_op jit(solution)/shard_map/ppermute | solution.py:20
  72.7 1.8 %collective-permute-start.25 = (f32[32,256]{1,0:T(8,128)S(1)}, f32[32,256]{1,0:T(8,128)S(1)}, u32[]{:S(2)}, u32[]{:S(2)}) collective-permute-start(f32[32,256]{1,0:T(8,128)S(1)} %get-tuple-element.114), channel_id=1, source_target_pairs={{0,1},{1,0},{2,3},{3,2},{4,5},{5,4},{6,7},{7,6},{8,9},{9,8},{10,11... | collective-permute-start | bytes 98312 | tf_op jit(solution)/shard_map/ppermute | solution.py:20
  72.9 1.7 %collective-permute-start.26 = (f32[32,256]{1,0:T(8,128)S(1)}, f32[32,256]{1,0:T(8,128)S(1)}, u32[]{:S(2)}, u32[]{:S(2)}) collective-permute-start(f32[32,256]{1,0:T(8,128)S(1)} %get-tuple-element.115), channel_id=1, source_target_pairs={{1,2},{3,4},{5,6},{7,8},{9,10},{11,12},{13,14},{15,16},{17,18},{19... | collective-permute-start | bytes 98312 | tf_op jit(solution)/shard_map/ppermute | solution.py:26
  75.5 14.6 %all-to-all-start = ((f32[32,1,128]{2,1,0:T(1,128)}), f32[32,1,128]{2,1,0:T(1,128)S(1)}, u32[]{:S(2)}, u32[]{:S(2)}) async-start(f32[32,1,128]{2,1,0:T(1,128)} %bitcast.1), calls=%async_computation | async-start | bytes 32768 | tf_op jit(solution)/shard_map/all_to_all | solution.py:516
